TPU v7x, 128 devices: a whole 4x4x4 slice. The times are simulated.
128 devices in a mesh: group: 4 (over z_lo, core), fsdp: 32 (over y, x, z_hi).
Axes of the slice: x: 4, y: 4, z: 4 (z_hi: 2, z_lo: 2; z = z_hi * 2 + z_lo), core: 2. Of those that a mesh axis runs over, the one named last changes fastest.
Arguments:
- tokens: bfloat16 [65536, 3072], P(('group', 'fsdp')), may hold values from -6 to 6
- student: float32 [4, 3072, 6144], P('group', 'fsdp'), may hold values from -6 to 6
- teacher: float32 [3072, 6144], P('fsdp', 'group'), may hold values from -6 to 6
- norm_gain: float32 [3072], replicated, may hold values from 0.5 to 1.5
- query_gain: float32 [128], replicated, may hold values from 0.5 to 1.5
- key_gain: float32 [128], replicated, may hold values from 0.5 to 1.5
Outputs:
- teacher_new: float32 [3072, 6144], P('fsdp', 'group')
- student_new: float32 [3072, 6144], P('fsdp', 'group')
- query: bfloat16 [65536, 3072], P(('group', 'fsdp'))
- key: bfloat16 [65536, 3072], P(('group', 'fsdp'))
All inputs are finite; a program needn't handle non-finite values.
Results may differ from a plain program's by a relative error of at most 0.0058.
Values may be sent and summed in bfloat16 or wider, within the bound.
No kernel may reach another device: no remote copies, remote signals or barrier semaphores. Data moves between devices by JAX's collectives and lax.ppermute only.
A program may use at most 192 MiB of HBM per device.

v0:
```python
import jax
import jax.numpy as jnp
from jax import lax
from jax.sharding import PartitionSpec as P

HEAD = 128


ema_decay = 0.99


def laid_out(blocks, dim):
    blocks = jnp.moveaxis(blocks, 0, dim)
    shape = blocks.shape
    return blocks.reshape(*shape[:dim], shape[dim] * shape[dim + 1], *shape[dim + 2 :])


def sent_to_all(x, axis):
    copies = jnp.broadcast_to(x, (lax.axis_size(axis), *x.shape))
    return lax.all_to_all(copies, axis, split_axis=0, concat_axis=0, tiled=True)


def collect(x, axis, dim):
    return laid_out(sent_to_all(x, axis), dim)


def head_norm(values, gain, model_width):
    shaped = values.reshape(values.shape[0], model_width // HEAD, HEAD)
    scaled = shaped * lax.rsqrt(jnp.mean(shaped * shaped, axis=-1, keepdims=True) + 1e-06) * gain
    return scaled.reshape(values.shape[0], model_width).astype(jnp.bfloat16)


def shards(tokens, student, teacher, norm_gain, query_gain, key_gain):
    model_width = tokens.shape[1]
    groups = lax.axis_size("group")
    local_part = student[0]
    wide = tokens.astype(jnp.float32)
    normed = (
        wide * lax.rsqrt(jnp.mean(wide * wide, axis=-1, keepdims=True) + 1e-06) * norm_gain
    ).astype(jnp.bfloat16)
    owned = lax.psum_scatter(local_part, "group", scatter_dimension=1, tiled=True) / groups
    copied = owned.astype(jnp.bfloat16)
    whole_rows = collect(copied, "group", 1)
    projected = jnp.dot(
        normed,
        lax.all_gather(whole_rows, "fsdp", axis=0, tiled=True),
        preferred_element_type=jnp.float32,
    )
    teacher_new = ema_decay * teacher + (1.0 - ema_decay) * owned
    projected = projected * model_width ** (-0.5)
    query = head_norm(projected[:, :model_width], query_gain, model_width)
    key_out = head_norm(projected[:, model_width:], key_gain, model_width)
    return (teacher_new, owned, query, key_out)


def solution(mesh):
    placed = (
        P(("group", "fsdp"), None),
        P("group", "fsdp", None),
        P("fsdp", "group"),
        P(),
        P(),
        P(),
    )
    return jax.shard_map(
        shards,
        mesh=mesh,
        in_specs=placed,
        out_specs=(
            P("fsdp", "group"),
            P("fsdp", "group"),
            P(("group", "fsdp"), None),
            P(("group", "fsdp"), None),
        ),
        check_vma=False,
    )
```

profile of v0, /device:TPU:0, one launch (start us, length us, event | category | flops | bytes accessed | tf_op | source)
XLA Modules:
  0.0 429.5 jit_solution(4200778437024442543)
XLA Ops:
  7.2 0.0 copy-start
  7.2 0.0 reduce-scatter.2.cloned.1.call-start
  7.2 0.7 reduce-scatter.2.cloned.1.call-update
  7.9 0.0 copy-start.1
  7.9 0.0 copy-start.2
  7.9 0.0 copy-start.3
  7.9 0.0 all-gather.2.cloned.1.call-start
  8.0 35.3 %reduce-scatter.2.cloned.1.call-done = f32[96,1536]{1,0:T(8,128)} async-done(((f32[96,6144]{1,0:T(8,128)}), f32[96,1536]{1,0:T(8,128)}) %reduce-scatter.2.cloned.1.call-update) | async-done | bytes 589840 | tf_op jit(solution)/shard_map/reduce_scatter | solution.py:41
  43.3 2.4 fusion.10
  45.7 0.1 broadcast_in_dim.2
  45.8 18.3 %all_to_all.5 = bf16[4,96,1536]{2,1,0:T(8,128)(2,1)S(1)} all-to-all(bf16[4,96,1536]{2,1,0:T(8,128)(2,1)S(1)} %broadcast_in_dim.2), channel_id=1, replica_groups=mesh['group'=4,'fsdp'=32] {'group'}, dimensions={0} | all-to-all | bytes 2359296 | tf_op jit(solution)/shard_map/all_to_all | solution.py:20
  64.0 1.1 copy.19
  65.1 0.0 all-gather.2.cloned.1.call-update
  65.2 0.0 copy-done
  65.2 0.7 fusion
  65.9 0.0 copy-done.1
  65.9 0.0 copy-done.2
  65.9 287.8 %all-gather.2.cloned.1.call-done = bf16[3072,6144]{1,0:T(8,128)(2,1)} async-done(((bf16[96,6144]{1,0:T(8,128)(2,1)}), bf16[3072,6144]{1,0:T(8,128)(2,1)}) %all-gather.2.cloned.1.call-update) | async-done | bytes 37748752 | tf_op jit(solution)/shard_map/all_gather | solution.py:46
  353.7 0.0 copy-done.3
  353.7 26.8 %convolution_multiply_fusion = f32[512,6144]{1,0:T(8,128)} fusion(bf16[3072,6144]{1,0:T(8,128)(2,1)} %all-gather.2.cloned.1.call-done, bf16[512,3072]{1,0:T(8,128)(2,1)S(1)} %copy-done, f32[3072]{0:T(1024)S(1)} %copy-done.3, f32[512]{0:T(512)S(1)} %add_rsqrt_fusion.2), kind=kOutput, calls=%fused_computation | convolution fusion | flops 19336790016 | bytes 53491712 | tf_op jit(solution)/shard_map/dot_general | solution.py:44
  380.4 9.0 %multiply_bitcast_fusion = (f32[64,8,24,128]{3,1,2,0:T(8,128)S(1)}, f32[64,8,24,128]{3,1,2,0:T(8,128)}) fusion(f32[512,6144]{1,0:T(8,128)} %convolution_multiply_fusion), kind=kLoop, calls=%fused_computation.12 | loop fusion | flops 3145728 | bytes 25165824
  389.5 4.0 copy.22
  393.5 4.5 %reduce_sum.29 = f32[512,24]{1,0:T(8,128)S(1)} reduce(f32[512,24,128]{2,1,0:T(8,128)} %bitcast.30, f32[]{:T(128)} %constant.7.clone.1), dimensions={2}, to_apply=%region_3.0 | reduce | flops 1560576 | bytes 6340612 | tf_op jit(solution)/shard_map/reduce_sum | solution.py:29
  398.0 0.1 copy.17
  398.1 0.1 copy.18
  398.3 6.8 %copy.20 = f32[64,8,24,128]{3,2,1,0:T(8,128)} copy(f32[64,8,24,128]{3,1,2,0:T(8,128)} %get-tuple-element.9) | data formatting | bytes 12582912
  405.1 4.5 %reduce_sum.28 = f32[512,24]{1,0:T(8,128)S(1)} reduce(f32[512,24,128]{2,1,0:T(8,128)} %bitcast.29, f32[]{:T(128)} %constant.7.clone.1), dimensions={2}, to_apply=%region_2.0 | reduce | flops 1560576 | bytes 6340612 | tf_op jit(solution)/shard_map/reduce_sum | solution.py:29
  409.6 0.1 copy.15
  409.7 0.1 copy.16
  409.8 1.8 mul.119
  411.6 1.8 mul.110
  413.4 9.2 %fusion.4 = (bf16[512,3072]{1,0:T(8,128)(2,1)}, bf16[512,3072]{1,0:T(8,128)(2,1)}) fusion(f32[64,8,24,128]{3,2,1,0:T(8,128)S(1)} %bitcast.31, f32[512,6144]{1,0:T(8,128)} %convolution_multiply_fusion, f32[3072]{0:T(1024)S(1)} %get-tuple-element.11, f32[3072]{0:T(1024)S(1)} %get-tuple-element.12, f32[64,8,24,128]{3,2,1,0:T(8,128)S(1)} %bitcast.32), kind=kLoop, calls=%fused_computation.8 | loop fusion | flops 9437184 | bytes 31481856 | tf_op jit(solution)/shard_map/convert_element_type | solution.py:30
  (4 shorter events, 0.1 us)
Async XLA Ops:
  7.2 58.0 %copy-start = (bf16[512,3072]{1,0:T(8,128)(2,1)S(1)}, bf16[512,3072]{1,0:T(8,128)(2,1)}, u32[]{:S(2)}) copy-start(bf16[512,3072]{1,0:T(8,128)(2,1)} %param.6) | copy-start | bytes 9437188
  7.2 36.1 %reduce-scatter.2.cloned.1.call-start = ((), (), s32[]{:S(2)}) async-start(), calls=%async_computation.2 | async-start | bytes 2949120 | tf_op jit(solution)/shard_map/reduce_scatter | solution.py:41
  7.9 58.0 %copy-start.1 = (f32[128]{0:T(128)S(1)}, f32[128]{0:T(128)}, u32[]{:S(2)}) copy-start(f32[128]{0:T(128)} %param.11) | copy-start | bytes 1540
  7.9 58.0 %copy-start.2 = (f32[128]{0:T(128)S(1)}, f32[128]{0:T(128)}, u32[]{:S(2)}) copy-start(f32[128]{0:T(128)} %param.10) | copy-start | bytes 1540
  7.9 345.7 %copy-start.3 = (f32[3072]{0:T(1024)S(1)}, f32[3072]{0:T(1024)}, u32[]{:S(2)}) copy-start(f32[3072]{0:T(1024)} %param.9) | copy-start | bytes 36868
  7.9 345.7 %all-gather.2.cloned.1.call-start = ((), (), s32[]{:S(2)}) async-start(), calls=%async_computation.3 | async-start | bytes 38928384 | tf_op jit(solution)/shard_map/all_gather | solution.py:46
Sparse Core Ops, SparseCore 0:
  10.4 32.8 reduce-scatter.1
  65.3 288.3 all-gather.1
where the time goes:
time: 430 us; the launch traced here: 429 us
  waiting for transfers between devices  324 us (75%)
  other arithmetic  30.4 us (7%)
  matrix products  26.8 us (6%)
  blocking collectives  18.3 us (4%)
  local copies, waits for them, and re-layouts  16.1 us (4%)
  between operations  14.2 us (3%)
    all_gather x1, waiting for transfers between devices, shards(): lax.all_gather(whole_rows, 'fsdp', axis=0, tiled=True)  288 us
    reduce_scatter x1, waiting for transfers between devices, shards(): lax.psum_scatter(local_part, 'group', scatter_dimension=1, tiled=True)  35.3 us
    dot_general x1, matrix products, shards(): jnp.dot(normed, lax.all_gather(whole_rows, 'fsdp', axis=0, tiled=True), p...  26.8 us
    all_to_all x1, blocking collectives, sent_to_all(): return lax.all_to_all(copies, axis, split_axis=0, concat_axis=0, tiled=True)  18.3 us
    unnamed x10, local copies, waits for them, and re-layouts  10.9 us
    convert_element_type x1, other arithmetic, head_norm(): return scaled.reshape(values.shape[0], model_width).astype(jnp.bfloat16)  9.22 us
    unnamed x1, other arithmetic  9.05 us
    reduce_sum x2, other arithmetic, head_norm(): jnp.mean(shaped * shaped, axis=-1, keepdims=True) + 1e-06  8.98 us
  transfers between devices with their start and end apart: 2, of which 2 were waited for; matrix products, arithmetic and copies ran while one was open for 0% of the time, Pallas kernels for 0%

commit v1 on v0

v1 whole, which is shorter than its diff:
```python
import jax
import jax.numpy as jnp
import numpy as np
from jax import lax
from jax.experimental import pallas as pl
from jax.experimental.pallas import tpu as pltpu
from jax.sharding import Mesh
from jax.sharding import PartitionSpec as P

HEAD = 128
EMA = 0.99
COLORS = 3
PARTS = (384, 128)
FIRST, SECOND = (1, 3), (3, 1)
ORDER = (180, 156)
DIMS = (("x", "y", "z"), ("y", "z", "x"), ("z", "x", "y"))


def exchange(x, dim, masks):
    if dim == "z":
        axes = ("zlo", "core", "zhi")
        pairs = []
        for zlo in range(2):
            for core in range(2):
                for zhi in range(2):
                    z = (2 * zhi + zlo) ^ masks[core]
                    pairs.append(((zlo * 2 + core) * 2 + zhi, ((z % 2) * 2 + core) * 2 + z // 2))
    else:
        axes = ("core", dim)
        pairs = [(core * 4 + i, core * 4 + (i ^ masks[core])) for core in range(2) for i in range(4)]
    return lax.ppermute(x, axes, pairs)


def project_body(colors, n, n_held, *refs):
    _, own, other, gains = refs[:4]
    units = refs[4 : 4 + 4 * len(colors)]
    q_out, k_out, send_out, tok, held, tok_sem, sem = refs[4 + 4 * len(colors) + n_held :]
    half, width = own.shape
    rows = units[0].shape[1]
    order = ORDER[0] + (ORDER[1] - ORDER[0]) * lax.axis_index("core")
    place = {
        "x": lax.axis_index("x"),
        "y": lax.axis_index("y"),
        "z": 2 * lax.axis_index("zhi") + lax.axis_index("zlo"),
    }

    def step(dim, i):
        return lax.bitwise_xor(place[dim], lax.bitwise_and(lax.shift_right_logical(order, 2 * i), 3))

    def fetch(c):
        dims = DIMS[colors[c]]
        for u in range(4):
            src = units[4 * c + u]

            def one(pos, carry):
                at = dict(zip(dims, (step(dims[0], pos % 4), step(dims[1], pos // 4), step(dims[2], jnp.int32(u)))))
                row = (at["y"] * 4 + at["x"]) * 2 + at["z"] // 2
                pltpu.make_async_copy(
                    src.at[pos],
                    held.at[
                        c,
                        pl.ds(pl.multiple_of(row * rows, rows), rows),
                        pl.ds(pl.multiple_of((at["z"] % 2) * n, HEAD), n),
                    ],
                    sem.at[c],
                ).start()
                return carry

            lax.fori_loop(0, 16, one, 0)

    first = pltpu.make_async_copy(own, tok.at[0], tok_sem.at[0])
    second = pltpu.make_async_copy(other, tok.at[1], tok_sem.at[1])
    first.start()
    fetch(0)
    second.start()
    for c in range(1, len(colors)):
        fetch(c)
    scale = width ** (-0.5)
    tile = 256
    for c in range(len(colors)):
        pltpu.make_async_copy(held.at[c], held.at[c], sem.at[c]).wait()
        for t, copy in enumerate((first, second)):
            if c == 0:
                copy.wait()
            for m in range(0, half, tile):
                y = jnp.dot(tok[t, m : m + tile, :], held[c], preferred_element_type=jnp.float32) * scale
                for i, out in enumerate((q_out, k_out)):
                    for h in range(0, n, HEAD):
                        v = y[:, i * n + h : i * n + h + HEAD]
                        v = v * lax.rsqrt(jnp.mean(v * v, axis=-1, keepdims=True) + 1e-06) * gains[i : i + 1, :]
                        v = v.astype(jnp.bfloat16)
                        at = c * n + h
                        if t == 0:
                            out[m : m + tile, at : at + HEAD] = v
                        else:
                            send_out[i, m : m + tile, at : at + HEAD] = v


def project(colors, block, core, own, other, gains, units, outputs):
    half, width = own.shape
    n = units[0].shape[2]
    col = lambda i, core: (0, core[0] * 4 + block)
    wide = n * len(colors)
    any_spec = pl.BlockSpec(memory_space=pl.ANY)
    operands = [own, other, gains, *units]
    specs = [any_spec, any_spec, pl.BlockSpec(gains.shape, lambda *_: (0, 0))] + [any_spec] * len(units)
    aliases = {}
    if outputs:
        aliases = {1 + len(operands): 0, 2 + len(operands): 1}
        operands += list(outputs)
        specs += [any_spec] * 2
    big = jax.ShapeDtypeStruct((half, width), jnp.bfloat16)
    return pl.pallas_call(
        lambda *refs: project_body(colors, n, len(outputs), *refs),
        grid_spec=pltpu.PrefetchScalarGridSpec(
            num_scalar_prefetch=1,
            grid=(1,),
            in_specs=specs,
            out_specs=[
                pl.BlockSpec((half, wide), col),
                pl.BlockSpec((half, wide), col),
                pl.BlockSpec((2, half, wide), lambda *_: (0, 0, 0)),
            ],
            scratch_shapes=[
                pltpu.VMEM((2, half, width), jnp.bfloat16),
                pltpu.VMEM((len(colors), width, 2 * n), jnp.bfloat16),
                pltpu.SemaphoreType.DMA((2,)),
                pltpu.SemaphoreType.DMA((len(colors),)),
            ],
        ),
        out_shape=[big, big, jax.ShapeDtypeStruct((2, half, wide), jnp.bfloat16)],
        input_output_aliases=aliases,
        compiler_params=pltpu.CompilerParams(vmem_limit_bytes=28 * 2**20),
        cost_estimate=pl.CostEstimate(
            flops=2 * 2 * half * width * 2 * wide,
            bytes_accessed=2 * width * (2 * half + 2 * wide),
            transcendentals=0,
        ),
    )(core, *operands)


def place_body(n_got, core, *refs):
    q_out, k_out = refs[n_got + 2 :]
    for i in range(n_got):

        @pl.when(pl.program_id(0) == i)
        def _():
            q_out[...] = refs[i][0]
            k_out[...] = refs[i][1]


def put(block, core, got, query, key_out):
    half = query.shape[0]
    wide = got[0].shape[2]
    col = lambda i, core: (0, (1 - core[0]) * 4 + block + i)
    any_spec = pl.BlockSpec(memory_space=pl.ANY)
    return pl.pallas_call(
        lambda *refs: place_body(len(got), *refs),
        grid_spec=pltpu.PrefetchScalarGridSpec(
            num_scalar_prefetch=1,
            grid=(len(got),),
            in_specs=[pl.BlockSpec(g.shape, lambda *_: (0, 0, 0)) for g in got] + [any_spec, any_spec],
            out_specs=[pl.BlockSpec((half, wide), col), pl.BlockSpec((half, wide), col)],
        ),
        out_shape=[jax.ShapeDtypeStruct(query.shape, query.dtype)] * 2,
        input_output_aliases={1 + len(got): 0, 2 + len(got): 1},
        compiler_params=pltpu.CompilerParams(vmem_limit_bytes=16 * 2**20),
        cost_estimate=pl.CostEstimate(flops=10**9, bytes_accessed=4 * sum(g.size for g in got), transcendentals=0),
    )(core, *got, query, key_out)


def shards(tokens, student, teacher, norm_gain, query_gain, key_gain):
    block = teacher.shape[1]
    core = lax.axis_index("core")
    zlo = lax.axis_index("zlo")
    swap = [(0, 1), (1, 0)]
    part_cols = [[slice(k * PARTS[0], (k + 1) * PARTS[0]), slice(3 * PARTS[0] + k * PARTS[1], 3 * PARTS[0] + (k + 1) * PARTS[1])] for k in range(COLORS)]

    local = student[0]
    blocks = [local[:, j * block : (j + 1) * block] for j in range(4)]
    give = jnp.stack([jnp.where(core == 0, blocks[2 * j + 1], blocks[2 * j]) for j in range(2)])
    got = lax.ppermute(give, "core", swap)
    pair = jnp.stack([jnp.where(core == 0, blocks[2 * j], blocks[2 * j + 1]) for j in range(2)]) + got
    keep = jnp.where(zlo == 0, pair[0], pair[1])
    give = jnp.where(zlo == 0, pair[1], pair[0])
    arrived = []
    for k in range(COLORS):
        cut = jnp.concatenate([give[:, c] for c in part_cols[k]], axis=1)
        arrived.append(lax.ppermute(cut, "zlo", swap))
    owned, copied = [], []
    for k in range(COLORS):
        cut = jnp.concatenate([keep[:, c] for c in part_cols[k]], axis=1)
        if k:
            cut, _ = lax.optimization_barrier((cut, copied[-1]))
        owned.append((cut + arrived[k]) / 4)
        copied.append(owned[-1].astype(jnp.bfloat16)[None])

    wide = tokens.astype(jnp.float32)
    normed = (
        wide * lax.rsqrt(jnp.mean(wide * wide, axis=-1, keepdims=True) + 1e-06) * norm_gain
    ).astype(jnp.bfloat16)
    other = lax.ppermute(normed, "core", swap)

    for phase in range(2):
        for s, masks in enumerate((FIRST, SECOND)):
            got = []
            for k in range(COLORS):
                got.append(exchange(copied[k], DIMS[k][phase], masks))
            if (phase, s) != (1, 1):
                copied = [jnp.concatenate([a, b], axis=0) for a, b in zip(copied, got)]
    units = []
    bounds = ((0, PARTS[0]), (PARTS[0], PARTS[0] + PARTS[1]))
    held = [[jnp.concatenate([a[:, :, lo:hi], b[:, :, lo:hi]], axis=0) for a, b in zip(copied, got)] for lo, hi in bounds]
    for part in range(2):
        one, two, three = [], [], []
        for k in range(COLORS):
            one.append(exchange(held[part][k], DIMS[k][2], FIRST))
            two.append(exchange(held[part][k], DIMS[k][2], SECOND))
            three.append(exchange(one[k], DIMS[k][2], SECOND))
        units.append([[held[part][k], one[k], two[k], three[k]] for k in range(COLORS)])

    core_at = core.astype(jnp.int32).reshape(1)
    gains = jnp.stack([query_gain, key_gain])
    outputs, got = (), []
    for k in range(COLORS):
        *outputs, send = project((k,), k, core_at, normed, other, gains, units[0][k], outputs)
        got.append(lax.ppermute(send, "core", swap))
    *outputs, send = project((0, 1, 2), 3, core_at, normed, other, gains, sum(units[1], []), outputs)
    last = lax.ppermute(send, "core", swap)
    outputs = put(0, core_at, got, *outputs)
    outputs = put(3, core_at, [last], *outputs)

    whole = [owned[k][:, : PARTS[0]] for k in range(COLORS)] + [owned[k][:, PARTS[0] :] for k in range(COLORS)]
    student_new = jnp.concatenate(whole, axis=1)
    teacher_new = EMA * teacher + (1.0 - EMA) * student_new
    return (teacher_new, student_new, *outputs)


def solution(mesh):
    split = Mesh(np.asarray(mesh.devices).reshape(2, 2, 4, 4, 2), ("zlo", "core", "y", "x", "zhi"))
    group, fsdp = ("zlo", "core"), ("y", "x", "zhi")
    rows = P(group + fsdp, None)

    return jax.shard_map(
        shards,
        mesh=split,
        in_specs=(rows, P(group, fsdp, None), P(fsdp, group), P(), P(), P()),
        out_specs=(P(fsdp, group), P(fsdp, group), rows, rows),
        check_vma=False,
    )
```

time: 430 us -> 171 us (0.40)
  waiting for transfers between devices: 324 us -> 53.5 us
  starting transfers between devices: 0.08 us -> 65 us
  Pallas kernels: 0 us -> 38.8 us
  matrix products: 26.8 us -> 0 us
  other arithmetic: 30.4 us -> 9.92 us
  blocking collectives: 18.3 us -> 0 us
  local copies, waits for them, and re-layouts: 16.1 us -> 1.18 us
  between operations: 14.2 us -> 1.1 us
    all_gather x1 -> x0, waiting for transfers between devices: 288 us -> none  [shards(): lax.all_gather(whole_rows, 'fsdp', axis=0, tiled=True)]
    ppermute x0 -> x39, starting transfers between devices: none -> 65 us  [the longest x30 59.1 us: exchange(): return lax.ppermute(x, axes, pairs)]
    ppermute x0 -> x39, waiting for transfers between devices: none -> 53.5 us  [the longest x30 46.8 us: exchange(): return lax.ppermute(x, axes, pairs)]
    pallas_call x0 -> x6, Pallas kernels: none -> 38.8 us  [the longest x4 35.9 us: project(): pl.pallas_call(lambda *refs: project_body(colors, n, len(outputs), *refs)...]
    reduce_scatter x1 -> x0, waiting for transfers between devices: 35.3 us -> none  [shards(): lax.psum_scatter(local_part, 'group', scatter_dimension=1, tiled=True)]
    dot_general x1 -> x0, matrix products: 26.8 us -> none  [shards(): jnp.dot(normed, lax.all_gather(whole_rows, 'fsdp', axis=0, tiled=True), p...]
    all_to_all x1 -> x0, blocking collectives: 18.3 us -> none  [sent_to_all(): return lax.all_to_all(copies, axis, split_axis=0, concat_axis=0, tiled=True)]
    convert_element_type x2 -> x1, other arithmetic: 11.6 us -> 1.22 us  [shards(): normed = (wide * lax.rsqrt(jnp.mean(wide * wide, axis=-1, keepdims=True)...]
  transfers between devices with their start and end apart: 2 -> 39, of which waited for: 2 -> 18; matrix products, arithmetic and copies ran while one was open for 0% -> 4% of each run, Pallas kernels for 0% -> 22%
where the time goes in v1:
time: 171 us; the launch traced here: 170 us
  starting transfers between devices  65 us (38%)
  waiting for transfers between devices  53.5 us (31%)
  Pallas kernels  38.8 us (23%)
  other arithmetic  9.92 us (6%)
    ppermute x30, starting transfers between devices, exchange(): return lax.ppermute(x, axes, pairs)  59.1 us
    ppermute x30, waiting for transfers between devices, exchange(): return lax.ppermute(x, axes, pairs)  46.8 us
    pallas_call x4, Pallas kernels, project(): pl.pallas_call(lambda *refs: project_body(colors, n, len(outputs), *refs)...  35.9 us
    ppermute x3, waiting for transfers between devices, shards(): arrived.append(lax.ppermute(cut, 'zlo', swap))  6 us
    ppermute x3, starting transfers between devices, shards(): arrived.append(lax.ppermute(cut, 'zlo', swap))  4.29 us
  transfers between devices with their start and end apart: 39, of which 18 were waited for; matrix products, arithmetic and copies ran while one was open for 4% of the time, Pallas kernels for 22%

profile of v1, /device:TPU:0, one launch (start us, length us, event | category | flops | bytes accessed | tf_op | source)
XLA Modules:
  0.0 169.5 jit_solution(16617240882919811584)
XLA Ops:
  0.6 3.0 %select_bitcast_fusion.5 = (f32[1,96,1536]{2,1,0:T(8,128)}, f32[1,96,1536]{2,1,0:T(8,128)}, f32[1,96,1536]{2,1,0:T(8,128)S(1)}, f32[1,96,1536]{2,1,0:T(8,128)S(1)}) fusion(f32[96,6144]{1,0:T(8,128)} %bitcast.22, pred[]{:T(512)S(6)} %eq.5), kind=kLoop, calls=%fused_computation.19 | loop fusion | flops 589824 | bytes 4718593 | tf_op jit(solution)/shard_map/stack | solution.py:183
  9.9 2.1 %collective-permute-start.1 = (f32[96,512]{1,0:T(8,128)S(1)}, f32[96,512]{1,0:T(8,128)S(1)}, u32[]{:S(2)}, u32[]{:S(2)}) collective-permute-start(f32[96,512]{1,0:T(8,128)S(1)} %pad_maximum_fusion.13), channel_id=1, source_target_pairs={{0,64},{64,0},{1,65},{65,1},{2,66},{66,2},{3,67},{67,3},{4,68},{68... | collective-permute-start | bytes 589832 | tf_op jit(solution)/shard_map/ppermute | solution.py:189
  12.1 2.1 %collective-permute-start.3 = (f32[96,512]{1,0:T(8,128)S(1)}, f32[96,512]{1,0:T(8,128)S(1)}, u32[]{:S(2)}, u32[]{:S(2)}) collective-permute-start(f32[96,512]{1,0:T(8,128)S(1)} %pad_maximum_fusion.17), channel_id=1, source_target_pairs={{0,64},{64,0},{1,65},{65,1},{2,66},{66,2},{3,67},{67,3},{4,68},{68... | collective-permute-start | bytes 589832 | tf_op jit(solution)/shard_map/ppermute | solution.py:189
  14.3 3.5 %collective-permute-done.1 = f32[96,512]{1,0:T(8,128)S(1)} collective-permute-done((f32[96,512]{1,0:T(8,128)S(1)}, f32[96,512]{1,0:T(8,128)S(1)}, u32[]{:S(2)}, u32[]{:S(2)}) %collective-permute-start.1) | collective-permute-done | bytes 196640 | tf_op jit(solution)/shard_map/ppermute | solution.py:189
  19.5 2.5 %collective-permute-done.2 = f32[96,512]{1,0:T(8,128)S(1)} collective-permute-done((f32[96,512]{1,0:T(8,128)S(1)}, f32[96,512]{1,0:T(8,128)S(1)}, u32[]{:S(2)}, u32[]{:S(2)}) %collective-permute-start.2) | collective-permute-done | bytes 196640 | tf_op jit(solution)/shard_map/ppermute | solution.py:189
  23.8 2.8 %collective-permute-start.6 = (bf16[2,96,512]{2,1,0:T(8,128)(2,1)S(1)}, bf16[2,96,512]{2,1,0:T(8,128)(2,1)S(1)}, u32[]{:S(2)}, u32[]{:S(2)}) collective-permute-start(bf16[2,96,512]{2,1,0:T(8,128)(2,1)S(1)} %pad_maximum_fusion.18), channel_id=1, source_target_pairs={{0,6},{2,4},{4,2},{6,0},{32,34},{34,32},{36,38},{38,36},{1,7},{3,5... | collective-permute-start | bytes 589832 | tf_op jit(solution)/shard_map/ppermute | solution.py:31
  26.7 2.0 %collective-permute-start.19 = (bf16[1,96,512]{2,1,0:T(8,128)(2,1)S(1)}, bf16[1,96,512]{2,1,0:T(8,128)(2,1)S(1)}, u32[]{:S(2)}, u32[]{:S(2)}) collective-permute-start(bf16[1,96,512]{2,1,0:T(8,128)(2,1)S(1)} %get-tuple-element.40), channel_id=1, source_target_pairs={{0,64},{1,65},{32,97},{33,96},{64,0},{65,1},{96,33},{97,32},{2,66}... | collective-permute-start | bytes 294920 | tf_op jit(solution)/shard_map/ppermute | solution.py:31
  28.7 2.1 %collective-permute-done.6 = bf16[2,96,512]{2,1,0:T(8,128)(2,1)S(1)} collective-permute-done((bf16[2,96,512]{2,1,0:T(8,128)(2,1)S(1)}, bf16[2,96,512]{2,1,0:T(8,128)(2,1)S(1)}, u32[]{:S(2)}, u32[]{:S(2)}) %collective-permute-start.6) | collective-permute-done | bytes 196640 | tf_op jit(solution)/shard_map/ppermute | solution.py:31
  31.3 3.1 %collective-permute-start.13 = (bf16[2,96,512]{2,1,0:T(8,128)(2,1)S(1)}, bf16[2,96,512]{2,1,0:T(8,128)(2,1)S(1)}, u32[]{:S(2)}, u32[]{:S(2)}) collective-permute-start(bf16[2,96,512]{2,1,0:T(8,128)(2,1)S(1)} %pad_maximum_fusion.19), channel_id=1, source_target_pairs={{0,24},{8,16},{16,8},{24,0},{32,40},{40,32},{48,56},{56,48},{1,25}... | collective-permute-start | bytes 589832 | tf_op jit(solution)/shard_map/ppermute | solution.py:31
  34.5 4.1 %collective-permute-start.20 = (bf16[2,96,512]{2,1,0:T(8,128)(2,1)S(1)}, bf16[2,96,512]{2,1,0:T(8,128)(2,1)S(1)}, u32[]{:S(2)}, u32[]{:S(2)}) collective-permute-start(bf16[2,96,512]{2,1,0:T(8,128)(2,1)S(1)} %pad_maximum_fusion.20), channel_id=1, source_target_pairs={{0,65},{1,64},{32,96},{33,97},{64,1},{65,0},{96,32},{97,33},{2,67}... | collective-permute-start | bytes 589832 | tf_op jit(solution)/shard_map/ppermute | solution.py:31
  40.6 3.0 %collective-permute-start.8 = (bf16[8,96,512]{2,1,0:T(8,128)(2,1)S(1)}, bf16[8,96,512]{2,1,0:T(8,128)(2,1)S(1)}, u32[]{:S(2)}, u32[]{:S(2)}) collective-permute-start(bf16[8,96,512]{2,1,0:T(8,128)(2,1)S(1)} %pad_maximum_fusion.4), channel_id=1, source_target_pairs={{0,24},{8,16},{16,8},{24,0},{32,40},{40,32},{48,56},{56,48},{1,25}... | collective-permute-start | bytes 2359304 | tf_op jit(solution)/shard_map/ppermute | solution.py:31
  44.0 2.8 %collective-permute-done.14 = bf16[4,96,512]{2,1,0:T(8,128)(2,1)S(1)} collective-permute-done((bf16[4,96,512]{2,1,0:T(8,128)(2,1)S(1)}, bf16[4,96,512]{2,1,0:T(8,128)(2,1)S(1)}, u32[]{:S(2)}, u32[]{:S(2)}) %collective-permute-start.14) | collective-permute-done | bytes 393248 | tf_op jit(solution)/shard_map/ppermute | solution.py:31
  46.9 3.5 %collective-permute-start.15 = (bf16[8,96,512]{2,1,0:T(8,128)(2,1)S(1)}, bf16[8,96,512]{2,1,0:T(8,128)(2,1)S(1)}, u32[]{:S(2)}, u32[]{:S(2)}) collective-permute-start(bf16[8,96,512]{2,1,0:T(8,128)(2,1)S(1)} %pad_maximum_fusion.5), channel_id=1, source_target_pairs={{0,65},{1,64},{32,96},{33,97},{64,1},{65,0},{96,32},{97,33},{2,67}... | collective-permute-start | bytes 2359304 | tf_op jit(solution)/shard_map/ppermute | solution.py:31
  50.5 3.5 %collective-permute-done.21 = bf16[4,96,512]{2,1,0:T(8,128)(2,1)S(1)} collective-permute-done((bf16[4,96,512]{2,1,0:T(8,128)(2,1)S(1)}, bf16[4,96,512]{2,1,0:T(8,128)(2,1)S(1)}, u32[]{:S(2)}, u32[]{:S(2)}) %collective-permute-start.21) | collective-permute-done | bytes 393248 | tf_op jit(solution)/shard_map/ppermute | solution.py:31
  54.1 2.8 %collective-permute-start.22 = (bf16[8,96,512]{2,1,0:T(8,128)(2,1)S(1)}, bf16[8,96,512]{2,1,0:T(8,128)(2,1)S(1)}, u32[]{:S(2)}, u32[]{:S(2)}) collective-permute-start(bf16[8,96,512]{2,1,0:T(8,128)(2,1)S(1)} %pad_maximum_fusion.6), channel_id=1, source_target_pairs={{0,6},{2,4},{4,2},{6,0},{32,34},{34,32},{36,38},{38,36},{1,7},{3,5... | collective-permute-start | bytes 2359304 | tf_op jit(solution)/shard_map/ppermute | solution.py:31
  57.3 9.7 %collective-permute-done.15 = bf16[8,96,512]{2,1,0:T(8,128)(2,1)S(1)} collective-permute-done((bf16[8,96,512]{2,1,0:T(8,128)(2,1)S(1)}, bf16[8,96,512]{2,1,0:T(8,128)(2,1)S(1)}, u32[]{:S(2)}, u32[]{:S(2)}) %collective-permute-start.15) | collective-permute-done | bytes 786464 | tf_op jit(solution)/shard_map/ppermute | solution.py:31
  68.6 3.6 %collective-permute-start.33 = (bf16[16,96,384]{2,1,0:T(8,128)(2,1)S(1)}, bf16[16,96,384]{2,1,0:T(8,128)(2,1)S(1)}, u32[]{:S(2)}, u32[]{:S(2)}) collective-permute-start(bf16[16,96,384]{2,1,0:T(8,128)(2,1)S(1)} %pad_maximum_fusion.3.refs_4_), channel_id=1, source_target_pairs={{0,65},{1,64},{32,96},{33,97},{64,1},{65,0},{96,32},{97,33},{2,67}... | collective-permute-start | bytes 3538952 | tf_op jit(solution)/shard_map/ppermute | solution.py:31
  73.5 9.9 %collective-permute-done.32.refs_5_ = bf16[16,96,384]{2,1,0:T(8,128)(2,1)S(1)} collective-permute-done((bf16[16,96,384]{2,1,0:T(8,128)(2,1)S(1)}, bf16[16,96,384]{2,1,0:T(8,128)(2,1)S(1)}, u32[]{:S(2)}, u32[]{:S(2)}) %collective-permute-start.32) | collective-permute-done | bytes 1179680 | tf_op jit(solution)/shard_map/ppermute | solution.py:31
  83.4 6.6 %collective-permute-start.34 = (bf16[16,96,384]{2,1,0:T(8,128)(2,1)S(1)}, bf16[16,96,384]{2,1,0:T(8,128)(2,1)S(1)}, u32[]{:S(2)}, u32[]{:S(2)}) collective-permute-start(bf16[16,96,384]{2,1,0:T(8,128)(2,1)S(1)} %collective-permute-done.32.refs_5_), channel_id=1, source_target_pairs={{0,65},{1,64},{32,96},{33,97},{64,1},{65,0},{96,32},{97,33},{2,67}... | collective-permute-start | bytes 3538952 | tf_op jit(solution)/shard_map/ppermute | solution.py:31
  90.9 2.9 %collective-permute-start.31 = (bf16[16,96,384]{2,1,0:T(8,128)(2,1)S(1)}, bf16[16,96,384]{2,1,0:T(8,128)(2,1)S(1)}, u32[]{:S(2)}, u32[]{:S(2)}) collective-permute-start(bf16[16,96,384]{2,1,0:T(8,128)(2,1)S(1)} %collective-permute-done.29.refs_5_), channel_id=1, source_target_pairs={{0,6},{2,4},{4,2},{6,0},{32,34},{34,32},{36,38},{38,36},{1,7},{3,5... | collective-permute-start | bytes 3538952 | tf_op jit(solution)/shard_map/ppermute | solution.py:31
  93.9 7.8 %collective-permute-start.27 = (bf16[16,96,384]{2,1,0:T(8,128)(2,1)S(1)}, bf16[16,96,384]{2,1,0:T(8,128)(2,1)S(1)}, u32[]{:S(2)}, u32[]{:S(2)}) collective-permute-start(bf16[16,96,384]{2,1,0:T(8,128)(2,1)S(1)} %pad_maximum_fusion.1.refs_4_), channel_id=1, source_target_pairs={{0,24},{8,16},{16,8},{24,0},{32,40},{40,32},{48,56},{56,48},{1,25}... | collective-permute-start | bytes 3538952 | tf_op jit(solution)/shard_map/ppermute | solution.py:31
  102.0 2.1 %collective-permute-done.34.refs_7_ = bf16[16,96,384]{2,1,0:T(8,128)(2,1)S(1)} collective-permute-done((bf16[16,96,384]{2,1,0:T(8,128)(2,1)S(1)}, bf16[16,96,384]{2,1,0:T(8,128)(2,1)S(1)}, u32[]{:S(2)}, u32[]{:S(2)}) %collective-permute-start.34) | collective-permute-done | bytes 1179680 | tf_op jit(solution)/shard_map/ppermute | solution.py:31
  104.2 8.0 %shard_map.93 = (bf16[512,3072]{1,0:T(8,128)(2,1)}, bf16[512,3072]{1,0:T(8,128)(2,1)}, bf16[2,512,384]{2,1,0:T(8,128)(2,1)S(1)}) custom-call(s32[1]{0:T(128)} %bitcast.9.refs_0_, bf16[512,3072]{1,0:T(8,128)(2,1)S(1)} %fusion.2.refs_1_, bf16[512,3072]{1,0:T(8,128)(2,1)} %collective-permute-done.4.refs_2_, f32[2,128]{1,0:T(2,128)S(1)} %pad_maximum_fusion.21.refs_3_, ...), custom_call_target="tpu_custom_call" | custom-call | flops 4831838208 | bytes 11010048 | tf_op jit(solution)/shard_map/pallas_call | solution.py:113
  112.2 4.0 %collective-permute-done.23.refs_13_ = bf16[16,96,128]{2,1,0:T(8,128)(2,1)S(1)} collective-permute-done((bf16[16,96,128]{2,1,0:T(8,128)(2,1)S(1)}, bf16[16,96,128]{2,1,0:T(8,128)(2,1)S(1)}, u32[]{:S(2)}, u32[]{:S(2)}) %collective-permute-start.23) | collective-permute-done | bytes 393248 | tf_op jit(solution)/shard_map/ppermute | solution.py:31
  117.4 6.9 %collective-permute-done.31.refs_7_ = bf16[16,96,384]{2,1,0:T(8,128)(2,1)S(1)} collective-permute-done((bf16[16,96,384]{2,1,0:T(8,128)(2,1)S(1)}, bf16[16,96,384]{2,1,0:T(8,128)(2,1)S(1)}, u32[]{:S(2)}, u32[]{:S(2)}) %collective-permute-start.31) | collective-permute-done | bytes 1179680 | tf_op jit(solution)/shard_map/ppermute | solution.py:31
  124.4 8.0 %shard_map.94 = (bf16[512,3072]{1,0:T(8,128)(2,1)}, bf16[512,3072]{1,0:T(8,128)(2,1)}, bf16[2,512,384]{2,1,0:T(8,128)(2,1)S(1)}) custom-call(s32[1]{0:T(128)} %bitcast.9.refs_0_, bf16[512,3072]{1,0:T(8,128)(2,1)S(1)} %fusion.2.refs_1_, bf16[512,3072]{1,0:T(8,128)(2,1)} %collective-permute-done.4.refs_2_, ...), custom_call_target="tpu_custom_call", output_to_operand_aliasing={{0}: (8, {}), {1}: (9, {})} | custom-call | flops 4831838208 | bytes 11010048 | tf_op jit(solution)/shard_map/pallas_call | solution.py:113
  132.4 3.9 %collective-permute-done.24.refs_14_ = bf16[16,96,128]{2,1,0:T(8,128)(2,1)S(1)} collective-permute-done((bf16[16,96,128]{2,1,0:T(8,128)(2,1)S(1)}, bf16[16,96,128]{2,1,0:T(8,128)(2,1)S(1)}, u32[]{:S(2)}, u32[]{:S(2)}) %collective-permute-start.24) | collective-permute-done | bytes 393248 | tf_op jit(solution)/shard_map/ppermute | solution.py:31
  136.8 4.5 %collective-permute-start.10 = (bf16[16,96,128]{2,1,0:T(8,128)(2,1)S(1)}, bf16[16,96,128]{2,1,0:T(8,128)(2,1)S(1)}, u32[]{:S(2)}, u32[]{:S(2)}) collective-permute-start(bf16[16,96,128]{2,1,0:T(8,128)(2,1)S(1)} %pad_maximum_fusion.8.refs_4_), channel_id=1, source_target_pairs={{0,65},{1,64},{32,96},{33,97},{64,1},{65,0},{96,32},{97,33},{2,67}... | collective-permute-start | bytes 1179656 | tf_op jit(solution)/shard_map/ppermute | solution.py:31
  141.5 2.8 %collective-permute-start.18 = (bf16[16,96,128]{2,1,0:T(8,128)(2,1)S(1)}, bf16[16,96,128]{2,1,0:T(8,128)(2,1)S(1)}, u32[]{:S(2)}, u32[]{:S(2)}) collective-permute-start(bf16[16,96,128]{2,1,0:T(8,128)(2,1)S(1)} %collective-permute-done.16.refs_9_), channel_id=1, source_target_pairs={{0,6},{2,4},{4,2},{6,0},{32,34},{34,32},{36,38},{38,36},{1,7},{3,5... | collective-permute-start | bytes 1179656 | tf_op jit(solution)/shard_map/ppermute | solution.py:31
  144.4 8.0 %shard_map.95 = (bf16[512,3072]{1,0:T(8,128)(2,1)}, bf16[512,3072]{1,0:T(8,128)(2,1)}, bf16[2,512,384]{2,1,0:T(8,128)(2,1)S(1)}) custom-call(s32[1]{0:T(128)} %bitcast.9.refs_0_, bf16[512,3072]{1,0:T(8,128)(2,1)S(1)} %fusion.2.refs_1_, bf16[512,3072]{1,0:T(8,128)(2,1)} %collective-permute-done.4.refs_2_, ...), custom_call_target="tpu_custom_call", output_to_operand_aliasing={{0}: (8, {}), {1}: (9, {})} | custom-call | flops 4831838208 | bytes 11010048 | tf_op jit(solution)/shard_map/pallas_call | solution.py:113
  153.3 11.9 %shard_map.96 = (bf16[512,3072]{1,0:T(8,128)(2,1)}, bf16[512,3072]{1,0:T(8,128)(2,1)}, bf16[2,512,384]{2,1,0:T(8,128)(2,1)S(1)}) custom-call(s32[1]{0:T(128)} %bitcast.9.refs_0_, bf16[512,3072]{1,0:T(8,128)(2,1)S(1)} %fusion.2.refs_1_, bf16[512,3072]{1,0:T(8,128)(2,1)} %collective-permute-done.4.refs_2_, ...), custom_call_target="tpu_custom_call", output_to_operand_aliasing={{0}: (16, {}), {1}: (17, {})} | custom-call | flops 4831838208 | bytes 11010048 | tf_op jit(solution)/shard_map/pallas_call | solution.py:113
  166.6 2.0 %shard_map.97 = (bf16[512,3072]{1,0:T(8,128)(2,1)}, bf16[512,3072]{1,0:T(8,128)(2,1)}) custom-call(s32[1]{0:T(128)} %bitcast.9.refs_0_, bf16[2,512,384]{2,1,0:T(8,128)(2,1)S(1)} %collective-permute-done.36.refs_1_, bf16[2,512,384]{2,1,0:T(8,128)(2,1)S(1)} %collective-permute-done.37.refs_2_, ...), custom_call_target="tpu_custom_call", output_to_operand_aliasing={{0}: (4, {}), {1}: (5, {})} | custom-call | flops 1000000000 | bytes 4718592 | tf_op jit(solution)/shard_map/pallas_call | solution.py:157
  (118 shorter events, 23.0 us)
Async XLA Ops:
  6.7 83.4 %collective-permute-start.4 = (bf16[512,3072]{1,0:T(8,128)(2,1)S(1)}, bf16[512,3072]{1,0:T(8,128)(2,1)}, u32[]{:S(2)}, u32[]{:S(2)}) collective-permute-start(bf16[512,3072]{1,0:T(8,128)(2,1)S(1)} %fusion.2.refs_1_), channel_id=1, source_target_pairs={{0,32},{32,0},{1,33},{33,1},{2,34},{34,2},{3,35},{35,3},{4,36},{36... | collective-permute-start | bytes 9437192 | tf_op jit(solution)/shard_map/ppermute | solution.py:202
  9.9 7.9 %collective-permute-start.1 = (f32[96,512]{1,0:T(8,128)S(1)}, f32[96,512]{1,0:T(8,128)S(1)}, u32[]{:S(2)}, u32[]{:S(2)}) collective-permute-start(f32[96,512]{1,0:T(8,128)S(1)} %pad_maximum_fusion.13), channel_id=1, source_target_pairs={{0,64},{64,0},{1,65},{65,1},{2,66},{66,2},{3,67},{67,3},{4,68},{68... | collective-permute-start | bytes 589832 | tf_op jit(solution)/shard_map/ppermute | solution.py:189
  12.0 9.9 %collective-permute-start.2 = (f32[96,512]{1,0:T(8,128)S(1)}, f32[96,512]{1,0:T(8,128)S(1)}, u32[]{:S(2)}, u32[]{:S(2)}) collective-permute-start(f32[96,512]{1,0:T(8,128)S(1)} %pad_maximum_fusion.15), channel_id=1, source_target_pairs={{0,64},{64,0},{1,65},{65,1},{2,66},{66,2},{3,67},{67,3},{4,68},{68... | collective-permute-start | bytes 589832 | tf_op jit(solution)/shard_map/ppermute | solution.py:189
  12.1 14.5 %collective-permute-start.3 = (f32[96,512]{1,0:T(8,128)S(1)}, f32[96,512]{1,0:T(8,128)S(1)}, u32[]{:S(2)}, u32[]{:S(2)}) collective-permute-start(f32[96,512]{1,0:T(8,128)S(1)} %pad_maximum_fusion.17), channel_id=1, source_target_pairs={{0,64},{64,0},{1,65},{65,1},{2,66},{66,2},{3,67},{67,3},{4,68},{68... | collective-permute-start | bytes 589832 | tf_op jit(solution)/shard_map/ppermute | solution.py:189
  22.0 9.3 %collective-permute-start.12 = (bf16[1,96,512]{2,1,0:T(8,128)(2,1)S(1)}, bf16[1,96,512]{2,1,0:T(8,128)(2,1)S(1)}, u32[]{:S(2)}, u32[]{:S(2)}) collective-permute-start(bf16[1,96,512]{2,1,0:T(8,128)(2,1)S(1)} %get-tuple-element.42), channel_id=1, source_target_pairs={{0,8},{8,0},{16,24},{24,16},{32,56},{40,48},{48,40},{56,32},{1,9},... | collective-permute-start | bytes 294920 | tf_op jit(solution)/shard_map/ppermute | solution.py:31
  30.8 9.7 %collective-permute-start.7 = (bf16[4,96,512]{2,1,0:T(8,128)(2,1)S(1)}, bf16[4,96,512]{2,1,0:T(8,128)(2,1)S(1)}, u32[]{:S(2)}, u32[]{:S(2)}) collective-permute-start(bf16[4,96,512]{2,1,0:T(8,128)(2,1)S(1)} %pad_maximum_fusion.7), channel_id=1, source_target_pairs={{0,8},{8,0},{16,24},{24,16},{32,56},{40,48},{48,40},{56,32},{1,9},... | collective-permute-start | bytes 1179656 | tf_op jit(solution)/shard_map/ppermute | solution.py:31
  34.5 9.4 %collective-permute-start.20 = (bf16[2,96,512]{2,1,0:T(8,128)(2,1)S(1)}, bf16[2,96,512]{2,1,0:T(8,128)(2,1)S(1)}, u32[]{:S(2)}, u32[]{:S(2)}) collective-permute-start(bf16[2,96,512]{2,1,0:T(8,128)(2,1)S(1)} %pad_maximum_fusion.20), channel_id=1, source_target_pairs={{0,65},{1,64},{32,96},{33,97},{64,1},{65,0},{96,32},{97,33},{2,67}... | collective-permute-start | bytes 589832 | tf_op jit(solution)/shard_map/ppermute | solution.py:31
  40.6 16.3 %collective-permute-start.8 = (bf16[8,96,512]{2,1,0:T(8,128)(2,1)S(1)}, bf16[8,96,512]{2,1,0:T(8,128)(2,1)S(1)}, u32[]{:S(2)}, u32[]{:S(2)}) collective-permute-start(bf16[8,96,512]{2,1,0:T(8,128)(2,1)S(1)} %pad_maximum_fusion.4), channel_id=1, source_target_pairs={{0,24},{8,16},{16,8},{24,0},{32,40},{40,32},{48,56},{56,48},{1,25}... | collective-permute-start | bytes 2359304 | tf_op jit(solution)/shard_map/ppermute | solution.py:31
  43.9 10.0 %collective-permute-start.21 = (bf16[4,96,512]{2,1,0:T(8,128)(2,1)S(1)}, bf16[4,96,512]{2,1,0:T(8,128)(2,1)S(1)}, u32[]{:S(2)}, u32[]{:S(2)}) collective-permute-start(bf16[4,96,512]{2,1,0:T(8,128)(2,1)S(1)} %pad_maximum_fusion.11), channel_id=1, source_target_pairs={{0,2},{2,0},{4,6},{6,4},{32,38},{34,36},{36,34},{38,32},{1,3},{3,1... | collective-permute-start | bytes 1179656 | tf_op jit(solution)/shard_map/ppermute | solution.py:31
  46.9 20.1 %collective-permute-start.15 = (bf16[8,96,512]{2,1,0:T(8,128)(2,1)S(1)}, bf16[8,96,512]{2,1,0:T(8,128)(2,1)S(1)}, u32[]{:S(2)}, u32[]{:S(2)}) collective-permute-start(bf16[8,96,512]{2,1,0:T(8,128)(2,1)S(1)} %pad_maximum_fusion.5), channel_id=1, source_target_pairs={{0,65},{1,64},{32,96},{33,97},{64,1},{65,0},{96,32},{97,33},{2,67}... | collective-permute-start | bytes 2359304 | tf_op jit(solution)/shard_map/ppermute | solution.py:31
  54.1 18.7 %collective-permute-start.22 = (bf16[8,96,512]{2,1,0:T(8,128)(2,1)S(1)}, bf16[8,96,512]{2,1,0:T(8,128)(2,1)S(1)}, u32[]{:S(2)}, u32[]{:S(2)}) collective-permute-start(bf16[8,96,512]{2,1,0:T(8,128)(2,1)S(1)} %pad_maximum_fusion.6), channel_id=1, source_target_pairs={{0,6},{2,4},{4,2},{6,0},{32,34},{34,32},{36,38},{38,36},{1,7},{3,5... | collective-permute-start | bytes 2359304 | tf_op jit(solution)/shard_map/ppermute | solution.py:31
  57.1 26.3 %collective-permute-start.32 = (bf16[16,96,384]{2,1,0:T(8,128)(2,1)S(1)}, bf16[16,96,384]{2,1,0:T(8,128)(2,1)S(1)}, u32[]{:S(2)}, u32[]{:S(2)}) collective-permute-start(bf16[16,96,384]{2,1,0:T(8,128)(2,1)S(1)} %pad_maximum_fusion.3.refs_4_), channel_id=1, source_target_pairs={{0,64},{1,65},{32,97},{33,96},{64,0},{65,1},{96,33},{97,32},{2,66}... | collective-permute-start | bytes 3538952 | tf_op jit(solution)/shard_map/ppermute | solution.py:31
  67.2 23.7 %collective-permute-start.29 = (bf16[16,96,384]{2,1,0:T(8,128)(2,1)S(1)}, bf16[16,96,384]{2,1,0:T(8,128)(2,1)S(1)}, u32[]{:S(2)}, u32[]{:S(2)}) collective-permute-start(bf16[16,96,384]{2,1,0:T(8,128)(2,1)S(1)} %pad_maximum_fusion.2.refs_4_), channel_id=1, source_target_pairs={{0,2},{2,0},{4,6},{6,4},{32,38},{34,36},{36,34},{38,32},{1,3},{3,1... | collective-permute-start | bytes 3538952 | tf_op jit(solution)/shard_map/ppermute | solution.py:31
  68.6 25.3 %collective-permute-start.33 = (bf16[16,96,384]{2,1,0:T(8,128)(2,1)S(1)}, bf16[16,96,384]{2,1,0:T(8,128)(2,1)S(1)}, u32[]{:S(2)}, u32[]{:S(2)}) collective-permute-start(bf16[16,96,384]{2,1,0:T(8,128)(2,1)S(1)} %pad_maximum_fusion.3.refs_4_), channel_id=1, source_target_pairs={{0,65},{1,64},{32,96},{33,97},{64,1},{65,0},{96,32},{97,33},{2,67}... | collective-permute-start | bytes 3538952 | tf_op jit(solution)/shard_map/ppermute | solution.py:31
  72.9 28.8 %collective-permute-start.26 = (bf16[16,96,384]{2,1,0:T(8,128)(2,1)S(1)}, bf16[16,96,384]{2,1,0:T(8,128)(2,1)S(1)}, u32[]{:S(2)}, u32[]{:S(2)}) collective-permute-start(bf16[16,96,384]{2,1,0:T(8,128)(2,1)S(1)} %pad_maximum_fusion.1.refs_4_), channel_id=1, source_target_pairs={{0,8},{8,0},{16,24},{24,16},{32,56},{40,48},{48,40},{56,32},{1,9},... | collective-permute-start | bytes 3538952 | tf_op jit(solution)/shard_map/ppermute | solution.py:31
  83.4 20.8 %collective-permute-start.34 = (bf16[16,96,384]{2,1,0:T(8,128)(2,1)S(1)}, bf16[16,96,384]{2,1,0:T(8,128)(2,1)S(1)}, u32[]{:S(2)}, u32[]{:S(2)}) collective-permute-start(bf16[16,96,384]{2,1,0:T(8,128)(2,1)S(1)} %collective-permute-done.32.refs_5_), channel_id=1, source_target_pairs={{0,65},{1,64},{32,96},{33,97},{64,1},{65,0},{96,32},{97,33},{2,67}... | collective-permute-start | bytes 3538952 | tf_op jit(solution)/shard_map/ppermute | solution.py:31
  90.0 27.4 %collective-permute-start.30 = (bf16[16,96,384]{2,1,0:T(8,128)(2,1)S(1)}, bf16[16,96,384]{2,1,0:T(8,128)(2,1)S(1)}, u32[]{:S(2)}, u32[]{:S(2)}) collective-permute-start(bf16[16,96,384]{2,1,0:T(8,128)(2,1)S(1)} %pad_maximum_fusion.2.refs_4_), channel_id=1, source_target_pairs={{0,6},{2,4},{4,2},{6,0},{32,34},{34,32},{36,38},{38,36},{1,7},{3,5... | collective-permute-start | bytes 3538952 | tf_op jit(solution)/shard_map/ppermute | solution.py:31
  90.9 33.5 %collective-permute-start.31 = (bf16[16,96,384]{2,1,0:T(8,128)(2,1)S(1)}, bf16[16,96,384]{2,1,0:T(8,128)(2,1)S(1)}, u32[]{:S(2)}, u32[]{:S(2)}) collective-permute-start(bf16[16,96,384]{2,1,0:T(8,128)(2,1)S(1)} %collective-permute-done.29.refs_5_), channel_id=1, source_target_pairs={{0,6},{2,4},{4,2},{6,0},{32,34},{34,32},{36,38},{38,36},{1,7},{3,5... | collective-permute-start | bytes 3538952 | tf_op jit(solution)/shard_map/ppermute | solution.py:31
  93.9 47.6 %collective-permute-start.27 = (bf16[16,96,384]{2,1,0:T(8,128)(2,1)S(1)}, bf16[16,96,384]{2,1,0:T(8,128)(2,1)S(1)}, u32[]{:S(2)}, u32[]{:S(2)}) collective-permute-start(bf16[16,96,384]{2,1,0:T(8,128)(2,1)S(1)} %pad_maximum_fusion.1.refs_4_), channel_id=1, source_target_pairs={{0,24},{8,16},{16,8},{24,0},{32,40},{40,32},{48,56},{56,48},{1,25}... | collective-permute-start | bytes 3538952 | tf_op jit(solution)/shard_map/ppermute | solution.py:31
  101.7 42.6 %collective-permute-start.28 = (bf16[16,96,384]{2,1,0:T(8,128)(2,1)S(1)}, bf16[16,96,384]{2,1,0:T(8,128)(2,1)S(1)}, u32[]{:S(2)}, u32[]{:S(2)}) collective-permute-start(bf16[16,96,384]{2,1,0:T(8,128)(2,1)S(1)} %collective-permute-done.26.refs_5_), channel_id=1, source_target_pairs={{0,24},{8,16},{16,8},{24,0},{32,40},{40,32},{48,56},{56,48},{1,25}... | collective-permute-start | bytes 3538952 | tf_op jit(solution)/shard_map/ppermute | solution.py:31
  104.2 12.0 %collective-permute-start.23 = (bf16[16,96,128]{2,1,0:T(8,128)(2,1)S(1)}, bf16[16,96,128]{2,1,0:T(8,128)(2,1)S(1)}, u32[]{:S(2)}, u32[]{:S(2)}) collective-permute-start(bf16[16,96,128]{2,1,0:T(8,128)(2,1)S(1)} %pad_maximum_fusion.12.refs_12_), channel_id=1, source_target_pairs={{0,8},{8,0},{16,24},{24,16},{32,56},{40,48},{48,40},{56,32},{1,9},... | collective-permute-start | bytes 1179656 | tf_op jit(solution)/shard_map/ppermute | solution.py:31
  116.2 20.1 %collective-permute-start.24 = (bf16[16,96,128]{2,1,0:T(8,128)(2,1)S(1)}, bf16[16,96,128]{2,1,0:T(8,128)(2,1)S(1)}, u32[]{:S(2)}, u32[]{:S(2)}) collective-permute-start(bf16[16,96,128]{2,1,0:T(8,128)(2,1)S(1)} %pad_maximum_fusion.12.refs_12_), channel_id=1, source_target_pairs={{0,24},{8,16},{16,8},{24,0},{32,40},{40,32},{48,56},{56,48},{1,25}... | collective-permute-start | bytes 1179656 | tf_op jit(solution)/shard_map/ppermute | solution.py:31
  117.4 19.3 %collective-permute-start.16 = (bf16[16,96,128]{2,1,0:T(8,128)(2,1)S(1)}, bf16[16,96,128]{2,1,0:T(8,128)(2,1)S(1)}, u32[]{:S(2)}, u32[]{:S(2)}) collective-permute-start(bf16[16,96,128]{2,1,0:T(8,128)(2,1)S(1)} %pad_maximum_fusion.10.refs_8_), channel_id=1, source_target_pairs={{0,2},{2,0},{4,6},{6,4},{32,38},{34,36},{36,34},{38,32},{1,3},{3,1... | collective-permute-start | bytes 1179656 | tf_op jit(solution)/shard_map/ppermute | solution.py:31
  124.4 16.8 %collective-permute-start.9 = (bf16[16,96,128]{2,1,0:T(8,128)(2,1)S(1)}, bf16[16,96,128]{2,1,0:T(8,128)(2,1)S(1)}, u32[]{:S(2)}, u32[]{:S(2)}) collective-permute-start(bf16[16,96,128]{2,1,0:T(8,128)(2,1)S(1)} %pad_maximum_fusion.8.refs_4_), channel_id=1, source_target_pairs={{0,64},{1,65},{32,97},{33,96},{64,0},{65,1},{96,33},{97,32},{2,66}... | collective-permute-start | bytes 1179656 | tf_op jit(solution)/shard_map/ppermute | solution.py:31
  136.3 16.1 %collective-permute-start.17 = (bf16[16,96,128]{2,1,0:T(8,128)(2,1)S(1)}, bf16[16,96,128]{2,1,0:T(8,128)(2,1)S(1)}, u32[]{:S(2)}, u32[]{:S(2)}) collective-permute-start(bf16[16,96,128]{2,1,0:T(8,128)(2,1)S(1)} %pad_maximum_fusion.10.refs_8_), channel_id=1, source_target_pairs={{0,6},{2,4},{4,2},{6,0},{32,34},{34,32},{36,38},{38,36},{1,7},{3,5... | collective-permute-start | bytes 1179656 | tf_op jit(solution)/shard_map/ppermute | solution.py:31
  136.8 15.7 %collective-permute-start.10 = (bf16[16,96,128]{2,1,0:T(8,128)(2,1)S(1)}, bf16[16,96,128]{2,1,0:T(8,128)(2,1)S(1)}, u32[]{:S(2)}, u32[]{:S(2)}) collective-permute-start(bf16[16,96,128]{2,1,0:T(8,128)(2,1)S(1)} %pad_maximum_fusion.8.refs_4_), channel_id=1, source_target_pairs={{0,65},{1,64},{32,96},{33,97},{64,1},{65,0},{96,32},{97,33},{2,67}... | collective-permute-start | bytes 1179656 | tf_op jit(solution)/shard_map/ppermute | solution.py:31
  141.2 11.7 %collective-permute-start.25 = (bf16[16,96,128]{2,1,0:T(8,128)(2,1)S(1)}, bf16[16,96,128]{2,1,0:T(8,128)(2,1)S(1)}, u32[]{:S(2)}, u32[]{:S(2)}) collective-permute-start(bf16[16,96,128]{2,1,0:T(8,128)(2,1)S(1)} %collective-permute-done.23.refs_13_), channel_id=1, source_target_pairs={{0,24},{8,16},{16,8},{24,0},{32,40},{40,32},{48,56},{56,48},{1,25}... | collective-permute-start | bytes 1179656 | tf_op jit(solution)/shard_map/ppermute | solution.py:31
  141.5 11.6 %collective-permute-start.18 = (bf16[16,96,128]{2,1,0:T(8,128)(2,1)S(1)}, bf16[16,96,128]{2,1,0:T(8,128)(2,1)S(1)}, u32[]{:S(2)}, u32[]{:S(2)}) collective-permute-start(bf16[16,96,128]{2,1,0:T(8,128)(2,1)S(1)} %collective-permute-done.16.refs_9_), channel_id=1, source_target_pairs={{0,6},{2,4},{4,2},{6,0},{32,34},{34,32},{36,38},{38,36},{1,7},{3,5... | collective-permute-start | bytes 1179656 | tf_op jit(solution)/shard_map/ppermute | solution.py:31
  144.3 9.0 %collective-permute-start.11 = (bf16[16,96,128]{2,1,0:T(8,128)(2,1)S(1)}, bf16[16,96,128]{2,1,0:T(8,128)(2,1)S(1)}, u32[]{:S(2)}, u32[]{:S(2)}) collective-permute-start(bf16[16,96,128]{2,1,0:T(8,128)(2,1)S(1)} %collective-permute-done.9.refs_5_), channel_id=1, source_target_pairs={{0,65},{1,64},{32,96},{33,97},{64,1},{65,0},{96,32},{97,33},{2,67}... | collective-permute-start | bytes 1179656 | tf_op jit(solution)/shard_map/ppermute | solution.py:31
  152.4 14.2 %collective-permute-start.38 = (bf16[2,512,384]{2,1,0:T(8,128)(2,1)S(1)}, bf16[2,512,384]{2,1,0:T(8,128)(2,1)S(1)}, u32[]{:S(2)}, u32[]{:S(2)}) collective-permute-start(bf16[2,512,384]{2,1,0:T(8,128)(2,1)S(1)} %get-tuple-element.33), channel_id=1, source_target_pairs={{0,32},{32,0},{1,33},{33,1},{2,34},{34,2},{3,35},{35,3},{4,36},{36... | collective-permute-start | bytes 2359304 | tf_op jit(solution)/shard_map/ppermute | solution.py:227
  152.5 14.1 %collective-permute-start.37 = (bf16[2,512,384]{2,1,0:T(8,128)(2,1)S(1)}, bf16[2,512,384]{2,1,0:T(8,128)(2,1)S(1)}, u32[]{:S(2)}, u32[]{:S(2)}) collective-permute-start(bf16[2,512,384]{2,1,0:T(8,128)(2,1)S(1)} %get-tuple-element.32), channel_id=1, source_target_pairs={{0,32},{32,0},{1,33},{33,1},{2,34},{34,2},{3,35},{35,3},{4,36},{36... | collective-permute-start | bytes 2359304 | tf_op jit(solution)/shard_map/ppermute | solution.py:227
  153.0 13.6 %collective-permute-start.36 = (bf16[2,512,384]{2,1,0:T(8,128)(2,1)S(1)}, bf16[2,512,384]{2,1,0:T(8,128)(2,1)S(1)}, u32[]{:S(2)}, u32[]{:S(2)}) collective-permute-start(bf16[2,512,384]{2,1,0:T(8,128)(2,1)S(1)} %get-tuple-element.31), channel_id=1, source_target_pairs={{0,32},{32,0},{1,33},{33,1},{2,34},{34,2},{3,35},{35,3},{4,36},{36... | collective-permute-start | bytes 2359304 | tf_op jit(solution)/shard_map/ppermute | solution.py:227
  (13 other events, 64.1 us)

commit v2 on v0

v2 whole, which is shorter than its diff:
```python
import jax
import jax.numpy as jnp
import numpy as np
from jax import lax
from jax.experimental import pallas as pl
from jax.experimental.pallas import tpu as pltpu
from jax.sharding import Mesh
from jax.sharding import PartitionSpec as P

HEAD = 128
EMA = 0.99
COLORS = 3
PARTS = 2
VMEM_LIMIT = 16 * 2**20
FIRST, SECOND = (1, 3), (3, 1)
ORDER = (180, 156)
DIMS = (("x", "y", "z"), ("y", "z", "x"), ("z", "x", "y"))


def exchange(x, dim, masks):
    if dim == "z":
        axes = ("zlo", "core", "zhi")
        pairs = []
        for zlo in range(2):
            for core in range(2):
                for zhi in range(2):
                    z = (2 * zhi + zlo) ^ masks[core]
                    pairs.append(((zlo * 2 + core) * 2 + zhi, ((z % 2) * 2 + core) * 2 + z // 2))
    else:
        axes = ("core", dim)
        pairs = [(core * 4 + i, core * 4 + (i ^ masks[core])) for core in range(2) for i in range(4)]
    return lax.ppermute(x, axes, pairs)


def project_body(color, n_held, *refs):
    _, own, other, gains = refs[:4]
    units = refs[4:8]
    q_out, k_out, send_out, held = refs[8 + n_held :]
    half, width = own.shape
    rows, n = units[0].shape[1:]
    order = ORDER[0] + (ORDER[1] - ORDER[0]) * lax.axis_index("core")
    place = {
        "x": lax.axis_index("x"),
        "y": lax.axis_index("y"),
        "z": 2 * lax.axis_index("zhi") + lax.axis_index("zlo"),
    }
    seen = {d: [lax.bitwise_xor(v, lax.bitwise_and(lax.shift_right_logical(order, 2 * i), 3)) for i in range(4)] for d, v in place.items()}
    starts = {
        "x": [(0, v * (2 * rows)) for v in seen["x"]],
        "y": [(0, v * (8 * rows)) for v in seen["y"]],
        "z": [(lax.bitwise_and(v, 1) * n, lax.shift_right_logical(v, 1) * rows) for v in seen["z"]],
    }
    for u in range(4):
        for pos in range(16):
            at = [starts[d][i] for d, i in zip(DIMS[color], (pos % 4, pos // 4, u))]
            col = pl.multiple_of(at[0][0] + at[1][0] + at[2][0], n)
            row = pl.multiple_of(at[0][1] + at[1][1] + at[2][1], rows)
            held[pl.ds(row, rows), pl.ds(col, n)] = units[u][pos]
    scale = width ** (-0.5)
    tile = 256
    for t, src in enumerate((own, other)):
        for m in range(0, half, tile):
            y = jnp.dot(src[m : m + tile, :], held[...], preferred_element_type=jnp.float32) * scale
            for i, out in enumerate((q_out, k_out)):
                for h in range(0, n, HEAD):
                    v = y[:, i * n + h : i * n + h + HEAD]
                    v = v * lax.rsqrt(jnp.mean(v * v, axis=-1, keepdims=True) + 1e-06) * gains[i : i + 1, :]
                    v = v.astype(jnp.bfloat16)
                    if t == 0:
                        out[m : m + tile, h : h + HEAD] = v
                    else:
                        send_out[i, m : m + tile, h : h + HEAD] = v


def project(part, color, where, own, other, gains, units, outputs):
    half, width = own.shape
    n = units[0].shape[2]
    col = lambda i, where: (0, (where[0] * PARTS + part) * COLORS + color)
    any_spec = pl.BlockSpec(memory_space=pl.ANY)
    operands = [own, other, gains, *units, *outputs]
    specs = [pl.BlockSpec(memory_space=pltpu.VMEM)] * (3 + len(units)) + [any_spec] * len(outputs)
    first = 4 + len(units)
    big = jax.ShapeDtypeStruct((half, width), jnp.bfloat16)
    return pl.pallas_call(
        lambda *refs: project_body(color, len(outputs), *refs),
        grid_spec=pltpu.PrefetchScalarGridSpec(
            num_scalar_prefetch=1,
            grid=(1,),
            in_specs=specs,
            out_specs=[
                pl.BlockSpec((half, n), col),
                pl.BlockSpec((half, n), col),
                pl.BlockSpec((2, half, n), lambda *_: (0, 0, 0)),
            ],
            scratch_shapes=[pltpu.VMEM((width, 2 * n), jnp.bfloat16)],
        ),
        out_shape=[big, big, jax.ShapeDtypeStruct((2, half, n), jnp.bfloat16)],
        input_output_aliases={first: 0, first + 1: 1} if outputs else {},
        compiler_params=pltpu.CompilerParams(vmem_limit_bytes=VMEM_LIMIT),
        cost_estimate=pl.CostEstimate(
            flops=2 * 2 * half * width * 2 * n,
            bytes_accessed=2 * width * (2 * half + 2 * n),
            transcendentals=0,
        ),
    )(where, *operands)


def put_body(where, *refs):
    q_out, k_out = refs[COLORS + 2 :]
    n = refs[0].shape[2]
    for k in range(COLORS):
        q_out[:, k * n : (k + 1) * n] = refs[k][0]
        k_out[:, k * n : (k + 1) * n] = refs[k][1]


def put(part, where, got, query, key_out):
    _, half, n = got[0].shape
    rows = half // 4
    col = lambda i, where: (i, (1 - where[0]) * PARTS + part)
    any_spec = pl.BlockSpec(memory_space=pl.ANY)
    return pl.pallas_call(
        put_body,
        grid_spec=pltpu.PrefetchScalarGridSpec(
            num_scalar_prefetch=1,
            grid=(half // rows,),
            in_specs=[pl.BlockSpec((2, rows, n), lambda i, *_: (0, i, 0))] * COLORS + [any_spec, any_spec],
            out_specs=[pl.BlockSpec((rows, COLORS * n), col)] * 2,
        ),
        out_shape=[jax.ShapeDtypeStruct(query.shape, query.dtype)] * 2,
        input_output_aliases={COLORS + 1: 0, COLORS + 2: 1},
        compiler_params=pltpu.CompilerParams(vmem_limit_bytes=8 * 2**20),
        cost_estimate=pl.CostEstimate(flops=10**9, bytes_accessed=8 * COLORS * got[0].size, transcendentals=0),
    )(where, *got, query, key_out)


def join_body(n, a, b, *outs):
    for p, out in enumerate(outs):
        out[0] = a[:, :, p * n : (p + 1) * n]
        out[1] = b[:, :, p * n : (p + 1) * n]


def join(a, b):
    places, rows, width = a.shape
    n = width // PARTS
    step = 2
    made = pl.pallas_call(
        lambda *refs: join_body(n, *refs),
        grid=(places // step,),
        in_specs=[pl.BlockSpec((step, rows, width), lambda i: (i, 0, 0))] * 2,
        out_specs=[pl.BlockSpec((2, step, rows, n), lambda i: (0, i, 0, 0))] * PARTS,
        out_shape=[jax.ShapeDtypeStruct((2, places, rows, n), a.dtype)] * PARTS,
        compiler_params=pltpu.CompilerParams(vmem_limit_bytes=8 * 2**20),
        cost_estimate=pl.CostEstimate(flops=10**9, bytes_accessed=8 * a.size, transcendentals=0),
        name="join",
    )(a, b)
    return [m.reshape(2 * places, rows, n) for m in made]


def pick_body(core, local, out):
    out[0] = local[...]


def pick(core, local, block):
    rows = local.shape[0]
    return pl.pallas_call(
        pick_body,
        grid_spec=pltpu.PrefetchScalarGridSpec(
            num_scalar_prefetch=1,
            grid=(2,),
            in_specs=[pl.BlockSpec((rows, block), lambda j, core: (0, 2 * j + 1 - core[0]))],
            out_specs=pl.BlockSpec((1, rows, block), lambda j, core: (j, 0, 0)),
        ),
        out_shape=jax.ShapeDtypeStruct((2, rows, block), jnp.float32),
        compiler_params=pltpu.CompilerParams(vmem_limit_bytes=8 * 2**20),
        cost_estimate=pl.CostEstimate(flops=10**9, bytes_accessed=16 * rows * block, transcendentals=0),
        name="pick",
    )(core, local)


def merge_body(n, where, local, got, keep, *give):
    total = local[...] + got[0]
    mine = pl.program_id(0) == where[1]

    @pl.when(mine)
    def _():
        keep[...] = total

    @pl.when(jnp.logical_not(mine))
    def _():
        for k in range(COLORS):
            for p in range(PARTS):
                at = (p * COLORS + k) * n // PARTS
                give[k][:, p * n // PARTS : (p + 1) * n // PARTS] = total[:, at : at + n // PARTS]


def merge(where, local, got):
    _, rows, block = got.shape
    n = block // COLORS
    return pl.pallas_call(
        lambda *refs: merge_body(n, *refs),
        grid_spec=pltpu.PrefetchScalarGridSpec(
            num_scalar_prefetch=1,
            grid=(2,),
            in_specs=[
                pl.BlockSpec((rows, block), lambda j, where: (0, 2 * j + where[0])),
                pl.BlockSpec((1, rows, block), lambda j, where: (j, 0, 0)),
            ],
            out_specs=[pl.BlockSpec((rows, block), lambda *_: (0, 0))] + [pl.BlockSpec((rows, n), lambda *_: (0, 0))] * COLORS,
        ),
        out_shape=[jax.ShapeDtypeStruct((rows, block), jnp.float32)] + [jax.ShapeDtypeStruct((rows, n), jnp.float32)] * COLORS,
        compiler_params=pltpu.CompilerParams(vmem_limit_bytes=16 * 2**20),
        cost_estimate=pl.CostEstimate(flops=10**9, bytes_accessed=24 * rows * block, transcendentals=0),
        name="merge",
    )(where, local, got)


def shards(tokens, student, teacher, norm_gain, query_gain, key_gain):
    block = teacher.shape[1]
    n = block // COLORS
    core = lax.axis_index("core")
    where = jnp.stack([core, lax.axis_index("zlo")]).astype(jnp.int32)
    swap = [(0, 1), (1, 0)]

    local = student[0]
    got = lax.ppermute(pick(where, local, block), "core", swap)
    keep, *give = merge(where, local, got)
    arrived, owned, copied = [], [], []
    for k in range(COLORS):
        arrived.append(lax.ppermute(give[k], "zlo", swap))
    for k in range(COLORS):
        spans = [(p * COLORS + k) * n // PARTS for p in range(PARTS)]
        cut = jnp.concatenate([keep[:, at : at + n // PARTS] for at in spans], axis=1)
        if k:
            cut, _ = lax.optimization_barrier((cut, copied[-1]))
        owned.append((cut + arrived[k]) / 4)
        copied.append(owned[k].astype(jnp.bfloat16)[None])
    student_new = jnp.concatenate(
        [o[:, p * n // PARTS : (p + 1) * n // PARTS] for p in range(PARTS) for o in owned], axis=1
    )
    teacher_new = EMA * teacher + (1.0 - EMA) * student_new

    wide = tokens.astype(jnp.float32)
    normed = (
        wide * lax.rsqrt(jnp.mean(wide * wide, axis=-1, keepdims=True) + 1e-06) * norm_gain
    ).astype(jnp.bfloat16)
    other = lax.ppermute(normed, "core", swap)

    parts = [None] * COLORS
    for s in range(4):
        for k in range(COLORS):
            got = exchange(copied[k], DIMS[k][s // 2], (FIRST, SECOND)[s % 2])
            if s < 3:
                copied[k] = jnp.concatenate([copied[k], got], axis=0)
            else:
                parts[k] = join(copied[k], got)
    gains = jnp.stack([query_gain, key_gain])
    where, student_new, teacher_new = lax.optimization_barrier((where, student_new, teacher_new))
    outputs, back = (), []
    for p in range(PARTS):
        back.append([])
        for k in range(COLORS):
            one = exchange(parts[k][p], DIMS[k][2], FIRST)
            two = exchange(parts[k][p], DIMS[k][2], SECOND)
            three = exchange(one, DIMS[k][2], SECOND)
            units = [parts[k][p], one, two, three]
            *outputs, send = project(p, k, where, normed, other, gains, units, outputs)
            back[p].append(lax.ppermute(send, "core", swap))
    for p in range(PARTS):
        outputs = put(p, where, back[p], *outputs)
    return (teacher_new, student_new, *outputs)


def solution(mesh):
    split = Mesh(np.asarray(mesh.devices).reshape(2, 2, 4, 4, 2), ("zlo", "core", "y", "x", "zhi"))
    group, fsdp = ("zlo", "core"), ("y", "x", "zhi")
    rows = P(group + fsdp, None)

    return jax.shard_map(
        shards,
        mesh=split,
        in_specs=(rows, P(group, fsdp, None), P(fsdp, group), P(), P(), P()),
        out_specs=(P(fsdp, group), P(fsdp, group), rows, rows),
        check_vma=False,
    )
```

time: 430 us -> 154 us (0.36)
  waiting for transfers between devices: 324 us -> 32.9 us
  starting transfers between devices: 0.08 us -> 77.6 us
  Pallas kernels: 0 us -> 34.3 us
  other arithmetic: 30.4 us -> 3.41 us
  matrix products: 26.8 us -> 0 us
  blocking collectives: 18.3 us -> 0 us
  between operations: 14.2 us -> 1.06 us
  local copies, waits for them, and re-layouts: 16.1 us -> 3.18 us
    all_gather x1 -> x0, waiting for transfers between devices: 288 us -> none  [shards(): lax.all_gather(whole_rows, 'fsdp', axis=0, tiled=True)]
    ppermute x0 -> x41, starting transfers between devices: none -> 77.6 us  [the longest x30 71.8 us: exchange(): return lax.ppermute(x, axes, pairs)]
    reduce_scatter x1 -> x0, waiting for transfers between devices: 35.3 us -> none  [shards(): lax.psum_scatter(local_part, 'group', scatter_dimension=1, tiled=True)]
    pallas_call x0 -> x13, Pallas kernels: none -> 34.3 us  [the longest x6 27.1 us: project(): pl.pallas_call(lambda *refs: project_body(color, len(outputs), *refs), gr...]
    ppermute x0 -> x41, waiting for transfers between devices: none -> 32.9 us  [the longest x30 26.2 us: exchange(): return lax.ppermute(x, axes, pairs)]
    dot_general x1 -> x0, matrix products: 26.8 us -> none  [shards(): jnp.dot(normed, lax.all_gather(whole_rows, 'fsdp', axis=0, tiled=True), p...]
    all_to_all x1 -> x0, blocking collectives: 18.3 us -> none  [sent_to_all(): return lax.all_to_all(copies, axis, split_axis=0, concat_axis=0, tiled=True)]
    convert_element_type x2 -> x1, other arithmetic: 11.6 us -> 1.17 us  [shards(): normed = (wide * lax.rsqrt(jnp.mean(wide * wide, axis=-1, keepdims=True)...]
  transfers between devices with their start and end apart: 2 -> 41, of which waited for: 2 -> 15; matrix products, arithmetic and copies ran while one was open for 0% -> 2% of each run, Pallas kernels for 0% -> 20%
where the time goes in v2:
time: 154 us; the launch traced here: 152 us
  starting transfers between devices  77.6 us (50%)
  Pallas kernels  34.3 us (22%)
  waiting for transfers between devices  32.9 us (21%)
  other arithmetic  3.41 us (2%)
  local copies, waits for them, and re-layouts  3.18 us (2%)
    ppermute x30, starting transfers between devices, exchange(): return lax.ppermute(x, axes, pairs)  71.8 us
    pallas_call x6, Pallas kernels, project(): pl.pallas_call(lambda *refs: project_body(color, len(outputs), *refs), gr...  27.1 us
    ppermute x30, waiting for transfers between devices, exchange(): return lax.ppermute(x, axes, pairs)  26.2 us
    ppermute x3, waiting for transfers between devices, shards(): arrived.append(lax.ppermute(give[k], 'zlo', swap))  6.19 us
    pallas_call x2, Pallas kernels, put(): pl.pallas_call(put_body, grid_spec=pltpu.PrefetchScalarGridSpec(num_scala...  4.69 us
    ppermute x3, starting transfers between devices, shards(): arrived.append(lax.ppermute(give[k], 'zlo', swap))  4.13 us
    unnamed x21, local copies, waits for them, and re-layouts  3.12 us
  transfers between devices with their start and end apart: 41, of which 15 were waited for; matrix products, arithmetic and copies ran while one was open for 2% of the time, Pallas kernels for 20%

profile of v2, /device:TPU:0, one launch (start us, length us, event | category | flops | bytes accessed | tf_op | source)
XLA Modules:
  0.0 152.5 jit_solution(8776944102887455999)
XLA Ops:
  7.6 2.1 %collective-permute-start.1 = (f32[96,512]{1,0:T(8,128)S(1)}, f32[96,512]{1,0:T(8,128)S(1)}, u32[]{:S(2)}, u32[]{:S(2)}) collective-permute-start(f32[96,512]{1,0:T(8,128)S(1)} %get-tuple-element.42), channel_id=1, source_target_pairs={{0,64},{64,0},{1,65},{65,1},{2,66},{66,2},{3,67},{67,3},{4,68},{68... | collective-permute-start | bytes 589832 | tf_op jit(solution)/shard_map/ppermute | solution.py:229
  11.8 3.7 %collective-permute-done.1 = f32[96,512]{1,0:T(8,128)S(1)} collective-permute-done((f32[96,512]{1,0:T(8,128)S(1)}, f32[96,512]{1,0:T(8,128)S(1)}, u32[]{:S(2)}, u32[]{:S(2)}) %collective-permute-start.1) | collective-permute-done | bytes 196640 | tf_op jit(solution)/shard_map/ppermute | solution.py:229
  17.2 2.5 %collective-permute-done.2 = f32[96,512]{1,0:T(8,128)S(1)} collective-permute-done((f32[96,512]{1,0:T(8,128)S(1)}, f32[96,512]{1,0:T(8,128)S(1)}, u32[]{:S(2)}, u32[]{:S(2)}) %collective-permute-start.2) | collective-permute-done | bytes 196640 | tf_op jit(solution)/shard_map/ppermute | solution.py:229
  21.5 2.8 %collective-permute-start.6 = (bf16[2,96,512]{2,1,0:T(8,128)(2,1)S(1)}, bf16[2,96,512]{2,1,0:T(8,128)(2,1)S(1)}, u32[]{:S(2)}, u32[]{:S(2)}) collective-permute-start(bf16[2,96,512]{2,1,0:T(8,128)(2,1)S(1)} %pad_maximum_fusion.8), channel_id=1, source_target_pairs={{0,6},{2,4},{4,2},{6,0},{32,34},{34,32},{36,38},{38,36},{1,7},{3,5... | collective-permute-start | bytes 589832 | tf_op jit(solution)/shard_map/ppermute | solution.py:32
  26.4 2.3 %collective-permute-start.20 = (bf16[2,96,512]{2,1,0:T(8,128)(2,1)S(1)}, bf16[2,96,512]{2,1,0:T(8,128)(2,1)S(1)}, u32[]{:S(2)}, u32[]{:S(2)}) collective-permute-start(bf16[2,96,512]{2,1,0:T(8,128)(2,1)S(1)} %pad_maximum_fusion.10), channel_id=1, source_target_pairs={{0,24},{8,16},{16,8},{24,0},{32,40},{40,32},{48,56},{56,48},{1,25}... | collective-permute-start | bytes 589832 | tf_op jit(solution)/shard_map/ppermute | solution.py:32
  29.5 3.7 %collective-permute-start.13 = (bf16[2,96,512]{2,1,0:T(8,128)(2,1)S(1)}, bf16[2,96,512]{2,1,0:T(8,128)(2,1)S(1)}, u32[]{:S(2)}, u32[]{:S(2)}) collective-permute-start(bf16[2,96,512]{2,1,0:T(8,128)(2,1)S(1)} %pad_maximum_fusion.9), channel_id=1, source_target_pairs={{0,65},{1,64},{32,96},{33,97},{64,1},{65,0},{96,32},{97,33},{2,67}... | collective-permute-start | bytes 589832 | tf_op jit(solution)/shard_map/ppermute | solution.py:32
  35.5 3.3 %collective-permute-done.13 = bf16[2,96,512]{2,1,0:T(8,128)(2,1)S(1)} collective-permute-done((bf16[2,96,512]{2,1,0:T(8,128)(2,1)S(1)}, bf16[2,96,512]{2,1,0:T(8,128)(2,1)S(1)}, u32[]{:S(2)}, u32[]{:S(2)}) %collective-permute-start.13) | collective-permute-done | bytes 196640 | tf_op jit(solution)/shard_map/ppermute | solution.py:32
  39.1 3.0 %collective-permute-start.8 = (bf16[8,96,512]{2,1,0:T(8,128)(2,1)S(1)}, bf16[8,96,512]{2,1,0:T(8,128)(2,1)S(1)}, u32[]{:S(2)}, u32[]{:S(2)}) collective-permute-start(bf16[8,96,512]{2,1,0:T(8,128)(2,1)S(1)} %pad_maximum_fusion.refs_0_), channel_id=1, source_target_pairs={{0,24},{8,16},{16,8},{24,0},{32,40},{40,32},{48,56},{56,48},{1,25}... | collective-permute-start | bytes 2359304 | tf_op jit(solution)/shard_map/ppermute | solution.py:32
  43.1 4.2 %collective-permute-start.22 = (bf16[8,96,512]{2,1,0:T(8,128)(2,1)S(1)}, bf16[8,96,512]{2,1,0:T(8,128)(2,1)S(1)}, u32[]{:S(2)}, u32[]{:S(2)}) collective-permute-start(bf16[8,96,512]{2,1,0:T(8,128)(2,1)S(1)} %pad_maximum_fusion.2.refs_0_), channel_id=1, source_target_pairs={{0,65},{1,64},{32,96},{33,97},{64,1},{65,0},{96,32},{97,33},{2,67}... | collective-permute-start | bytes 2359304 | tf_op jit(solution)/shard_map/ppermute | solution.py:32
  48.3 2.1 %collective-permute-start.15 = (bf16[8,96,512]{2,1,0:T(8,128)(2,1)S(1)}, bf16[8,96,512]{2,1,0:T(8,128)(2,1)S(1)}, u32[]{:S(2)}, u32[]{:S(2)}) collective-permute-start(bf16[8,96,512]{2,1,0:T(8,128)(2,1)S(1)} %pad_maximum_fusion.1.refs_0_), channel_id=1, source_target_pairs={{0,6},{2,4},{4,2},{6,0},{32,34},{34,32},{36,38},{38,36},{1,7},{3,5... | collective-permute-start | bytes 2359304 | tf_op jit(solution)/shard_map/ppermute | solution.py:32
  52.8 3.6 %collective-permute-start.27 = (bf16[16,96,256]{2,1,0:T(8,128)(2,1)S(1)}, bf16[16,96,256]{2,1,0:T(8,128)(2,1)S(1)}, u32[]{:S(2)}, u32[]{:S(2)}) collective-permute-start(bf16[16,96,256]{2,1,0:T(8,128)(2,1)S(1)} %bitcast.35), channel_id=1, source_target_pairs={{0,65},{1,64},{32,96},{33,97},{64,1},{65,0},{96,32},{97,33},{2,67}... | collective-permute-start | bytes 2359304 | tf_op jit(solution)/shard_map/ppermute | solution.py:32
  56.4 5.4 %collective-permute-done.22.refs_1_ = bf16[8,96,512]{2,1,0:T(8,128)(2,1)S(1)} collective-permute-done((bf16[8,96,512]{2,1,0:T(8,128)(2,1)S(1)}, bf16[8,96,512]{2,1,0:T(8,128)(2,1)S(1)}, u32[]{:S(2)}, u32[]{:S(2)}) %collective-permute-start.22) | collective-permute-done | bytes 786464 | tf_op jit(solution)/shard_map/ppermute | solution.py:32
  62.3 4.5 %collective-permute-done.15.refs_1_ = bf16[8,96,512]{2,1,0:T(8,128)(2,1)S(1)} collective-permute-done((bf16[8,96,512]{2,1,0:T(8,128)(2,1)S(1)}, bf16[8,96,512]{2,1,0:T(8,128)(2,1)S(1)}, u32[]{:S(2)}, u32[]{:S(2)}) %collective-permute-start.15) | collective-permute-done | bytes 786464 | tf_op jit(solution)/shard_map/ppermute | solution.py:32
  68.5 3.2 %collective-permute-start.16 = (bf16[16,96,256]{2,1,0:T(8,128)(2,1)S(1)}, bf16[16,96,256]{2,1,0:T(8,128)(2,1)S(1)}, u32[]{:S(2)}, u32[]{:S(2)}) collective-permute-start(bf16[16,96,256]{2,1,0:T(8,128)(2,1)S(1)} %bitcast.26), channel_id=1, source_target_pairs={{0,8},{8,0},{16,24},{24,16},{32,56},{40,48},{48,40},{56,32},{1,9},... | collective-permute-start | bytes 2359304 | tf_op jit(solution)/shard_map/ppermute | solution.py:32
  71.7 3.5 %collective-permute-start.17 = (bf16[16,96,256]{2,1,0:T(8,128)(2,1)S(1)}, bf16[16,96,256]{2,1,0:T(8,128)(2,1)S(1)}, u32[]{:S(2)}, u32[]{:S(2)}) collective-permute-start(bf16[16,96,256]{2,1,0:T(8,128)(2,1)S(1)} %bitcast.27), channel_id=1, source_target_pairs={{0,24},{8,16},{16,8},{24,0},{32,40},{40,32},{48,56},{56,48},{1,25}... | collective-permute-start | bytes 2359304 | tf_op jit(solution)/shard_map/ppermute | solution.py:32
  75.2 4.8 %collective-permute-start.9 = (bf16[16,96,256]{2,1,0:T(8,128)(2,1)S(1)}, bf16[16,96,256]{2,1,0:T(8,128)(2,1)S(1)}, u32[]{:S(2)}, u32[]{:S(2)}) collective-permute-start(bf16[16,96,256]{2,1,0:T(8,128)(2,1)S(1)} %bitcast.23), channel_id=1, source_target_pairs={{0,64},{1,65},{32,97},{33,96},{64,0},{65,1},{96,33},{97,32},{2,66}... | collective-permute-start | bytes 2359304 | tf_op jit(solution)/shard_map/ppermute | solution.py:32
  80.0 2.9 %collective-permute-start.10 = (bf16[16,96,256]{2,1,0:T(8,128)(2,1)S(1)}, bf16[16,96,256]{2,1,0:T(8,128)(2,1)S(1)}, u32[]{:S(2)}, u32[]{:S(2)}) collective-permute-start(bf16[16,96,256]{2,1,0:T(8,128)(2,1)S(1)} %bitcast.24), channel_id=1, source_target_pairs={{0,65},{1,64},{32,96},{33,97},{64,1},{65,0},{96,32},{97,33},{2,67}... | collective-permute-start | bytes 2359304 | tf_op jit(solution)/shard_map/ppermute | solution.py:32
  82.9 11.4 %collective-permute-start.28 = (bf16[16,96,256]{2,1,0:T(8,128)(2,1)S(1)}, bf16[16,96,256]{2,1,0:T(8,128)(2,1)S(1)}, u32[]{:S(2)}, u32[]{:S(2)}) collective-permute-start(bf16[16,96,256]{2,1,0:T(8,128)(2,1)S(1)} %collective-permute-done.26.refs_5_), channel_id=1, source_target_pairs={{0,65},{1,64},{32,96},{33,97},{64,1},{65,0},{96,32},{97,33},{2,67}... | collective-permute-start | bytes 2359304 | tf_op jit(solution)/shard_map/ppermute | solution.py:32
  94.5 2.3 %collective-permute-start.34 = (bf16[16,96,256]{2,1,0:T(8,128)(2,1)S(1)}, bf16[16,96,256]{2,1,0:T(8,128)(2,1)S(1)}, u32[]{:S(2)}, u32[]{:S(2)}) collective-permute-start(bf16[16,96,256]{2,1,0:T(8,128)(2,1)S(1)} %bitcast.20), channel_id=1, source_target_pairs={{0,8},{8,0},{16,24},{24,16},{32,56},{40,48},{48,40},{56,32},{1,9},... | collective-permute-start | bytes 2359304 | tf_op jit(solution)/shard_map/ppermute | solution.py:32
  99.5 2.2 %collective-permute-start.18 = (bf16[16,96,256]{2,1,0:T(8,128)(2,1)S(1)}, bf16[16,96,256]{2,1,0:T(8,128)(2,1)S(1)}, u32[]{:S(2)}, u32[]{:S(2)}) collective-permute-start(bf16[16,96,256]{2,1,0:T(8,128)(2,1)S(1)} %collective-permute-done.16.refs_5_), channel_id=1, source_target_pairs={{0,24},{8,16},{16,8},{24,0},{32,40},{40,32},{48,56},{56,48},{1,25}... | collective-permute-start | bytes 2359304 | tf_op jit(solution)/shard_map/ppermute | solution.py:32
  104.3 3.2 %collective-permute-start.11 = (bf16[16,96,256]{2,1,0:T(8,128)(2,1)S(1)}, bf16[16,96,256]{2,1,0:T(8,128)(2,1)S(1)}, u32[]{:S(2)}, u32[]{:S(2)}) collective-permute-start(bf16[16,96,256]{2,1,0:T(8,128)(2,1)S(1)} %collective-permute-done.9.refs_5_), channel_id=1, source_target_pairs={{0,65},{1,64},{32,96},{33,97},{64,1},{65,0},{96,32},{97,33},{2,67}... | collective-permute-start | bytes 2359304 | tf_op jit(solution)/shard_map/ppermute | solution.py:32
  107.5 4.5 %shard_map.93 = (bf16[512,3072]{1,0:T(8,128)(2,1)}, bf16[512,3072]{1,0:T(8,128)(2,1)}, bf16[2,512,256]{2,1,0:T(8,128)(2,1)S(1)}) custom-call(s32[2]{0:T(128)S(1)} %pad_add_fusion.core.refs_0_.where, bf16[512,3072]{1,0:T(8,128)(2,1)S(1)} %fusion.2.refs_1_, bf16[512,3072]{1,0:T(8,128)(2,1)S(1)} %collective-permute-done.4.refs_2_, ...), custom_call_target="tpu_custom_call" | custom-call | flops 3221225472 | bytes 9437184 | tf_op jit(solution)/shard_map/pallas_call | solution.py:84
  112.2 3.6 %collective-permute-start.31 = (bf16[16,96,256]{2,1,0:T(8,128)(2,1)S(1)}, bf16[16,96,256]{2,1,0:T(8,128)(2,1)S(1)}, u32[]{:S(2)}, u32[]{:S(2)}) collective-permute-start(bf16[16,96,256]{2,1,0:T(8,128)(2,1)S(1)} %bitcast.18), channel_id=1, source_target_pairs={{0,6},{2,4},{4,2},{6,0},{32,34},{34,32},{36,38},{38,36},{1,7},{3,5... | collective-permute-start | bytes 2359304 | tf_op jit(solution)/shard_map/ppermute | solution.py:32
  115.9 4.5 %shard_map.94 = (bf16[512,3072]{1,0:T(8,128)(2,1)}, bf16[512,3072]{1,0:T(8,128)(2,1)}, bf16[2,512,256]{2,1,0:T(8,128)(2,1)S(1)}) custom-call(s32[2]{0:T(128)S(1)} %pad_add_fusion.core.refs_0_.where, bf16[512,3072]{1,0:T(8,128)(2,1)S(1)} %fusion.2.refs_1_, ...), custom_call_target="tpu_custom_call", output_to_operand_aliasing={{0}: (8, {}), {1}: (9, {})} | custom-call | flops 3221225472 | bytes 9437184 | tf_op jit(solution)/shard_map/pallas_call | solution.py:84
  120.4 3.1 %collective-permute-start.35 = (bf16[16,96,256]{2,1,0:T(8,128)(2,1)S(1)}, bf16[16,96,256]{2,1,0:T(8,128)(2,1)S(1)}, u32[]{:S(2)}, u32[]{:S(2)}) collective-permute-start(bf16[16,96,256]{2,1,0:T(8,128)(2,1)S(1)} %bitcast.21), channel_id=1, source_target_pairs={{0,24},{8,16},{16,8},{24,0},{32,40},{40,32},{48,56},{56,48},{1,25}... | collective-permute-start | bytes 2359304 | tf_op jit(solution)/shard_map/ppermute | solution.py:32
  123.8 4.5 %shard_map.95 = (bf16[512,3072]{1,0:T(8,128)(2,1)}, bf16[512,3072]{1,0:T(8,128)(2,1)}, bf16[2,512,256]{2,1,0:T(8,128)(2,1)S(1)}) custom-call(s32[2]{0:T(128)S(1)} %pad_add_fusion.core.refs_0_.where, bf16[512,3072]{1,0:T(8,128)(2,1)S(1)} %fusion.2.refs_1_, ...), custom_call_target="tpu_custom_call", output_to_operand_aliasing={{0}: (8, {}), {1}: (9, {})} | custom-call | flops 3221225472 | bytes 9437184 | tf_op jit(solution)/shard_map/pallas_call | solution.py:84
  128.6 4.5 %shard_map.96 = (bf16[512,3072]{1,0:T(8,128)(2,1)}, bf16[512,3072]{1,0:T(8,128)(2,1)}, bf16[2,512,256]{2,1,0:T(8,128)(2,1)S(1)}) custom-call(s32[2]{0:T(128)S(1)} %pad_add_fusion.core.refs_0_.where, bf16[512,3072]{1,0:T(8,128)(2,1)S(1)} %fusion.2.refs_1_, ...), custom_call_target="tpu_custom_call", output_to_operand_aliasing={{0}: (8, {}), {1}: (9, {})} | custom-call | flops 3221225472 | bytes 9437184 | tf_op jit(solution)/shard_map/pallas_call | solution.py:84
  134.2 4.5 %shard_map.97 = (bf16[512,3072]{1,0:T(8,128)(2,1)}, bf16[512,3072]{1,0:T(8,128)(2,1)}, bf16[2,512,256]{2,1,0:T(8,128)(2,1)S(1)}) custom-call(s32[2]{0:T(128)S(1)} %pad_add_fusion.core.refs_0_.where, bf16[512,3072]{1,0:T(8,128)(2,1)S(1)} %fusion.2.refs_1_, ...), custom_call_target="tpu_custom_call", output_to_operand_aliasing={{0}: (8, {}), {1}: (9, {})} | custom-call | flops 3221225472 | bytes 9437184 | tf_op jit(solution)/shard_map/pallas_call | solution.py:84
  138.7 3.4 %collective-permute-done.36.refs_7_ = bf16[16,96,256]{2,1,0:T(8,128)(2,1)S(1)} collective-permute-done((bf16[16,96,256]{2,1,0:T(8,128)(2,1)S(1)}, bf16[16,96,256]{2,1,0:T(8,128)(2,1)S(1)}, u32[]{:S(2)}, u32[]{:S(2)}) %collective-permute-start.36) | collective-permute-done | bytes 786464 | tf_op jit(solution)/shard_map/ppermute | solution.py:32
  142.1 4.5 %shard_map.98 = (bf16[512,3072]{1,0:T(8,128)(2,1)}, bf16[512,3072]{1,0:T(8,128)(2,1)}, bf16[2,512,256]{2,1,0:T(8,128)(2,1)S(1)}) custom-call(s32[2]{0:T(128)S(1)} %pad_add_fusion.core.refs_0_.where, bf16[512,3072]{1,0:T(8,128)(2,1)S(1)} %fusion.2.refs_1_, ...), custom_call_target="tpu_custom_call", output_to_operand_aliasing={{0}: (8, {}), {1}: (9, {})} | custom-call | flops 3221225472 | bytes 9437184 | tf_op jit(solution)/shard_map/pallas_call | solution.py:84
  147.3 2.3 %shard_map.99 = (bf16[512,3072]{1,0:T(8,128)(2,1)}, bf16[512,3072]{1,0:T(8,128)(2,1)}) custom-call(s32[2]{0:T(128)S(1)} %pad_add_fusion.core.refs_0_.where, bf16[2,512,256]{2,1,0:T(8,128)(2,1)S(1)} %collective-permute-done.38.refs_0_, bf16[2,512,256]{2,1,0:T(8,128)(2,1)S(1)} %collective-permute-done.39.refs_1_, ...), custom_call_target="tpu_custom_call", output_to_operand_aliasing={{0}: (4, {}), {1}: (5, {})} | custom-call | flops 1000000000 | bytes 6291456 | tf_op jit(solution)/shard_map/pallas_call | solution.py:121
  150.1 2.3 %shard_map.100 = (bf16[512,3072]{1,0:T(8,128)(2,1)}, bf16[512,3072]{1,0:T(8,128)(2,1)}) custom-call(s32[2]{0:T(128)S(1)} %pad_add_fusion.core.refs_0_.where, bf16[2,512,256]{2,1,0:T(8,128)(2,1)S(1)} %collective-permute-done.29.refs_0_, bf16[2,512,256]{2,1,0:T(8,128)(2,1)S(1)} %collective-permute-done.33.refs_1_, ...), custom_call_target="tpu_custom_call", output_to_operand_aliasing={{0}: (4, {}), {1}: (5, {})} | custom-call | flops 1000000000 | bytes 6291456 | tf_op jit(solution)/shard_map/pallas_call | solution.py:121
  (106 shorter events, 32.6 us)
Async XLA Ops:
  6.2 62.3 %collective-permute-start.4 = (bf16[512,3072]{1,0:T(8,128)(2,1)S(1)}, bf16[512,3072]{1,0:T(8,128)(2,1)S(1)}, u32[]{:S(2)}, u32[]{:S(2)}) collective-permute-start(bf16[512,3072]{1,0:T(8,128)(2,1)S(1)} %fusion.2.refs_1_), channel_id=1, source_target_pairs={{0,32},{32,0},{1,33},{33,1},{2,34},{34,2},{3,35},{35,3},{4,36},{36... | collective-permute-start | bytes 9437192 | tf_op jit(solution)/shard_map/ppermute | solution.py:246
  7.6 7.9 %collective-permute-start.1 = (f32[96,512]{1,0:T(8,128)S(1)}, f32[96,512]{1,0:T(8,128)S(1)}, u32[]{:S(2)}, u32[]{:S(2)}) collective-permute-start(f32[96,512]{1,0:T(8,128)S(1)} %get-tuple-element.42), channel_id=1, source_target_pairs={{0,64},{64,0},{1,65},{65,1},{2,66},{66,2},{3,67},{67,3},{4,68},{68... | collective-permute-start | bytes 589832 | tf_op jit(solution)/shard_map/ppermute | solution.py:229
  9.7 10.0 %collective-permute-start.2 = (f32[96,512]{1,0:T(8,128)S(1)}, f32[96,512]{1,0:T(8,128)S(1)}, u32[]{:S(2)}, u32[]{:S(2)}) collective-permute-start(f32[96,512]{1,0:T(8,128)S(1)} %get-tuple-element.44), channel_id=1, source_target_pairs={{0,64},{64,0},{1,65},{65,1},{2,66},{66,2},{3,67},{67,3},{4,68},{68... | collective-permute-start | bytes 589832 | tf_op jit(solution)/shard_map/ppermute | solution.py:229
  9.8 14.5 %collective-permute-start.3 = (f32[96,512]{1,0:T(8,128)S(1)}, f32[96,512]{1,0:T(8,128)S(1)}, u32[]{:S(2)}, u32[]{:S(2)}) collective-permute-start(f32[96,512]{1,0:T(8,128)S(1)} %get-tuple-element.46), channel_id=1, source_target_pairs={{0,64},{64,0},{1,65},{65,1},{2,66},{66,2},{3,67},{67,3},{4,68},{68... | collective-permute-start | bytes 589832 | tf_op jit(solution)/shard_map/ppermute | solution.py:229
  26.4 8.7 %collective-permute-start.20 = (bf16[2,96,512]{2,1,0:T(8,128)(2,1)S(1)}, bf16[2,96,512]{2,1,0:T(8,128)(2,1)S(1)}, u32[]{:S(2)}, u32[]{:S(2)}) collective-permute-start(bf16[2,96,512]{2,1,0:T(8,128)(2,1)S(1)} %pad_maximum_fusion.10), channel_id=1, source_target_pairs={{0,24},{8,16},{16,8},{24,0},{32,40},{40,32},{48,56},{56,48},{1,25}... | collective-permute-start | bytes 589832 | tf_op jit(solution)/shard_map/ppermute | solution.py:32
  28.7 10.3 %collective-permute-start.7 = (bf16[4,96,512]{2,1,0:T(8,128)(2,1)S(1)}, bf16[4,96,512]{2,1,0:T(8,128)(2,1)S(1)}, u32[]{:S(2)}, u32[]{:S(2)}) collective-permute-start(bf16[4,96,512]{2,1,0:T(8,128)(2,1)S(1)} %pad_maximum_fusion.3), channel_id=1, source_target_pairs={{0,8},{8,0},{16,24},{24,16},{32,56},{40,48},{48,40},{56,32},{1,9},... | collective-permute-start | bytes 1179656 | tf_op jit(solution)/shard_map/ppermute | solution.py:32
  29.5 9.4 %collective-permute-start.13 = (bf16[2,96,512]{2,1,0:T(8,128)(2,1)S(1)}, bf16[2,96,512]{2,1,0:T(8,128)(2,1)S(1)}, u32[]{:S(2)}, u32[]{:S(2)}) collective-permute-start(bf16[2,96,512]{2,1,0:T(8,128)(2,1)S(1)} %pad_maximum_fusion.9), channel_id=1, source_target_pairs={{0,65},{1,64},{32,96},{33,97},{64,1},{65,0},{96,32},{97,33},{2,67}... | collective-permute-start | bytes 589832 | tf_op jit(solution)/shard_map/ppermute | solution.py:32
  38.9 9.3 %collective-permute-start.14 = (bf16[4,96,512]{2,1,0:T(8,128)(2,1)S(1)}, bf16[4,96,512]{2,1,0:T(8,128)(2,1)S(1)}, u32[]{:S(2)}, u32[]{:S(2)}) collective-permute-start(bf16[4,96,512]{2,1,0:T(8,128)(2,1)S(1)} %pad_maximum_fusion.4), channel_id=1, source_target_pairs={{0,2},{2,0},{4,6},{6,4},{32,38},{34,36},{36,34},{38,32},{1,3},{3,1... | collective-permute-start | bytes 1179656 | tf_op jit(solution)/shard_map/ppermute | solution.py:32
  39.1 13.3 %collective-permute-start.8 = (bf16[8,96,512]{2,1,0:T(8,128)(2,1)S(1)}, bf16[8,96,512]{2,1,0:T(8,128)(2,1)S(1)}, u32[]{:S(2)}, u32[]{:S(2)}) collective-permute-start(bf16[8,96,512]{2,1,0:T(8,128)(2,1)S(1)} %pad_maximum_fusion.refs_0_), channel_id=1, source_target_pairs={{0,24},{8,16},{16,8},{24,0},{32,40},{40,32},{48,56},{56,48},{1,25}... | collective-permute-start | bytes 2359304 | tf_op jit(solution)/shard_map/ppermute | solution.py:32
  43.1 18.8 %collective-permute-start.22 = (bf16[8,96,512]{2,1,0:T(8,128)(2,1)S(1)}, bf16[8,96,512]{2,1,0:T(8,128)(2,1)S(1)}, u32[]{:S(2)}, u32[]{:S(2)}) collective-permute-start(bf16[8,96,512]{2,1,0:T(8,128)(2,1)S(1)} %pad_maximum_fusion.2.refs_0_), channel_id=1, source_target_pairs={{0,65},{1,64},{32,96},{33,97},{64,1},{65,0},{96,32},{97,33},{2,67}... | collective-permute-start | bytes 2359304 | tf_op jit(solution)/shard_map/ppermute | solution.py:32
  48.3 18.5 %collective-permute-start.15 = (bf16[8,96,512]{2,1,0:T(8,128)(2,1)S(1)}, bf16[8,96,512]{2,1,0:T(8,128)(2,1)S(1)}, u32[]{:S(2)}, u32[]{:S(2)}) collective-permute-start(bf16[8,96,512]{2,1,0:T(8,128)(2,1)S(1)} %pad_maximum_fusion.1.refs_0_), channel_id=1, source_target_pairs={{0,6},{2,4},{4,2},{6,0},{32,34},{34,32},{36,38},{38,36},{1,7},{3,5... | collective-permute-start | bytes 2359304 | tf_op jit(solution)/shard_map/ppermute | solution.py:32
  52.7 19.0 %collective-permute-start.26 = (bf16[16,96,256]{2,1,0:T(8,128)(2,1)S(1)}, bf16[16,96,256]{2,1,0:T(8,128)(2,1)S(1)}, u32[]{:S(2)}, u32[]{:S(2)}) collective-permute-start(bf16[16,96,256]{2,1,0:T(8,128)(2,1)S(1)} %bitcast.34), channel_id=1, source_target_pairs={{0,64},{1,65},{32,97},{33,96},{64,0},{65,1},{96,33},{97,32},{2,66}... | collective-permute-start | bytes 2359304 | tf_op jit(solution)/shard_map/ppermute | solution.py:32
  52.8 22.3 %collective-permute-start.27 = (bf16[16,96,256]{2,1,0:T(8,128)(2,1)S(1)}, bf16[16,96,256]{2,1,0:T(8,128)(2,1)S(1)}, u32[]{:S(2)}, u32[]{:S(2)}) collective-permute-start(bf16[16,96,256]{2,1,0:T(8,128)(2,1)S(1)} %bitcast.35), channel_id=1, source_target_pairs={{0,65},{1,64},{32,96},{33,97},{64,1},{65,0},{96,32},{97,33},{2,67}... | collective-permute-start | bytes 2359304 | tf_op jit(solution)/shard_map/ppermute | solution.py:32
  62.1 17.9 %collective-permute-start.23 = (bf16[16,96,256]{2,1,0:T(8,128)(2,1)S(1)}, bf16[16,96,256]{2,1,0:T(8,128)(2,1)S(1)}, u32[]{:S(2)}, u32[]{:S(2)}) collective-permute-start(bf16[16,96,256]{2,1,0:T(8,128)(2,1)S(1)} %bitcast.29), channel_id=1, source_target_pairs={{0,2},{2,0},{4,6},{6,4},{32,38},{34,36},{36,34},{38,32},{1,3},{3,1... | collective-permute-start | bytes 2359304 | tf_op jit(solution)/shard_map/ppermute | solution.py:32
  66.8 16.1 %collective-permute-start.24 = (bf16[16,96,256]{2,1,0:T(8,128)(2,1)S(1)}, bf16[16,96,256]{2,1,0:T(8,128)(2,1)S(1)}, u32[]{:S(2)}, u32[]{:S(2)}) collective-permute-start(bf16[16,96,256]{2,1,0:T(8,128)(2,1)S(1)} %bitcast.30), channel_id=1, source_target_pairs={{0,6},{2,4},{4,2},{6,0},{32,34},{34,32},{36,38},{38,36},{1,7},{3,5... | collective-permute-start | bytes 2359304 | tf_op jit(solution)/shard_map/ppermute | solution.py:32
  68.5 25.9 %collective-permute-start.16 = (bf16[16,96,256]{2,1,0:T(8,128)(2,1)S(1)}, bf16[16,96,256]{2,1,0:T(8,128)(2,1)S(1)}, u32[]{:S(2)}, u32[]{:S(2)}) collective-permute-start(bf16[16,96,256]{2,1,0:T(8,128)(2,1)S(1)} %bitcast.26), channel_id=1, source_target_pairs={{0,8},{8,0},{16,24},{24,16},{32,56},{40,48},{48,40},{56,32},{1,9},... | collective-permute-start | bytes 2359304 | tf_op jit(solution)/shard_map/ppermute | solution.py:32
  71.7 22.7 %collective-permute-start.17 = (bf16[16,96,256]{2,1,0:T(8,128)(2,1)S(1)}, bf16[16,96,256]{2,1,0:T(8,128)(2,1)S(1)}, u32[]{:S(2)}, u32[]{:S(2)}) collective-permute-start(bf16[16,96,256]{2,1,0:T(8,128)(2,1)S(1)} %bitcast.27), channel_id=1, source_target_pairs={{0,24},{8,16},{16,8},{24,0},{32,40},{40,32},{48,56},{56,48},{1,25}... | collective-permute-start | bytes 2359304 | tf_op jit(solution)/shard_map/ppermute | solution.py:32
  75.2 23.2 %collective-permute-start.9 = (bf16[16,96,256]{2,1,0:T(8,128)(2,1)S(1)}, bf16[16,96,256]{2,1,0:T(8,128)(2,1)S(1)}, u32[]{:S(2)}, u32[]{:S(2)}) collective-permute-start(bf16[16,96,256]{2,1,0:T(8,128)(2,1)S(1)} %bitcast.23), channel_id=1, source_target_pairs={{0,64},{1,65},{32,97},{33,96},{64,0},{65,1},{96,33},{97,32},{2,66}... | collective-permute-start | bytes 2359304 | tf_op jit(solution)/shard_map/ppermute | solution.py:32
  80.0 19.5 %collective-permute-start.10 = (bf16[16,96,256]{2,1,0:T(8,128)(2,1)S(1)}, bf16[16,96,256]{2,1,0:T(8,128)(2,1)S(1)}, u32[]{:S(2)}, u32[]{:S(2)}) collective-permute-start(bf16[16,96,256]{2,1,0:T(8,128)(2,1)S(1)} %bitcast.24), channel_id=1, source_target_pairs={{0,65},{1,64},{32,96},{33,97},{64,1},{65,0},{96,32},{97,33},{2,67}... | collective-permute-start | bytes 2359304 | tf_op jit(solution)/shard_map/ppermute | solution.py:32
  82.9 21.3 %collective-permute-start.28 = (bf16[16,96,256]{2,1,0:T(8,128)(2,1)S(1)}, bf16[16,96,256]{2,1,0:T(8,128)(2,1)S(1)}, u32[]{:S(2)}, u32[]{:S(2)}) collective-permute-start(bf16[16,96,256]{2,1,0:T(8,128)(2,1)S(1)} %collective-permute-done.26.refs_5_), channel_id=1, source_target_pairs={{0,65},{1,64},{32,96},{33,97},{64,1},{65,0},{96,32},{97,33},{2,67}... | collective-permute-start | bytes 2359304 | tf_op jit(solution)/shard_map/ppermute | solution.py:32
  94.4 17.8 %collective-permute-start.30 = (bf16[16,96,256]{2,1,0:T(8,128)(2,1)S(1)}, bf16[16,96,256]{2,1,0:T(8,128)(2,1)S(1)}, u32[]{:S(2)}, u32[]{:S(2)}) collective-permute-start(bf16[16,96,256]{2,1,0:T(8,128)(2,1)S(1)} %bitcast.17), channel_id=1, source_target_pairs={{0,2},{2,0},{4,6},{6,4},{32,38},{34,36},{36,34},{38,32},{1,3},{3,1... | collective-permute-start | bytes 2359304 | tf_op jit(solution)/shard_map/ppermute | solution.py:32
  94.5 26.0 %collective-permute-start.34 = (bf16[16,96,256]{2,1,0:T(8,128)(2,1)S(1)}, bf16[16,96,256]{2,1,0:T(8,128)(2,1)S(1)}, u32[]{:S(2)}, u32[]{:S(2)}) collective-permute-start(bf16[16,96,256]{2,1,0:T(8,128)(2,1)S(1)} %bitcast.20), channel_id=1, source_target_pairs={{0,8},{8,0},{16,24},{24,16},{32,56},{40,48},{48,40},{56,32},{1,9},... | collective-permute-start | bytes 2359304 | tf_op jit(solution)/shard_map/ppermute | solution.py:32
  98.4 17.4 %collective-permute-start.25 = (bf16[16,96,256]{2,1,0:T(8,128)(2,1)S(1)}, bf16[16,96,256]{2,1,0:T(8,128)(2,1)S(1)}, u32[]{:S(2)}, u32[]{:S(2)}) collective-permute-start(bf16[16,96,256]{2,1,0:T(8,128)(2,1)S(1)} %collective-permute-done.23.refs_5_), channel_id=1, source_target_pairs={{0,6},{2,4},{4,2},{6,0},{32,34},{34,32},{36,38},{38,36},{1,7},{3,5... | collective-permute-start | bytes 2359304 | tf_op jit(solution)/shard_map/ppermute | solution.py:32
  99.5 24.0 %collective-permute-start.18 = (bf16[16,96,256]{2,1,0:T(8,128)(2,1)S(1)}, bf16[16,96,256]{2,1,0:T(8,128)(2,1)S(1)}, u32[]{:S(2)}, u32[]{:S(2)}) collective-permute-start(bf16[16,96,256]{2,1,0:T(8,128)(2,1)S(1)} %collective-permute-done.16.refs_5_), channel_id=1, source_target_pairs={{0,24},{8,16},{16,8},{24,0},{32,40},{40,32},{48,56},{56,48},{1,25}... | collective-permute-start | bytes 2359304 | tf_op jit(solution)/shard_map/ppermute | solution.py:32
  104.3 24.0 %collective-permute-start.11 = (bf16[16,96,256]{2,1,0:T(8,128)(2,1)S(1)}, bf16[16,96,256]{2,1,0:T(8,128)(2,1)S(1)}, u32[]{:S(2)}, u32[]{:S(2)}) collective-permute-start(bf16[16,96,256]{2,1,0:T(8,128)(2,1)S(1)} %collective-permute-done.9.refs_5_), channel_id=1, source_target_pairs={{0,65},{1,64},{32,96},{33,97},{64,1},{65,0},{96,32},{97,33},{2,67}... | collective-permute-start | bytes 2359304 | tf_op jit(solution)/shard_map/ppermute | solution.py:32
  112.2 21.0 %collective-permute-start.31 = (bf16[16,96,256]{2,1,0:T(8,128)(2,1)S(1)}, bf16[16,96,256]{2,1,0:T(8,128)(2,1)S(1)}, u32[]{:S(2)}, u32[]{:S(2)}) collective-permute-start(bf16[16,96,256]{2,1,0:T(8,128)(2,1)S(1)} %bitcast.18), channel_id=1, source_target_pairs={{0,6},{2,4},{4,2},{6,0},{32,34},{34,32},{36,38},{38,36},{1,7},{3,5... | collective-permute-start | bytes 2359304 | tf_op jit(solution)/shard_map/ppermute | solution.py:32
  115.8 18.4 %collective-permute-start.32 = (bf16[16,96,256]{2,1,0:T(8,128)(2,1)S(1)}, bf16[16,96,256]{2,1,0:T(8,128)(2,1)S(1)}, u32[]{:S(2)}, u32[]{:S(2)}) collective-permute-start(bf16[16,96,256]{2,1,0:T(8,128)(2,1)S(1)} %collective-permute-done.30.refs_5_), channel_id=1, source_target_pairs={{0,6},{2,4},{4,2},{6,0},{32,34},{34,32},{36,38},{38,36},{1,7},{3,5... | collective-permute-start | bytes 2359304 | tf_op jit(solution)/shard_map/ppermute | solution.py:32
  120.4 18.3 %collective-permute-start.35 = (bf16[16,96,256]{2,1,0:T(8,128)(2,1)S(1)}, bf16[16,96,256]{2,1,0:T(8,128)(2,1)S(1)}, u32[]{:S(2)}, u32[]{:S(2)}) collective-permute-start(bf16[16,96,256]{2,1,0:T(8,128)(2,1)S(1)} %bitcast.21), channel_id=1, source_target_pairs={{0,24},{8,16},{16,8},{24,0},{32,40},{40,32},{48,56},{56,48},{1,25}... | collective-permute-start | bytes 2359304 | tf_op jit(solution)/shard_map/ppermute | solution.py:32
  123.5 18.6 %collective-permute-start.36 = (bf16[16,96,256]{2,1,0:T(8,128)(2,1)S(1)}, bf16[16,96,256]{2,1,0:T(8,128)(2,1)S(1)}, u32[]{:S(2)}, u32[]{:S(2)}) collective-permute-start(bf16[16,96,256]{2,1,0:T(8,128)(2,1)S(1)} %collective-permute-done.34.refs_5_), channel_id=1, source_target_pairs={{0,24},{8,16},{16,8},{24,0},{32,40},{40,32},{48,56},{56,48},{1,25}... | collective-permute-start | bytes 2359304 | tf_op jit(solution)/shard_map/ppermute | solution.py:32
  128.3 19.0 %collective-permute-start.40 = (bf16[2,512,256]{2,1,0:T(8,128)(2,1)S(1)}, bf16[2,512,256]{2,1,0:T(8,128)(2,1)S(1)}, u32[]{:S(2)}, u32[]{:S(2)}) collective-permute-start(bf16[2,512,256]{2,1,0:T(8,128)(2,1)S(1)} %get-tuple-element.71), channel_id=1, source_target_pairs={{0,32},{32,0},{1,33},{33,1},{2,34},{34,2},{3,35},{35,3},{4,36},{36... | collective-permute-start | bytes 1572872 | tf_op jit(solution)/shard_map/ppermute | solution.py:267
  133.2 14.2 %collective-permute-start.39 = (bf16[2,512,256]{2,1,0:T(8,128)(2,1)S(1)}, bf16[2,512,256]{2,1,0:T(8,128)(2,1)S(1)}, u32[]{:S(2)}, u32[]{:S(2)}) collective-permute-start(bf16[2,512,256]{2,1,0:T(8,128)(2,1)S(1)} %get-tuple-element.70), channel_id=1, source_target_pairs={{0,32},{32,0},{1,33},{33,1},{2,34},{34,2},{3,35},{35,3},{4,36},{36... | collective-permute-start | bytes 1572872 | tf_op jit(solution)/shard_map/ppermute | solution.py:267
  134.2 13.2 %collective-permute-start.38 = (bf16[2,512,256]{2,1,0:T(8,128)(2,1)S(1)}, bf16[2,512,256]{2,1,0:T(8,128)(2,1)S(1)}, u32[]{:S(2)}, u32[]{:S(2)}) collective-permute-start(bf16[2,512,256]{2,1,0:T(8,128)(2,1)S(1)} %get-tuple-element.69), channel_id=1, source_target_pairs={{0,32},{32,0},{1,33},{33,1},{2,34},{34,2},{3,35},{35,3},{4,36},{36... | collective-permute-start | bytes 1572872 | tf_op jit(solution)/shard_map/ppermute | solution.py:267
  (17 other events, 137.8 us)

commit v3 on v2

v3 whole, which is shorter than its diff:
```python
import jax
import jax.numpy as jnp
import numpy as np
from jax import lax
from jax.experimental import pallas as pl
from jax.experimental.pallas import tpu as pltpu
from jax.sharding import Mesh
from jax.sharding import PartitionSpec as P

HEAD = 128
EMA = 0.99
COLORS = 3
VMEM_LIMIT = 20 * 2**20
TILE = 256
FIRST, SECOND = (1, 3), (3, 1)
ORDER = (180, 156)
DIMS = (("x", "y", "z"), ("y", "z", "x"), ("z", "x", "y"))


def exchange(x, dim, masks):
    if dim == "z":
        axes = ("zlo", "core", "zhi")
        pairs = []
        for zlo in range(2):
            for core in range(2):
                for zhi in range(2):
                    z = (2 * zhi + zlo) ^ masks[core]
                    pairs.append(((zlo * 2 + core) * 2 + zhi, ((z % 2) * 2 + core) * 2 + z // 2))
    else:
        axes = ("core", dim)
        pairs = [(core * 4 + i, core * 4 + (i ^ masks[core])) for core in range(2) for i in range(4)]
    return lax.ppermute(x, axes, pairs)


def fill(color, half, units, held, n):
    core = lax.axis_index("core")
    order = ORDER[0] + (ORDER[1] - ORDER[0]) * core
    dims = DIMS[color]
    place = {
        "x": lax.axis_index("x"),
        "y": lax.axis_index("y"),
        "z": 2 * lax.axis_index("zhi") + lax.axis_index("zlo"),
    }
    seen = {d: [lax.bitwise_xor(v, lax.bitwise_and(lax.shift_right_logical(order, 2 * i), 3)) for i in range(4)] for d, v in place.items()}
    low = lambda v: lax.bitwise_and(v, 1)
    high = lambda v: lax.shift_right_logical(v, 1)
    rows = units[0].shape[1]
    if dims[2] == "z":
        row_of = {"x": lambda v: v * 2, "y": lambda v: v * 8, "z": high}
    elif dims[2] == "x":
        row_of = {"x": lambda v: low(v) * 2, "y": lambda v: v * 4, "z": high}
    else:
        row_of = {"x": lambda v: v * 2, "y": lambda v: low(v) * 8, "z": high}
    at_row = {d: [row_of[d](v) * rows for v in seen[d]] for d in dims}
    at_col = [0 if dims[2] == "z" else low(v) * n for v in seen["z"]]

    def copy(u):
        for pos in range(16):
            i = dict(zip(dims, (pos % 4, pos // 4, u)))
            row = pl.multiple_of(at_row["x"][i["x"]] + at_row["y"][i["y"]] + at_row["z"][i["z"]], rows)
            col = at_col[i["z"]]
            col = col if isinstance(col, int) else pl.multiple_of(col, n)
            held[pl.ds(row, rows), pl.ds(col, n)] = units[u][pos]

    if dims[2] == "z":
        for u in ((1, 2), (0, 3))[half]:
            copy(u)
    else:
        copy((0, 3)[half])
        for u in (1, 2):
            pl.when(core == (u - 1 if half == 0 else 2 - u))(lambda u=u: copy(u))


def tokens_of(color, half, src, m):
    last = DIMS[color][2]
    span = slice(m, m + TILE)
    if last == "z":
        return src[span, :]
    width = src.shape[1]
    side = lax.bitwise_xor(lax.shift_right_logical(lax.axis_index(last), 1), half)
    if last == "y":
        return src[span, pl.ds(pl.multiple_of(side * (width // 2), HEAD), width // 2)]
    cut = width // 8
    return jnp.concatenate(
        [src[span, pl.ds(pl.multiple_of(side * cut + y * 2 * cut, HEAD), cut)] for y in range(4)], axis=1
    )


def head_norm(v, gain):
    v = v * lax.rsqrt(jnp.mean(v * v, axis=-1, keepdims=True) + 1e-06) * gain
    return v.astype(jnp.bfloat16)


def begin_body(color, where, own, other, gains, *refs):
    units, (out, held) = refs[:4], refs[4:]
    n = units[0].shape[2]
    fill(color, 0, units, held, n)
    for t, src in enumerate((own, other)):
        for m in range(0, own.shape[0], TILE):
            y = jnp.dot(tokens_of(color, 0, src, m), held[...], preferred_element_type=jnp.float32)
            if DIMS[color][2] == "z":
                y = y * own.shape[1] ** (-0.5)
                gain = jnp.where(where[1] == 0, gains[1:2, :], gains[0:1, :])
                for h in range(0, n, HEAD):
                    out[t, m : m + TILE, h : h + HEAD] = head_norm(y[:, h : h + HEAD], gain)
            else:
                out[t, m : m + TILE, :] = y


def end_body(color, n_held, where, own, other, gains, begun, *refs):
    units = refs[:4]
    q_out, k_out, send_out, held = refs[4 + n_held :]
    n = units[0].shape[2]
    scale = own.shape[1] ** (-0.5)
    fill(color, 1, units, held, n)
    for t, src in enumerate((own, other)):
        for m in range(0, own.shape[0], TILE):
            span = slice(m, m + TILE)
            y = jnp.dot(tokens_of(color, 1, src, m), held[...], preferred_element_type=jnp.float32)
            outs = (q_out, k_out) if t == 0 else (send_out.at[0], send_out.at[1])
            if DIMS[color][2] == "z":
                y = y * scale
                gain = jnp.where(where[1] == 0, gains[0:1, :], gains[1:2, :])
                mine = jnp.concatenate([head_norm(y[:, h : h + HEAD], gain) for h in range(0, n, HEAD)], axis=1)
                early = begun[t, span, :]
                for i, out in enumerate(outs):

                    @pl.when(where[1] == i)
                    def _():
                        out[span, :] = mine

                    @pl.when(where[1] != i)
                    def _():
                        out[span, :] = early
            else:
                y = (y + begun[t, span, :]) * scale
                for i, out in enumerate(outs):
                    for h in range(0, n, HEAD):
                        out[span, h : h + HEAD] = head_norm(y[:, i * n + h : i * n + h + HEAD], gains[i : i + 1, :])


def project_half(color, half, where, own, other, gains, units, begun=None, outputs=()):
    tokens, width = own.shape
    n = units[0].shape[2]
    vmem, any_spec = pl.BlockSpec(memory_space=pltpu.VMEM), pl.BlockSpec(memory_space=pl.ANY)
    operands = [own, other, gains, *([] if half == 0 else [begun]), *units, *outputs]
    specs = [vmem] * (len(operands) - len(outputs)) + [any_spec] * len(outputs)
    by_block = DIMS[color][2] == "z"
    whole = lambda *shape: pl.BlockSpec(shape, lambda i, *_: (0,) * len(shape))
    if half == 0:
        body = lambda *refs: begin_body(color, *refs)
        out_shape = [jax.ShapeDtypeStruct((2, tokens, n), jnp.bfloat16) if by_block else jax.ShapeDtypeStruct((2, tokens, 2 * n), jnp.float32)]
        out_specs = [vmem]
        aliases = {}
    else:
        body = lambda *refs: end_body(color, len(outputs), *refs)
        big = jax.ShapeDtypeStruct((tokens, width), jnp.bfloat16)
        out_shape = [big, big, jax.ShapeDtypeStruct((2, tokens, n), jnp.bfloat16)]
        col = lambda i, where: (0, where[0] * COLORS + color)
        out_specs = [pl.BlockSpec((tokens, n), col), pl.BlockSpec((tokens, n), col), whole(2, tokens, n)]
        first = 1 + len(operands) - len(outputs)
        aliases = {first: 0, first + 1: 1} if outputs else {}
    return pl.pallas_call(
        body,
        grid_spec=pltpu.PrefetchScalarGridSpec(
            num_scalar_prefetch=1,
            grid=(1,),
            in_specs=specs,
            out_specs=out_specs,
            scratch_shapes=[pltpu.VMEM((width, n) if by_block else (width // 2, 2 * n), jnp.bfloat16)],
        ),
        out_shape=out_shape,
        input_output_aliases=aliases,
        compiler_params=pltpu.CompilerParams(vmem_limit_bytes=VMEM_LIMIT),
        cost_estimate=pl.CostEstimate(
            flops=2 * 2 * tokens * width * n,
            bytes_accessed=2 * width * (2 * tokens + 2 * n),
            transcendentals=0,
        ),
    )(where, *operands)


def put_body(where, got, q_in, k_in, q_out, k_out):
    q_out[...] = got[0]
    k_out[...] = got[1]


def put(color, where, got, query, key_out):
    _, half, n = got.shape
    col = lambda i, where: (i, (1 - where[0]) * COLORS + color)
    any_spec = pl.BlockSpec(memory_space=pl.ANY)
    return pl.pallas_call(
        put_body,
        grid_spec=pltpu.PrefetchScalarGridSpec(
            num_scalar_prefetch=1,
            grid=(2,),
            in_specs=[pl.BlockSpec((2, half // 2, n), lambda i, *_: (0, i, 0)), any_spec, any_spec],
            out_specs=[pl.BlockSpec((half // 2, n), col)] * 2,
        ),
        out_shape=[jax.ShapeDtypeStruct(query.shape, query.dtype)] * 2,
        input_output_aliases={2: 0, 3: 1},
        compiler_params=pltpu.CompilerParams(vmem_limit_bytes=8 * 2**20),
        cost_estimate=pl.CostEstimate(flops=10**9, bytes_accessed=8 * got.size, transcendentals=0),
    )(where, got, query, key_out)


def pick_body(core, local, out):
    out[0] = local[...]


def pick(core, local, block):
    rows = local.shape[0]
    return pl.pallas_call(
        pick_body,
        grid_spec=pltpu.PrefetchScalarGridSpec(
            num_scalar_prefetch=1,
            grid=(2,),
            in_specs=[pl.BlockSpec((rows, block), lambda j, core: (0, 2 * j + 1 - core[0]))],
            out_specs=pl.BlockSpec((1, rows, block), lambda j, core: (j, 0, 0)),
        ),
        out_shape=jax.ShapeDtypeStruct((2, rows, block), jnp.float32),
        compiler_params=pltpu.CompilerParams(vmem_limit_bytes=8 * 2**20),
        cost_estimate=pl.CostEstimate(flops=10**9, bytes_accessed=16 * rows * block, transcendentals=0),
        name="pick",
    )(core, local)


def merge_body(n, where, local, got, keep, rest, *give):
    total = local[...] + got[0]
    mine = pl.program_id(0) == where[1]

    @pl.when(mine)
    def _():
        keep[...] = total

    @pl.when(jnp.logical_not(mine))
    def _():
        high = total.astype(jnp.bfloat16)
        rest[...] = (total - high.astype(jnp.float32)).astype(jnp.bfloat16)
        for k in range(COLORS):
            give[k][...] = high[:, k * n : (k + 1) * n]


def merge(where, local, got):
    _, rows, block = got.shape
    n = block // COLORS
    return pl.pallas_call(
        lambda *refs: merge_body(n, *refs),
        grid_spec=pltpu.PrefetchScalarGridSpec(
            num_scalar_prefetch=1,
            grid=(2,),
            in_specs=[
                pl.BlockSpec((rows, block), lambda j, where: (0, 2 * j + where[0])),
                pl.BlockSpec((1, rows, block), lambda j, where: (j, 0, 0)),
            ],
            out_specs=[pl.BlockSpec((rows, block), lambda *_: (0, 0))] * 2 + [pl.BlockSpec((rows, n), lambda *_: (0, 0))] * COLORS,
        ),
        out_shape=[jax.ShapeDtypeStruct((rows, block), jnp.float32), jax.ShapeDtypeStruct((rows, block), jnp.bfloat16)]
        + [jax.ShapeDtypeStruct((rows, n), jnp.bfloat16)] * COLORS,
        compiler_params=pltpu.CompilerParams(vmem_limit_bytes=16 * 2**20),
        cost_estimate=pl.CostEstimate(flops=10**9, bytes_accessed=24 * rows * block, transcendentals=0),
        name="merge",
    )(where, local, got)


def shards(tokens, student, teacher, norm_gain, query_gain, key_gain):
    block = teacher.shape[1]
    n = block // COLORS
    core = lax.axis_index("core")
    where = jnp.stack([core, lax.axis_index("zlo")]).astype(jnp.int32)
    swap = [(0, 1), (1, 0)]

    local = student[0]
    got = lax.ppermute(pick(where, local, block), "core", swap)
    keep, rest, *give = merge(where, local, got)
    arrived, copied = [], []
    for k in range(COLORS):
        arrived.append(lax.ppermute(give[k], "zlo", swap).astype(jnp.float32))
    rest = lax.ppermute(rest, "zlo", swap).astype(jnp.float32)
    for k in range(COLORS):
        cut = keep[:, k * n : (k + 1) * n]
        if k:
            cut, _ = lax.optimization_barrier((cut, copied[-1]))
        copied.append(((cut + arrived[k]) / 4).astype(jnp.bfloat16)[None])
    high = jnp.concatenate(arrived, axis=1)
    student_new = (keep + (high + rest)) / 4
    teacher_new = EMA * teacher + (1.0 - EMA) * student_new

    wide = tokens.astype(jnp.float32)
    normed = (
        wide * lax.rsqrt(jnp.mean(wide * wide, axis=-1, keepdims=True) + 1e-06) * norm_gain
    ).astype(jnp.bfloat16)
    other = lax.ppermute(normed, "core", swap)

    for s in range(4):
        for k in range(COLORS):
            got = exchange(copied[k], DIMS[k][s // 2], (FIRST, SECOND)[s % 2])
            copied[k] = jnp.concatenate([copied[k], got], axis=0)
    gains = jnp.stack([query_gain, key_gain])
    units, begun = [], []
    for k in range(COLORS):
        one = exchange(copied[k], DIMS[k][2], FIRST)
        two = exchange(copied[k], DIMS[k][2], SECOND)
        three = exchange(one, DIMS[k][2], SECOND)
        units.append([copied[k], one, two, three])
        begun += project_half(k, 0, where, normed, other, gains, [copied[k], one, two, copied[k]])
    outputs, back = (), []
    for k in range(COLORS):
        *outputs, send = project_half(k, 1, where, normed, other, gains, units[k], begun[k], outputs)
        back.append(lax.ppermute(send, "core", swap))
    where, student_new, teacher_new = lax.optimization_barrier((where, student_new, teacher_new))
    for k in range(COLORS):
        outputs = put(k, where, back[k], *outputs)
    return (teacher_new, student_new, *outputs)


def solution(mesh):
    split = Mesh(np.asarray(mesh.devices).reshape(2, 2, 4, 4, 2), ("zlo", "core", "y", "x", "zhi"))
    group, fsdp = ("zlo", "core"), ("y", "x", "zhi")
    rows = P(group + fsdp, None)

    return jax.shard_map(
        shards,
        mesh=split,
        in_specs=(rows, P(group, fsdp, None), P(fsdp, group), P(), P(), P()),
        out_specs=(P(fsdp, group), P(fsdp, group), rows, rows),
        check_vma=False,
    )
```

time: 154 us -> 159 us (1.032)
  waiting for transfers between devices: 32.9 us -> 61.3 us
  starting transfers between devices: 77.6 us -> 50.2 us
  Pallas kernels: 34.3 us -> 37.3 us
    ppermute x30 -> x21, starting transfers between devices: 71.8 us -> 45.3 us  [exchange(): return lax.ppermute(x, axes, pairs)]
    ppermute x30 -> x21, waiting for transfers between devices: 26.2 us -> 49 us  [exchange(): return lax.ppermute(x, axes, pairs)]
    ppermute x9 -> x7, waiting for transfers between devices: 6.64 us -> 11.2 us  [the longest x1 9.32 us: shards(): rest = lax.ppermute(rest, 'zlo', swap).astype(jnp.float32)]
    pallas_call x9 -> x6, Pallas kernels: 28 us -> 30.6 us  [project_half(): pl.pallas_call(body, grid_spec=pltpu.PrefetchScalarGridSpec(num_scalar_pr...]
    ppermute x9 -> x7, starting transfers between devices: 5.68 us -> 4.76 us  [the longest x3 4.21 us: shards(): arrived.append(lax.ppermute(give[k], 'zlo', swap).astype(jnp.float32))]
    pallas_call x2 -> x3, Pallas kernels: 4.69 us -> 4.96 us  [put(): pl.pallas_call(put_body, grid_spec=pltpu.PrefetchScalarGridSpec(num_scala...]
  transfers between devices with their start and end apart: 41 -> 30, of which waited for: 15 -> 13; matrix products, arithmetic and copies ran while one was open for 2% -> 3% of each run, Pallas kernels for 20% -> 22%
where the time goes in v3:
time: 159 us; the launch traced here: 157 us
  waiting for transfers between devices  61.3 us (39%)
  starting transfers between devices  50.2 us (32%)
  Pallas kernels  37.3 us (23%)
  other arithmetic  3.68 us (2%)
  local copies, waits for them, and re-layouts  3.02 us (2%)
    ppermute x21, waiting for transfers between devices, exchange(): return lax.ppermute(x, axes, pairs)  49 us
    ppermute x21, starting transfers between devices, exchange(): return lax.ppermute(x, axes, pairs)  45.3 us
    pallas_call x6, Pallas kernels, project_half(): pl.pallas_call(body, grid_spec=pltpu.PrefetchScalarGridSpec(num_scalar_pr...  30.6 us
    ppermute x1, waiting for transfers between devices, shards(): rest = lax.ppermute(rest, 'zlo', swap).astype(jnp.float32)  9.32 us
    pallas_call x3, Pallas kernels, put(): pl.pallas_call(put_body, grid_spec=pltpu.PrefetchScalarGridSpec(num_scala...  4.96 us
    ppermute x3, starting transfers between devices, shards(): arrived.append(lax.ppermute(give[k], 'zlo', swap).astype(jnp.float32))  4.21 us
  transfers between devices with their start and end apart: 30, of which 13 were waited for; matrix products, arithmetic and copies ran while one was open for 3% of the time, Pallas kernels for 22%

profile of v3, /device:TPU:0, one launch (start us, length us, event | category | flops | bytes accessed | tf_op | source)
XLA Modules:
  0.0 156.5 jit_solution(6168664568216972010)
XLA Ops:
  0.7 1.7 %copy-done = f32[1,96,6144]{2,1,0:T(8,128)S(1)} copy-done((f32[1,96,6144]{2,1,0:T(8,128)S(1)}, f32[1,96,6144]{2,1,0:T(8,128)}, u32[]{:S(2)}) %copy-start) | copy-done | bytes 2359320
  7.1 2.1 %collective-permute-start.1 = (bf16[96,512]{1,0:T(8,128)(2,1)S(1)}, bf16[96,512]{1,0:T(8,128)(2,1)S(1)}, u32[]{:S(2)}, u32[]{:S(2)}) collective-permute-start(bf16[96,512]{1,0:T(8,128)(2,1)S(1)} %get-tuple-element.30), channel_id=1, source_target_pairs={{0,64},{64,0},{1,65},{65,1},{2,66},{66,2},{3,67},{67,3},{4,68},{68... | collective-permute-start | bytes 294920 | tf_op jit(solution)/shard_map/ppermute | solution.py:278
  10.5 1.8 %collective-permute-done.1 = bf16[96,512]{1,0:T(8,128)(2,1)S(1)} collective-permute-done((bf16[96,512]{1,0:T(8,128)(2,1)S(1)}, bf16[96,512]{1,0:T(8,128)(2,1)S(1)}, u32[]{:S(2)}, u32[]{:S(2)}) %collective-permute-start.1) | collective-permute-done | bytes 98336 | tf_op jit(solution)/shard_map/ppermute | solution.py:278
  13.9 1.8 %collective-permute-start.2 = (bf16[96,512]{1,0:T(8,128)(2,1)S(1)}, bf16[96,512]{1,0:T(8,128)(2,1)S(1)}, u32[]{:S(2)}, u32[]{:S(2)}) collective-permute-start(bf16[96,512]{1,0:T(8,128)(2,1)S(1)} %get-tuple-element.31), channel_id=1, source_target_pairs={{0,64},{64,0},{1,65},{65,1},{2,66},{66,2},{3,67},{67,3},{4,68},{68... | collective-permute-start | bytes 294920 | tf_op jit(solution)/shard_map/ppermute | solution.py:278
  17.0 2.8 %collective-permute-start.21 = (bf16[2,96,512]{2,1,0:T(8,128)(2,1)S(1)}, bf16[2,96,512]{2,1,0:T(8,128)(2,1)S(1)}, u32[]{:S(2)}, u32[]{:S(2)}) collective-permute-start(bf16[2,96,512]{2,1,0:T(8,128)(2,1)S(1)} %pad_maximum_fusion.8), channel_id=1, source_target_pairs={{0,6},{2,4},{4,2},{6,0},{32,34},{34,32},{36,38},{38,36},{1,7},{3,5... | collective-permute-start | bytes 589832 | tf_op jit(solution)/shard_map/ppermute | solution.py:32
  19.9 1.7 %collective-permute-start.13 = (bf16[1,96,512]{2,1,0:T(8,128)(2,1)S(1)}, bf16[1,96,512]{2,1,0:T(8,128)(2,1)S(1)}, u32[]{:S(2)}, u32[]{:S(2)}) collective-permute-start(bf16[1,96,512]{2,1,0:T(8,128)(2,1)S(1)} %get-tuple-element.57), channel_id=1, source_target_pairs={{0,8},{8,0},{16,24},{24,16},{32,56},{40,48},{48,40},{56,32},{1,9},... | collective-permute-start | bytes 294920 | tf_op jit(solution)/shard_map/ppermute | solution.py:32
  21.6 2.4 %collective-permute-done.21 = bf16[2,96,512]{2,1,0:T(8,128)(2,1)S(1)} collective-permute-done((bf16[2,96,512]{2,1,0:T(8,128)(2,1)S(1)}, bf16[2,96,512]{2,1,0:T(8,128)(2,1)S(1)}, u32[]{:S(2)}, u32[]{:S(2)}) %collective-permute-start.21) | collective-permute-done | bytes 196640 | tf_op jit(solution)/shard_map/ppermute | solution.py:32
  24.0 1.7 %collective-permute-start.22 = (bf16[4,96,512]{2,1,0:T(8,128)(2,1)S(1)}, bf16[4,96,512]{2,1,0:T(8,128)(2,1)S(1)}, u32[]{:S(2)}, u32[]{:S(2)}) collective-permute-start(bf16[4,96,512]{2,1,0:T(8,128)(2,1)S(1)} %pad_maximum_fusion.5), channel_id=1, source_target_pairs={{0,8},{8,0},{16,24},{24,16},{32,56},{40,48},{48,40},{56,32},{1,9},... | collective-permute-start | bytes 1179656 | tf_op jit(solution)/shard_map/ppermute | solution.py:32
  25.7 1.8 %collective-permute-start.6 = (bf16[1,96,512]{2,1,0:T(8,128)(2,1)S(1)}, bf16[1,96,512]{2,1,0:T(8,128)(2,1)S(1)}, u32[]{:S(2)}, u32[]{:S(2)}) collective-permute-start(bf16[1,96,512]{2,1,0:T(8,128)(2,1)S(1)} %get-tuple-element.59), channel_id=1, source_target_pairs={{0,64},{1,65},{32,97},{33,96},{64,0},{65,1},{96,33},{97,32},{2,66}... | collective-permute-start | bytes 294920 | tf_op jit(solution)/shard_map/ppermute | solution.py:32
  27.6 2.3 %collective-permute-start.14 = (bf16[2,96,512]{2,1,0:T(8,128)(2,1)S(1)}, bf16[2,96,512]{2,1,0:T(8,128)(2,1)S(1)}, u32[]{:S(2)}, u32[]{:S(2)}) collective-permute-start(bf16[2,96,512]{2,1,0:T(8,128)(2,1)S(1)} %pad_maximum_fusion.7), channel_id=1, source_target_pairs={{0,24},{8,16},{16,8},{24,0},{32,40},{40,32},{48,56},{56,48},{1,25}... | collective-permute-start | bytes 589832 | tf_op jit(solution)/shard_map/ppermute | solution.py:32
  30.5 3.9 %collective-permute-start.7 = (bf16[2,96,512]{2,1,0:T(8,128)(2,1)S(1)}, bf16[2,96,512]{2,1,0:T(8,128)(2,1)S(1)}, u32[]{:S(2)}, u32[]{:S(2)}) collective-permute-start(bf16[2,96,512]{2,1,0:T(8,128)(2,1)S(1)} %pad_maximum_fusion.6), channel_id=1, source_target_pairs={{0,65},{1,64},{32,96},{33,97},{64,1},{65,0},{96,32},{97,33},{2,67}... | collective-permute-start | bytes 589832 | tf_op jit(solution)/shard_map/ppermute | solution.py:32
  34.5 4.6 %collective-permute-start.23 = (bf16[8,96,512]{2,1,0:T(8,128)(2,1)S(1)}, bf16[8,96,512]{2,1,0:T(8,128)(2,1)S(1)}, u32[]{:S(2)}, u32[]{:S(2)}) collective-permute-start(bf16[8,96,512]{2,1,0:T(8,128)(2,1)S(1)} %pad_maximum_fusion.2), channel_id=1, source_target_pairs={{0,24},{8,16},{16,8},{24,0},{32,40},{40,32},{48,56},{56,48},{1,25}... | collective-permute-start | bytes 2359304 | tf_op jit(solution)/shard_map/ppermute | solution.py:32
  40.1 8.8 %collective-permute-done.15 = bf16[4,96,512]{2,1,0:T(8,128)(2,1)S(1)} collective-permute-done((bf16[4,96,512]{2,1,0:T(8,128)(2,1)S(1)}, bf16[4,96,512]{2,1,0:T(8,128)(2,1)S(1)}, u32[]{:S(2)}, u32[]{:S(2)}) %collective-permute-start.15) | collective-permute-done | bytes 393248 | tf_op jit(solution)/shard_map/ppermute | solution.py:32
  49.6 3.0 %collective-permute-start.9 = (bf16[8,96,512]{2,1,0:T(8,128)(2,1)S(1)}, bf16[8,96,512]{2,1,0:T(8,128)(2,1)S(1)}, u32[]{:S(2)}, u32[]{:S(2)}) collective-permute-start(bf16[8,96,512]{2,1,0:T(8,128)(2,1)S(1)} %pad_maximum_fusion), channel_id=1, source_target_pairs={{0,6},{2,4},{4,2},{6,0},{32,34},{34,32},{36,38},{38,36},{1,7},{3,5... | collective-permute-start | bytes 2359304 | tf_op jit(solution)/shard_map/ppermute | solution.py:32
  54.2 3.2 %collective-permute-start.25 = (bf16[16,96,512]{2,1,0:T(8,128)(2,1)S(1)}, bf16[16,96,512]{2,1,0:T(8,128)(2,1)S(1)}, u32[]{:S(2)}, u32[]{:S(2)}) collective-permute-start(bf16[16,96,512]{2,1,0:T(8,128)(2,1)S(1)} %constant_dynamic-update-slice_fusion.10.refs_4_.refs_7_.refs_5_), channel_id=1, source_target_pairs={{0,65},{1,64},{32,96},{33,97},{64,1},{65,0},{96,32},{97,33},{2,67}... | collective-permute-start | bytes 4718600 | tf_op jit(solution)/shard_map/ppermute | solution.py:32
  57.4 13.2 %collective-permute-done.16 = bf16[8,96,512]{2,1,0:T(8,128)(2,1)S(1)} collective-permute-done((bf16[8,96,512]{2,1,0:T(8,128)(2,1)S(1)}, bf16[8,96,512]{2,1,0:T(8,128)(2,1)S(1)}, u32[]{:S(2)}, u32[]{:S(2)}) %collective-permute-start.16) | collective-permute-done | bytes 786464 | tf_op jit(solution)/shard_map/ppermute | solution.py:32
  71.4 2.6 %collective-permute-start.18 = (bf16[16,96,512]{2,1,0:T(8,128)(2,1)S(1)}, bf16[16,96,512]{2,1,0:T(8,128)(2,1)S(1)}, u32[]{:S(2)}, u32[]{:S(2)}) collective-permute-start(bf16[16,96,512]{2,1,0:T(8,128)(2,1)S(1)} %constant_dynamic-update-slice_fusion.5.refs_4_.refs_7_.refs_5_), channel_id=1, source_target_pairs={{0,6},{2,4},{4,2},{6,0},{32,34},{34,32},{36,38},{38,36},{1,7},{3,5... | collective-permute-start | bytes 4718600 | tf_op jit(solution)/shard_map/ppermute | solution.py:32
  74.0 15.1 %collective-permute-done.24.refs_5_.refs_6_ = bf16[16,96,512]{2,1,0:T(8,128)(2,1)S(1)} collective-permute-done((bf16[16,96,512]{2,1,0:T(8,128)(2,1)S(1)}, bf16[16,96,512]{2,1,0:T(8,128)(2,1)S(1)}, u32[]{:S(2)}, u32[]{:S(2)}) %collective-permute-start.24) | collective-permute-done | bytes 1572896 | tf_op jit(solution)/shard_map/ppermute | solution.py:32
  89.1 2.9 %collective-permute-start.11 = (bf16[16,96,512]{2,1,0:T(8,128)(2,1)S(1)}, bf16[16,96,512]{2,1,0:T(8,128)(2,1)S(1)}, u32[]{:S(2)}, u32[]{:S(2)}) collective-permute-start(bf16[16,96,512]{2,1,0:T(8,128)(2,1)S(1)} %constant_dynamic-update-slice_fusion.refs_4_.refs_7_.refs_5_), channel_id=1, source_target_pairs={{0,24},{8,16},{16,8},{24,0},{32,40},{40,32},{48,56},{56,48},{1,25}... | collective-permute-start | bytes 4718600 | tf_op jit(solution)/shard_map/ppermute | solution.py:32
  92.1 4.0 %collective-permute-start.26 = (bf16[16,96,512]{2,1,0:T(8,128)(2,1)S(1)}, bf16[16,96,512]{2,1,0:T(8,128)(2,1)S(1)}, u32[]{:S(2)}, u32[]{:S(2)}) collective-permute-start(bf16[16,96,512]{2,1,0:T(8,128)(2,1)S(1)} %collective-permute-done.24.refs_5_.refs_6_), channel_id=1, source_target_pairs={{0,65},{1,64},{32,96},{33,97},{64,1},{65,0},{96,32},{97,33},{2,67}... | collective-permute-start | bytes 4718600 | tf_op jit(solution)/shard_map/ppermute | solution.py:32
  96.0 5.2 %collective-permute-done.17.refs_5_.refs_6_ = bf16[16,96,512]{2,1,0:T(8,128)(2,1)S(1)} collective-permute-done((bf16[16,96,512]{2,1,0:T(8,128)(2,1)S(1)}, bf16[16,96,512]{2,1,0:T(8,128)(2,1)S(1)}, u32[]{:S(2)}, u32[]{:S(2)}) %collective-permute-start.17) | collective-permute-done | bytes 1572896 | tf_op jit(solution)/shard_map/ppermute | solution.py:32
  102.8 1.8 %collective-permute-done.10.refs_5_.refs_6_ = bf16[16,96,512]{2,1,0:T(8,128)(2,1)S(1)} collective-permute-done((bf16[16,96,512]{2,1,0:T(8,128)(2,1)S(1)}, bf16[16,96,512]{2,1,0:T(8,128)(2,1)S(1)}, u32[]{:S(2)}, u32[]{:S(2)}) %collective-permute-start.10) | collective-permute-done | bytes 1572896 | tf_op jit(solution)/shard_map/ppermute | solution.py:32
  104.6 5.2 %collective-permute-start.12 = (bf16[16,96,512]{2,1,0:T(8,128)(2,1)S(1)}, bf16[16,96,512]{2,1,0:T(8,128)(2,1)S(1)}, u32[]{:S(2)}, u32[]{:S(2)}) collective-permute-start(bf16[16,96,512]{2,1,0:T(8,128)(2,1)S(1)} %collective-permute-done.10.refs_5_.refs_6_), channel_id=1, source_target_pairs={{0,24},{8,16},{16,8},{24,0},{32,40},{40,32},{48,56},{56,48},{1,25}... | collective-permute-start | bytes 4718600 | tf_op jit(solution)/shard_map/ppermute | solution.py:32
  109.8 4.5 %shard_map.95.refs_4_ = bf16[2,512,512]{2,1,0:T(8,128)(2,1)S(1)} custom-call(s32[2]{0:T(128)S(1)} %pad_add_fusion.core.refs_0_.where, bf16[512,3072]{1,0:T(8,128)(2,1)S(1)} %fusion.2.refs_1_, bf16[512,3072]{1,0:T(8,128)(2,1)S(1)} %collective-permute-done.5.refs_2_, f32[2,128]{1,0:T(2,128)S(1)} %pad_maximum_fusion.9.refs_3_, ...), custom_call_target="tpu_custom_call" | custom-call | flops 3221225472 | bytes 12582912 | tf_op jit(solution)/shard_map/pallas_call | solution.py:163
  114.3 4.3 %shard_map.94.refs_4_ = f32[2,512,1024]{2,1,0:T(8,128)S(1)} custom-call(s32[2]{0:T(128)S(1)} %pad_add_fusion.core.refs_0_.where, bf16[512,3072]{1,0:T(8,128)(2,1)S(1)} %fusion.2.refs_1_, bf16[512,3072]{1,0:T(8,128)(2,1)S(1)} %collective-permute-done.5.refs_2_, f32[2,128]{1,0:T(2,128)S(1)} %pad_maximum_fusion.9.refs_3_, ...), custom_call_target="tpu_custom_call" | custom-call | flops 3221225472 | bytes 12582912 | tf_op jit(solution)/shard_map/pallas_call | solution.py:163
  118.6 4.3 %shard_map.93.refs_4_ = f32[2,512,1024]{2,1,0:T(8,128)S(1)} custom-call(s32[2]{0:T(128)S(1)} %pad_add_fusion.core.refs_0_.where, bf16[512,3072]{1,0:T(8,128)(2,1)S(1)} %fusion.2.refs_1_, bf16[512,3072]{1,0:T(8,128)(2,1)S(1)} %collective-permute-done.5.refs_2_, f32[2,128]{1,0:T(2,128)S(1)} %pad_maximum_fusion.9.refs_3_, ...), custom_call_target="tpu_custom_call" | custom-call | flops 3221225472 | bytes 12582912 | tf_op jit(solution)/shard_map/pallas_call | solution.py:163
  122.8 6.6 %shard_map.96 = (bf16[512,3072]{1,0:T(8,128)(2,1)}, bf16[512,3072]{1,0:T(8,128)(2,1)}, bf16[2,512,512]{2,1,0:T(8,128)(2,1)S(1)}) custom-call(s32[2]{0:T(128)S(1)} %pad_add_fusion.core.refs_0_.where, bf16[512,3072]{1,0:T(8,128)(2,1)S(1)} %fusion.2.refs_1_, bf16[512,3072]{1,0:T(8,128)(2,1)S(1)} %collective-permute-done.5.refs_2_, ...), custom_call_target="tpu_custom_call" | custom-call | flops 3221225472 | bytes 12582912 | tf_op jit(solution)/shard_map/pallas_call | solution.py:163
  129.4 5.5 %shard_map.97 = (bf16[512,3072]{1,0:T(8,128)(2,1)}, bf16[512,3072]{1,0:T(8,128)(2,1)}, bf16[2,512,512]{2,1,0:T(8,128)(2,1)S(1)}) custom-call(s32[2]{0:T(128)S(1)} %pad_add_fusion.core.refs_0_.where, bf16[512,3072]{1,0:T(8,128)(2,1)S(1)} %fusion.2.refs_1_, ...), custom_call_target="tpu_custom_call", output_to_operand_aliasing={{0}: (9, {}), {1}: (10, {})} | custom-call | flops 3221225472 | bytes 12582912 | tf_op jit(solution)/shard_map/pallas_call | solution.py:163
  135.5 5.5 %shard_map.98 = (bf16[512,3072]{1,0:T(8,128)(2,1)}, bf16[512,3072]{1,0:T(8,128)(2,1)}, bf16[2,512,512]{2,1,0:T(8,128)(2,1)S(1)}) custom-call(s32[2]{0:T(128)S(1)} %pad_add_fusion.core.refs_0_.where, bf16[512,3072]{1,0:T(8,128)(2,1)S(1)} %fusion.2.refs_1_, ...), custom_call_target="tpu_custom_call", output_to_operand_aliasing={{0}: (9, {}), {1}: (10, {})} | custom-call | flops 3221225472 | bytes 12582912 | tf_op jit(solution)/shard_map/pallas_call | solution.py:163
  141.0 9.3 %collective-permute-done.4 = bf16[96,1536]{1,0:T(8,128)(2,1)S(1)} collective-permute-done((bf16[96,1536]{1,0:T(8,128)(2,1)S(1)}, bf16[96,1536]{1,0:T(8,128)(2,1)S(1)}, u32[]{:S(2)}, u32[]{:S(2)}) %collective-permute-start.4) | collective-permute-done | bytes 294944 | tf_op jit(solution)/shard_map/ppermute | solution.py:279
  151.6 1.7 %shard_map.99 = (bf16[512,3072]{1,0:T(8,128)(2,1)}, bf16[512,3072]{1,0:T(8,128)(2,1)}) custom-call(s32[2]{0:T(128)S(1)} %pad_add_fusion.core.refs_0_.where, bf16[2,512,512]{2,1,0:T(8,128)(2,1)S(1)} %collective-permute-done.29.got, bf16[512,3072]{1,0:T(8,128)(2,1)} %get-tuple-element.46.q_in, ...), custom_call_target="tpu_custom_call", output_to_operand_aliasing={{0}: (2, {}), {1}: (3, {})} | custom-call | flops 1000000000 | bytes 4194304 | tf_op jit(solution)/shard_map/pallas_call | solution.py:192
  153.2 1.7 %shard_map.100 = (bf16[512,3072]{1,0:T(8,128)(2,1)}, bf16[512,3072]{1,0:T(8,128)(2,1)}) custom-call(s32[2]{0:T(128)S(1)} %pad_add_fusion.core.refs_0_.where, bf16[2,512,512]{2,1,0:T(8,128)(2,1)S(1)} %collective-permute-done.28.got, bf16[512,3072]{1,0:T(8,128)(2,1)} %get-tuple-element.48.q_in, ...), custom_call_target="tpu_custom_call", output_to_operand_aliasing={{0}: (2, {}), {1}: (3, {})} | custom-call | flops 1000000000 | bytes 4194304 | tf_op jit(solution)/shard_map/pallas_call | solution.py:192
  (87 shorter events, 18.7 us)
Async XLA Ops:
  3.2 2.9 %collective-permute-start = (f32[2,96,1536]{2,1,0:T(8,128)S(1)}, f32[2,96,1536]{2,1,0:T(8,128)S(1)}, u32[]{:S(2)}, u32[]{:S(2)}) collective-permute-start(f32[2,96,1536]{2,1,0:T(8,128)S(1)} %pick.1), channel_id=1, source_target_pairs={{0,32},{32,0},{1,33},{33,1},{2,34},{34,2},{3,35},{35,3},{4,36},{36... | collective-permute-start | bytes 3538952 | tf_op jit(solution)/shard_map/ppermute | solution.py:274
  7.1 5.2 %collective-permute-start.1 = (bf16[96,512]{1,0:T(8,128)(2,1)S(1)}, bf16[96,512]{1,0:T(8,128)(2,1)S(1)}, u32[]{:S(2)}, u32[]{:S(2)}) collective-permute-start(bf16[96,512]{1,0:T(8,128)(2,1)S(1)} %get-tuple-element.30), channel_id=1, source_target_pairs={{0,64},{64,0},{1,65},{65,1},{2,66},{66,2},{3,67},{67,3},{4,68},{68... | collective-permute-start | bytes 294920 | tf_op jit(solution)/shard_map/ppermute | solution.py:278
  10.4 61.0 %collective-permute-start.5 = (bf16[512,3072]{1,0:T(8,128)(2,1)S(1)}, bf16[512,3072]{1,0:T(8,128)(2,1)S(1)}, u32[]{:S(2)}, u32[]{:S(2)}) collective-permute-start(bf16[512,3072]{1,0:T(8,128)(2,1)S(1)} %fusion.2.refs_1_), channel_id=1, source_target_pairs={{0,32},{32,0},{1,33},{33,1},{2,34},{34,2},{3,35},{35,3},{4,36},{36... | collective-permute-start | bytes 9437192 | tf_op jit(solution)/shard_map/ppermute | solution.py:293
  12.3 4.7 %collective-permute-start.20 = (bf16[1,96,512]{2,1,0:T(8,128)(2,1)S(1)}, bf16[1,96,512]{2,1,0:T(8,128)(2,1)S(1)}, u32[]{:S(2)}, u32[]{:S(2)}) collective-permute-start(bf16[1,96,512]{2,1,0:T(8,128)(2,1)S(1)} %get-tuple-element.55), channel_id=1, source_target_pairs={{0,2},{2,0},{4,6},{6,4},{32,38},{34,36},{36,34},{38,32},{1,3},{3,1... | collective-permute-start | bytes 294920 | tf_op jit(solution)/shard_map/ppermute | solution.py:32
  13.9 6.0 %collective-permute-start.2 = (bf16[96,512]{1,0:T(8,128)(2,1)S(1)}, bf16[96,512]{1,0:T(8,128)(2,1)S(1)}, u32[]{:S(2)}, u32[]{:S(2)}) collective-permute-start(bf16[96,512]{1,0:T(8,128)(2,1)S(1)} %get-tuple-element.31), channel_id=1, source_target_pairs={{0,64},{64,0},{1,65},{65,1},{2,66},{66,2},{3,67},{67,3},{4,68},{68... | collective-permute-start | bytes 294920 | tf_op jit(solution)/shard_map/ppermute | solution.py:278
  15.7 10.0 %collective-permute-start.3 = (bf16[96,512]{1,0:T(8,128)(2,1)S(1)}, bf16[96,512]{1,0:T(8,128)(2,1)S(1)}, u32[]{:S(2)}, u32[]{:S(2)}) collective-permute-start(bf16[96,512]{1,0:T(8,128)(2,1)S(1)} %get-tuple-element.32), channel_id=1, source_target_pairs={{0,64},{64,0},{1,65},{65,1},{2,66},{66,2},{3,67},{67,3},{4,68},{68... | collective-permute-start | bytes 294920 | tf_op jit(solution)/shard_map/ppermute | solution.py:278
  17.0 7.0 %collective-permute-start.21 = (bf16[2,96,512]{2,1,0:T(8,128)(2,1)S(1)}, bf16[2,96,512]{2,1,0:T(8,128)(2,1)S(1)}, u32[]{:S(2)}, u32[]{:S(2)}) collective-permute-start(bf16[2,96,512]{2,1,0:T(8,128)(2,1)S(1)} %pad_maximum_fusion.8), channel_id=1, source_target_pairs={{0,6},{2,4},{4,2},{6,0},{32,34},{34,32},{36,38},{38,36},{1,7},{3,5... | collective-permute-start | bytes 589832 | tf_op jit(solution)/shard_map/ppermute | solution.py:32
  19.9 7.6 %collective-permute-start.13 = (bf16[1,96,512]{2,1,0:T(8,128)(2,1)S(1)}, bf16[1,96,512]{2,1,0:T(8,128)(2,1)S(1)}, u32[]{:S(2)}, u32[]{:S(2)}) collective-permute-start(bf16[1,96,512]{2,1,0:T(8,128)(2,1)S(1)} %get-tuple-element.57), channel_id=1, source_target_pairs={{0,8},{8,0},{16,24},{24,16},{32,56},{40,48},{48,40},{56,32},{1,9},... | collective-permute-start | bytes 294920 | tf_op jit(solution)/shard_map/ppermute | solution.py:32
  24.0 10.4 %collective-permute-start.22 = (bf16[4,96,512]{2,1,0:T(8,128)(2,1)S(1)}, bf16[4,96,512]{2,1,0:T(8,128)(2,1)S(1)}, u32[]{:S(2)}, u32[]{:S(2)}) collective-permute-start(bf16[4,96,512]{2,1,0:T(8,128)(2,1)S(1)} %pad_maximum_fusion.5), channel_id=1, source_target_pairs={{0,8},{8,0},{16,24},{24,16},{32,56},{40,48},{48,40},{56,32},{1,9},... | collective-permute-start | bytes 1179656 | tf_op jit(solution)/shard_map/ppermute | solution.py:32
  25.7 4.7 %collective-permute-start.6 = (bf16[1,96,512]{2,1,0:T(8,128)(2,1)S(1)}, bf16[1,96,512]{2,1,0:T(8,128)(2,1)S(1)}, u32[]{:S(2)}, u32[]{:S(2)}) collective-permute-start(bf16[1,96,512]{2,1,0:T(8,128)(2,1)S(1)} %get-tuple-element.59), channel_id=1, source_target_pairs={{0,64},{1,65},{32,97},{33,96},{64,0},{65,1},{96,33},{97,32},{2,66}... | collective-permute-start | bytes 294920 | tf_op jit(solution)/shard_map/ppermute | solution.py:32
  27.6 11.5 %collective-permute-start.14 = (bf16[2,96,512]{2,1,0:T(8,128)(2,1)S(1)}, bf16[2,96,512]{2,1,0:T(8,128)(2,1)S(1)}, u32[]{:S(2)}, u32[]{:S(2)}) collective-permute-start(bf16[2,96,512]{2,1,0:T(8,128)(2,1)S(1)} %pad_maximum_fusion.7), channel_id=1, source_target_pairs={{0,24},{8,16},{16,8},{24,0},{32,40},{40,32},{48,56},{56,48},{1,25}... | collective-permute-start | bytes 589832 | tf_op jit(solution)/shard_map/ppermute | solution.py:32
  30.5 9.2 %collective-permute-start.7 = (bf16[2,96,512]{2,1,0:T(8,128)(2,1)S(1)}, bf16[2,96,512]{2,1,0:T(8,128)(2,1)S(1)}, u32[]{:S(2)}, u32[]{:S(2)}) collective-permute-start(bf16[2,96,512]{2,1,0:T(8,128)(2,1)S(1)} %pad_maximum_fusion.6), channel_id=1, source_target_pairs={{0,65},{1,64},{32,96},{33,97},{64,1},{65,0},{96,32},{97,33},{2,67}... | collective-permute-start | bytes 589832 | tf_op jit(solution)/shard_map/ppermute | solution.py:32
  34.5 18.2 %collective-permute-start.23 = (bf16[8,96,512]{2,1,0:T(8,128)(2,1)S(1)}, bf16[8,96,512]{2,1,0:T(8,128)(2,1)S(1)}, u32[]{:S(2)}, u32[]{:S(2)}) collective-permute-start(bf16[8,96,512]{2,1,0:T(8,128)(2,1)S(1)} %pad_maximum_fusion.2), channel_id=1, source_target_pairs={{0,24},{8,16},{16,8},{24,0},{32,40},{40,32},{48,56},{56,48},{1,25}... | collective-permute-start | bytes 2359304 | tf_op jit(solution)/shard_map/ppermute | solution.py:32
  39.2 9.7 %collective-permute-start.15 = (bf16[4,96,512]{2,1,0:T(8,128)(2,1)S(1)}, bf16[4,96,512]{2,1,0:T(8,128)(2,1)S(1)}, u32[]{:S(2)}, u32[]{:S(2)}) collective-permute-start(bf16[4,96,512]{2,1,0:T(8,128)(2,1)S(1)} %pad_maximum_fusion.4), channel_id=1, source_target_pairs={{0,64},{1,65},{32,97},{33,96},{64,0},{65,1},{96,33},{97,32},{2,66}... | collective-permute-start | bytes 1179656 | tf_op jit(solution)/shard_map/ppermute | solution.py:32
  39.7 9.8 %collective-permute-start.8 = (bf16[4,96,512]{2,1,0:T(8,128)(2,1)S(1)}, bf16[4,96,512]{2,1,0:T(8,128)(2,1)S(1)}, u32[]{:S(2)}, u32[]{:S(2)}) collective-permute-start(bf16[4,96,512]{2,1,0:T(8,128)(2,1)S(1)} %pad_maximum_fusion.3), channel_id=1, source_target_pairs={{0,2},{2,0},{4,6},{6,4},{32,38},{34,36},{36,34},{38,32},{1,3},{3,1... | collective-permute-start | bytes 1179656 | tf_op jit(solution)/shard_map/ppermute | solution.py:32
  49.0 21.7 %collective-permute-start.16 = (bf16[8,96,512]{2,1,0:T(8,128)(2,1)S(1)}, bf16[8,96,512]{2,1,0:T(8,128)(2,1)S(1)}, u32[]{:S(2)}, u32[]{:S(2)}) collective-permute-start(bf16[8,96,512]{2,1,0:T(8,128)(2,1)S(1)} %pad_maximum_fusion.1), channel_id=1, source_target_pairs={{0,65},{1,64},{32,96},{33,97},{64,1},{65,0},{96,32},{97,33},{2,67}... | collective-permute-start | bytes 2359304 | tf_op jit(solution)/shard_map/ppermute | solution.py:32
  49.6 21.6 %collective-permute-start.9 = (bf16[8,96,512]{2,1,0:T(8,128)(2,1)S(1)}, bf16[8,96,512]{2,1,0:T(8,128)(2,1)S(1)}, u32[]{:S(2)}, u32[]{:S(2)}) collective-permute-start(bf16[8,96,512]{2,1,0:T(8,128)(2,1)S(1)} %pad_maximum_fusion), channel_id=1, source_target_pairs={{0,6},{2,4},{4,2},{6,0},{32,34},{34,32},{36,38},{38,36},{1,7},{3,5... | collective-permute-start | bytes 2359304 | tf_op jit(solution)/shard_map/ppermute | solution.py:32
  52.7 36.4 %collective-permute-start.24 = (bf16[16,96,512]{2,1,0:T(8,128)(2,1)S(1)}, bf16[16,96,512]{2,1,0:T(8,128)(2,1)S(1)}, u32[]{:S(2)}, u32[]{:S(2)}) collective-permute-start(bf16[16,96,512]{2,1,0:T(8,128)(2,1)S(1)} %constant_dynamic-update-slice_fusion.10.refs_4_.refs_7_.refs_5_), channel_id=1, source_target_pairs={{0,64},{1,65},{32,97},{33,96},{64,0},{65,1},{96,33},{97,32},{2,66}... | collective-permute-start | bytes 4718600 | tf_op jit(solution)/shard_map/ppermute | solution.py:32
  54.2 37.9 %collective-permute-start.25 = (bf16[16,96,512]{2,1,0:T(8,128)(2,1)S(1)}, bf16[16,96,512]{2,1,0:T(8,128)(2,1)S(1)}, u32[]{:S(2)}, u32[]{:S(2)}) collective-permute-start(bf16[16,96,512]{2,1,0:T(8,128)(2,1)S(1)} %constant_dynamic-update-slice_fusion.10.refs_4_.refs_7_.refs_5_), channel_id=1, source_target_pairs={{0,65},{1,64},{32,96},{33,97},{64,1},{65,0},{96,32},{97,33},{2,67}... | collective-permute-start | bytes 4718600 | tf_op jit(solution)/shard_map/ppermute | solution.py:32
  70.7 39.0 %copy-start.5 = (f32[128]{0:T(128)S(1)}, f32[128]{0:T(128)}, u32[]{:S(2)}) copy-start(f32[128]{0:T(128)} %param.11) | copy-start | bytes 1540
  70.7 39.0 %copy-start.6 = (f32[128]{0:T(128)S(1)}, f32[128]{0:T(128)}, u32[]{:S(2)}) copy-start(f32[128]{0:T(128)} %param.10) | copy-start | bytes 1540
  70.7 30.5 %collective-permute-start.17 = (bf16[16,96,512]{2,1,0:T(8,128)(2,1)S(1)}, bf16[16,96,512]{2,1,0:T(8,128)(2,1)S(1)}, u32[]{:S(2)}, u32[]{:S(2)}) collective-permute-start(bf16[16,96,512]{2,1,0:T(8,128)(2,1)S(1)} %constant_dynamic-update-slice_fusion.5.refs_4_.refs_7_.refs_5_), channel_id=1, source_target_pairs={{0,2},{2,0},{4,6},{6,4},{32,38},{34,36},{36,34},{38,32},{1,3},{3,1... | collective-permute-start | bytes 4718600 | tf_op jit(solution)/shard_map/ppermute | solution.py:32
  71.3 33.3 %collective-permute-start.10 = (bf16[16,96,512]{2,1,0:T(8,128)(2,1)S(1)}, bf16[16,96,512]{2,1,0:T(8,128)(2,1)S(1)}, u32[]{:S(2)}, u32[]{:S(2)}) collective-permute-start(bf16[16,96,512]{2,1,0:T(8,128)(2,1)S(1)} %constant_dynamic-update-slice_fusion.refs_4_.refs_7_.refs_5_), channel_id=1, source_target_pairs={{0,8},{8,0},{16,24},{24,16},{32,56},{40,48},{48,40},{56,32},{1,9},... | collective-permute-start | bytes 4718600 | tf_op jit(solution)/shard_map/ppermute | solution.py:32
  71.4 42.9 %collective-permute-start.18 = (bf16[16,96,512]{2,1,0:T(8,128)(2,1)S(1)}, bf16[16,96,512]{2,1,0:T(8,128)(2,1)S(1)}, u32[]{:S(2)}, u32[]{:S(2)}) collective-permute-start(bf16[16,96,512]{2,1,0:T(8,128)(2,1)S(1)} %constant_dynamic-update-slice_fusion.5.refs_4_.refs_7_.refs_5_), channel_id=1, source_target_pairs={{0,6},{2,4},{4,2},{6,0},{32,34},{34,32},{36,38},{38,36},{1,7},{3,5... | collective-permute-start | bytes 4718600 | tf_op jit(solution)/shard_map/ppermute | solution.py:32
  89.1 29.4 %collective-permute-start.11 = (bf16[16,96,512]{2,1,0:T(8,128)(2,1)S(1)}, bf16[16,96,512]{2,1,0:T(8,128)(2,1)S(1)}, u32[]{:S(2)}, u32[]{:S(2)}) collective-permute-start(bf16[16,96,512]{2,1,0:T(8,128)(2,1)S(1)} %constant_dynamic-update-slice_fusion.refs_4_.refs_7_.refs_5_), channel_id=1, source_target_pairs={{0,24},{8,16},{16,8},{24,0},{32,40},{40,32},{48,56},{56,48},{1,25}... | collective-permute-start | bytes 4718600 | tf_op jit(solution)/shard_map/ppermute | solution.py:32
  92.1 30.8 %collective-permute-start.26 = (bf16[16,96,512]{2,1,0:T(8,128)(2,1)S(1)}, bf16[16,96,512]{2,1,0:T(8,128)(2,1)S(1)}, u32[]{:S(2)}, u32[]{:S(2)}) collective-permute-start(bf16[16,96,512]{2,1,0:T(8,128)(2,1)S(1)} %collective-permute-done.24.refs_5_.refs_6_), channel_id=1, source_target_pairs={{0,65},{1,64},{32,96},{33,97},{64,1},{65,0},{96,32},{97,33},{2,67}... | collective-permute-start | bytes 4718600 | tf_op jit(solution)/shard_map/ppermute | solution.py:32
  101.3 28.2 %collective-permute-start.19 = (bf16[16,96,512]{2,1,0:T(8,128)(2,1)S(1)}, bf16[16,96,512]{2,1,0:T(8,128)(2,1)S(1)}, u32[]{:S(2)}, u32[]{:S(2)}) collective-permute-start(bf16[16,96,512]{2,1,0:T(8,128)(2,1)S(1)} %collective-permute-done.17.refs_5_.refs_6_), channel_id=1, source_target_pairs={{0,6},{2,4},{4,2},{6,0},{32,34},{34,32},{36,38},{38,36},{1,7},{3,5... | collective-permute-start | bytes 4718600 | tf_op jit(solution)/shard_map/ppermute | solution.py:32
  104.6 30.9 %collective-permute-start.12 = (bf16[16,96,512]{2,1,0:T(8,128)(2,1)S(1)}, bf16[16,96,512]{2,1,0:T(8,128)(2,1)S(1)}, u32[]{:S(2)}, u32[]{:S(2)}) collective-permute-start(bf16[16,96,512]{2,1,0:T(8,128)(2,1)S(1)} %collective-permute-done.10.refs_5_.refs_6_), channel_id=1, source_target_pairs={{0,24},{8,16},{16,8},{24,0},{32,40},{40,32},{48,56},{56,48},{1,25}... | collective-permute-start | bytes 4718600 | tf_op jit(solution)/shard_map/ppermute | solution.py:32
  129.4 22.1 %collective-permute-start.29 = (bf16[2,512,512]{2,1,0:T(8,128)(2,1)S(1)}, bf16[2,512,512]{2,1,0:T(8,128)(2,1)S(1)}, u32[]{:S(2)}, u32[]{:S(2)}) collective-permute-start(bf16[2,512,512]{2,1,0:T(8,128)(2,1)S(1)} %get-tuple-element.45), channel_id=1, source_target_pairs={{0,32},{32,0},{1,33},{33,1},{2,34},{34,2},{3,35},{35,3},{4,36},{36... | collective-permute-start | bytes 3145736 | tf_op jit(solution)/shard_map/ppermute | solution.py:310
  135.0 18.3 %collective-permute-start.28 = (bf16[2,512,512]{2,1,0:T(8,128)(2,1)S(1)}, bf16[2,512,512]{2,1,0:T(8,128)(2,1)S(1)}, u32[]{:S(2)}, u32[]{:S(2)}) collective-permute-start(bf16[2,512,512]{2,1,0:T(8,128)(2,1)S(1)} %get-tuple-element.44), channel_id=1, source_target_pairs={{0,32},{32,0},{1,33},{33,1},{2,34},{34,2},{3,35},{35,3},{4,36},{36... | collective-permute-start | bytes 3145736 | tf_op jit(solution)/shard_map/ppermute | solution.py:310
  140.9 13.9 %collective-permute-start.27 = (bf16[2,512,512]{2,1,0:T(8,128)(2,1)S(1)}, bf16[2,512,512]{2,1,0:T(8,128)(2,1)S(1)}, u32[]{:S(2)}, u32[]{:S(2)}) collective-permute-start(bf16[2,512,512]{2,1,0:T(8,128)(2,1)S(1)} %get-tuple-element.43), channel_id=1, source_target_pairs={{0,32},{32,0},{1,33},{33,1},{2,34},{34,2},{3,35},{35,3},{4,36},{36... | collective-permute-start | bytes 3145736 | tf_op jit(solution)/shard_map/ppermute | solution.py:310
  141.0 9.4 %collective-permute-start.4 = (bf16[96,1536]{1,0:T(8,128)(2,1)S(1)}, bf16[96,1536]{1,0:T(8,128)(2,1)S(1)}, u32[]{:S(2)}, u32[]{:S(2)}) collective-permute-start(bf16[96,1536]{1,0:T(8,128)(2,1)S(1)} %get-tuple-element.33), channel_id=1, source_target_pairs={{0,64},{64,0},{1,65},{65,1},{2,66},{66,2},{3,67},{67,3},{4,68},{68... | collective-permute-start | bytes 884744 | tf_op jit(solution)/shard_map/ppermute | solution.py:279
  (5 other events, 25.6 us)

commit v4 on v3

--- a/solution.py
+++ b/solution.py
@@ -124,14 +124,7 @@
                 mine = jnp.concatenate([head_norm(y[:, h : h + HEAD], gain) for h in range(0, n, HEAD)], axis=1)
                 early = begun[t, span, :]
                 for i, out in enumerate(outs):
-
-                    @pl.when(where[1] == i)
-                    def _():
-                        out[span, :] = mine
-
-                    @pl.when(where[1] != i)
-                    def _():
-                        out[span, :] = early
+                    out[span, :] = jnp.where(where[1] == i, mine, early)
             else:
                 y = (y + begun[t, span, :]) * scale
                 for i, out in enumerate(outs):
@@ -180,28 +173,33 @@
     )(where, *operands)
 
 
-def put_body(where, got, q_in, k_in, q_out, k_out):
-    q_out[...] = got[0]
-    k_out[...] = got[1]
+def put_body(n_got, where, *refs):
+    q_out, k_out = refs[n_got + 2 :]
+    for i in range(n_got):
+
+        @pl.when(pl.program_id(0) == i)
+        def _():
+            q_out[...] = refs[i][0]
+            k_out[...] = refs[i][1]
 
 
 def put(color, where, got, query, key_out):
-    _, half, n = got.shape
-    col = lambda i, where: (i, (1 - where[0]) * COLORS + color)
+    _, half, n = got[0].shape
+    col = lambda i, where: (0, (1 - where[0]) * COLORS + color + i)
     any_spec = pl.BlockSpec(memory_space=pl.ANY)
     return pl.pallas_call(
-        put_body,
+        lambda *refs: put_body(len(got), *refs),
         grid_spec=pltpu.PrefetchScalarGridSpec(
             num_scalar_prefetch=1,
-            grid=(2,),
-            in_specs=[pl.BlockSpec((2, half // 2, n), lambda i, *_: (0, i, 0)), any_spec, any_spec],
-            out_specs=[pl.BlockSpec((half // 2, n), col)] * 2,
+            grid=(len(got),),
+            in_specs=[pl.BlockSpec((2, half, n), lambda *_: (0, 0, 0))] * len(got) + [any_spec, any_spec],
+            out_specs=[pl.BlockSpec((half, n), col)] * 2,
         ),
         out_shape=[jax.ShapeDtypeStruct(query.shape, query.dtype)] * 2,
-        input_output_aliases={2: 0, 3: 1},
-        compiler_params=pltpu.CompilerParams(vmem_limit_bytes=8 * 2**20),
-        cost_estimate=pl.CostEstimate(flops=10**9, bytes_accessed=8 * got.size, transcendentals=0),
-    )(where, got, query, key_out)
+        input_output_aliases={1 + len(got): 0, 2 + len(got): 1},
+        compiler_params=pltpu.CompilerParams(vmem_limit_bytes=12 * 2**20),
+        cost_estimate=pl.CostEstimate(flops=10**9, bytes_accessed=8 * len(got) * got[0].size, transcendentals=0),
+    )(where, *got, query, key_out)
 
 
 def pick_body(core, local, out):
@@ -305,12 +303,12 @@
         units.append([copied[k], one, two, three])
         begun += project_half(k, 0, where, normed, other, gains, [copied[k], one, two, copied[k]])
     outputs, back = (), []
-    for k in range(COLORS):
+    for k in (1, 2, 0):
         *outputs, send = project_half(k, 1, where, normed, other, gains, units[k], begun[k], outputs)
         back.append(lax.ppermute(send, "core", swap))
     where, student_new, teacher_new = lax.optimization_barrier((where, student_new, teacher_new))
-    for k in range(COLORS):
-        outputs = put(k, where, back[k], *outputs)
+    outputs = put(1, where, back[:2], *outputs)
+    outputs = put(0, where, back[2:], *outputs)
     return (teacher_new, student_new, *outputs)
 
 

time: 159 us -> 164 us (1.031)
  the two profiles are of different devices: /device:TPU:0 before, /device:TPU:30 now
where the time goes in v4:
time: 164 us
  waiting for transfers between devices  102 us (62%)
  Pallas kernels  35 us (21%)
  starting transfers between devices  18.8 us (11%)
  other arithmetic  3.78 us (2%)
  local copies, waits for them, and re-layouts  3.03 us (2%)
    ppermute x21, waiting for transfers between devices, exchange(): return lax.ppermute(x, axes, pairs)  86.5 us
    pallas_call x6, Pallas kernels, project_half(): pl.pallas_call(body, grid_spec=pltpu.PrefetchScalarGridSpec(num_scalar_pr...  29.7 us
    ppermute x21, starting transfers between devices, exchange(): return lax.ppermute(x, axes, pairs)  14.1 us
    ppermute x1, waiting for transfers between devices, shards(): rest = lax.ppermute(rest, 'zlo', swap).astype(jnp.float32)  9.34 us
    ppermute x3, waiting for transfers between devices, shards(): arrived.append(lax.ppermute(give[k], 'zlo', swap).astype(jnp.float32))  4.96 us
    ppermute x3, starting transfers between devices, shards(): arrived.append(lax.ppermute(give[k], 'zlo', swap).astype(jnp.float32))  4 us
    pallas_call x2, Pallas kernels, put(): pl.pallas_call(lambda *refs: put_body(len(got), *refs), grid_spec=pltpu.P...  3.55 us
  transfers between devices with their start and end apart: 30, of which 16 were waited for; matrix products, arithmetic and copies ran while one was open for 2% of the time, Pallas kernels for 19%

profile of v4, /device:TPU:30, one launch (start us, length us, event | category | flops | bytes accessed | tf_op | source)
XLA Modules:
  0.0 163.6 jit_solution(10359386104633058861)
XLA Ops:
  0.7 1.7 %copy-done = f32[1,96,6144]{2,1,0:T(8,128)S(1)} copy-done((f32[1,96,6144]{2,1,0:T(8,128)S(1)}, f32[1,96,6144]{2,1,0:T(8,128)}, u32[]{:S(2)}) %copy-start) | copy-done | bytes 2359320
  5.0 1.1 collective-permute-done.refs_2_
  7.1 2.0 %collective-permute-start.1 = (bf16[96,512]{1,0:T(8,128)(2,1)S(1)}, bf16[96,512]{1,0:T(8,128)(2,1)S(1)}, u32[]{:S(2)}, u32[]{:S(2)}) collective-permute-start(bf16[96,512]{1,0:T(8,128)(2,1)S(1)} %get-tuple-element.28), channel_id=1, source_target_pairs={{0,64},{64,0},{1,65},{65,1},{2,66},{66,2},{3,67},{67,3},{4,68},{68... | collective-permute-start | bytes 294920 | tf_op jit(solution)/shard_map/ppermute | solution.py:276
  9.3 3.4 %collective-permute-done.1 = bf16[96,512]{1,0:T(8,128)(2,1)S(1)} collective-permute-done((bf16[96,512]{1,0:T(8,128)(2,1)S(1)}, bf16[96,512]{1,0:T(8,128)(2,1)S(1)}, u32[]{:S(2)}, u32[]{:S(2)}) %collective-permute-start.1) | collective-permute-done | bytes 98336 | tf_op jit(solution)/shard_map/ppermute | solution.py:276
  12.8 1.5 collective-permute-done.2
  15.2 3.9 %collective-permute-done.20 = bf16[1,96,512]{2,1,0:T(8,128)(2,1)S(1)} collective-permute-done((bf16[1,96,512]{2,1,0:T(8,128)(2,1)S(1)}, bf16[1,96,512]{2,1,0:T(8,128)(2,1)S(1)}, u32[]{:S(2)}, u32[]{:S(2)}) %collective-permute-start.20) | collective-permute-done | bytes 98336 | tf_op jit(solution)/shard_map/ppermute | solution.py:32
  19.4 1.2 fusion.2.refs_1_
  20.7 1.8 %collective-permute-start.3 = (bf16[96,512]{1,0:T(8,128)(2,1)S(1)}, bf16[96,512]{1,0:T(8,128)(2,1)S(1)}, u32[]{:S(2)}, u32[]{:S(2)}) collective-permute-start(bf16[96,512]{1,0:T(8,128)(2,1)S(1)} %get-tuple-element.30), channel_id=1, source_target_pairs={{0,64},{64,0},{1,65},{65,1},{2,66},{66,2},{3,67},{67,3},{4,68},{68... | collective-permute-start | bytes 294920 | tf_op jit(solution)/shard_map/ppermute | solution.py:276
  22.5 3.5 %collective-permute-done.21 = bf16[2,96,512]{2,1,0:T(8,128)(2,1)S(1)} collective-permute-done((bf16[2,96,512]{2,1,0:T(8,128)(2,1)S(1)}, bf16[2,96,512]{2,1,0:T(8,128)(2,1)S(1)}, u32[]{:S(2)}, u32[]{:S(2)}) %collective-permute-start.21) | collective-permute-done | bytes 196640 | tf_op jit(solution)/shard_map/ppermute | solution.py:32
  26.1 1.8 %collective-permute-start.22 = (bf16[4,96,512]{2,1,0:T(8,128)(2,1)S(1)}, bf16[4,96,512]{2,1,0:T(8,128)(2,1)S(1)}, u32[]{:S(2)}, u32[]{:S(2)}) collective-permute-start(bf16[4,96,512]{2,1,0:T(8,128)(2,1)S(1)} %pad_maximum_fusion.5), channel_id=1, source_target_pairs={{0,64},{1,65},{32,97},{33,96},{64,0},{65,1},{96,33},{97,32},{2,66}... | collective-permute-start | bytes 1179656 | tf_op jit(solution)/shard_map/ppermute | solution.py:32
  29.1 5.9 %collective-permute-done.13 = bf16[1,96,512]{2,1,0:T(8,128)(2,1)S(1)} collective-permute-done((bf16[1,96,512]{2,1,0:T(8,128)(2,1)S(1)}, bf16[1,96,512]{2,1,0:T(8,128)(2,1)S(1)}, u32[]{:S(2)}, u32[]{:S(2)}) %collective-permute-start.13) | collective-permute-done | bytes 98336 | tf_op jit(solution)/shard_map/ppermute | solution.py:32
  35.0 4.1 %collective-permute-start.14 = (bf16[2,96,512]{2,1,0:T(8,128)(2,1)S(1)}, bf16[2,96,512]{2,1,0:T(8,128)(2,1)S(1)}, u32[]{:S(2)}, u32[]{:S(2)}) collective-permute-start(bf16[2,96,512]{2,1,0:T(8,128)(2,1)S(1)} %pad_maximum_fusion.7), channel_id=1, source_target_pairs={{0,65},{1,64},{32,96},{33,97},{64,1},{65,0},{96,32},{97,33},{2,67}... | collective-permute-start | bytes 589832 | tf_op jit(solution)/shard_map/ppermute | solution.py:32
  40.0 2.9 %collective-permute-done.14 = bf16[2,96,512]{2,1,0:T(8,128)(2,1)S(1)} collective-permute-done((bf16[2,96,512]{2,1,0:T(8,128)(2,1)S(1)}, bf16[2,96,512]{2,1,0:T(8,128)(2,1)S(1)}, u32[]{:S(2)}, u32[]{:S(2)}) %collective-permute-start.14) | collective-permute-done | bytes 196640 | tf_op jit(solution)/shard_map/ppermute | solution.py:32
  43.8 4.0 %collective-permute-done.7 = bf16[2,96,512]{2,1,0:T(8,128)(2,1)S(1)} collective-permute-done((bf16[2,96,512]{2,1,0:T(8,128)(2,1)S(1)}, bf16[2,96,512]{2,1,0:T(8,128)(2,1)S(1)}, u32[]{:S(2)}, u32[]{:S(2)}) %collective-permute-start.7) | collective-permute-done | bytes 196640 | tf_op jit(solution)/shard_map/ppermute | solution.py:32
  48.0 3.3 %collective-permute-done.15 = bf16[4,96,512]{2,1,0:T(8,128)(2,1)S(1)} collective-permute-done((bf16[4,96,512]{2,1,0:T(8,128)(2,1)S(1)}, bf16[4,96,512]{2,1,0:T(8,128)(2,1)S(1)}, u32[]{:S(2)}, u32[]{:S(2)}) %collective-permute-start.15) | collective-permute-done | bytes 393248 | tf_op jit(solution)/shard_map/ppermute | solution.py:32
  52.2 7.7 %collective-permute-done.8 = bf16[4,96,512]{2,1,0:T(8,128)(2,1)S(1)} collective-permute-done((bf16[4,96,512]{2,1,0:T(8,128)(2,1)S(1)}, bf16[4,96,512]{2,1,0:T(8,128)(2,1)S(1)}, u32[]{:S(2)}, u32[]{:S(2)}) %collective-permute-start.8) | collective-permute-done | bytes 393248 | tf_op jit(solution)/shard_map/ppermute | solution.py:32
  60.9 12.1 %collective-permute-done.16 = bf16[8,96,512]{2,1,0:T(8,128)(2,1)S(1)} collective-permute-done((bf16[8,96,512]{2,1,0:T(8,128)(2,1)S(1)}, bf16[8,96,512]{2,1,0:T(8,128)(2,1)S(1)}, u32[]{:S(2)}, u32[]{:S(2)}) %collective-permute-start.16) | collective-permute-done | bytes 786464 | tf_op jit(solution)/shard_map/ppermute | solution.py:32
  73.3 8.4 %collective-permute-done.9 = bf16[8,96,512]{2,1,0:T(8,128)(2,1)S(1)} collective-permute-done((bf16[8,96,512]{2,1,0:T(8,128)(2,1)S(1)}, bf16[8,96,512]{2,1,0:T(8,128)(2,1)S(1)}, u32[]{:S(2)}, u32[]{:S(2)}) %collective-permute-start.9) | collective-permute-done | bytes 786464 | tf_op jit(solution)/shard_map/ppermute | solution.py:32
  82.2 12.6 %collective-permute-done.24.refs_5_.refs_6_ = bf16[16,96,512]{2,1,0:T(8,128)(2,1)S(1)} collective-permute-done((bf16[16,96,512]{2,1,0:T(8,128)(2,1)S(1)}, bf16[16,96,512]{2,1,0:T(8,128)(2,1)S(1)}, u32[]{:S(2)}, u32[]{:S(2)}) %collective-permute-start.24) | collective-permute-done | bytes 1572896 | tf_op jit(solution)/shard_map/ppermute | solution.py:32
  95.7 12.2 %collective-permute-done.17.refs_5_.refs_6_ = bf16[16,96,512]{2,1,0:T(8,128)(2,1)S(1)} collective-permute-done((bf16[16,96,512]{2,1,0:T(8,128)(2,1)S(1)}, bf16[16,96,512]{2,1,0:T(8,128)(2,1)S(1)}, u32[]{:S(2)}, u32[]{:S(2)}) %collective-permute-start.17) | collective-permute-done | bytes 1572896 | tf_op jit(solution)/shard_map/ppermute | solution.py:32
  107.9 1.2 collective-permute-start.19
  109.1 10.0 %collective-permute-done.10.refs_5_.refs_6_ = bf16[16,96,512]{2,1,0:T(8,128)(2,1)S(1)} collective-permute-done((bf16[16,96,512]{2,1,0:T(8,128)(2,1)S(1)}, bf16[16,96,512]{2,1,0:T(8,128)(2,1)S(1)}, u32[]{:S(2)}, u32[]{:S(2)}) %collective-permute-start.10) | collective-permute-done | bytes 1572896 | tf_op jit(solution)/shard_map/ppermute | solution.py:32
  119.1 4.4 %shard_map.95.refs_4_ = f32[2,512,1024]{2,1,0:T(8,128)S(1)} custom-call(s32[2]{0:T(128)S(1)} %pad_add_fusion.core.refs_0_, bf16[512,3072]{1,0:T(8,128)(2,1)S(1)} %fusion.2.refs_1_, bf16[512,3072]{1,0:T(8,128)(2,1)S(1)} %collective-permute-done.5.refs_2_, f32[2,128]{1,0:T(2,128)S(1)} %pad_maximum_fusion.9.refs_3_, ...), custom_call_target="tpu_custom_call" | custom-call | flops 3221225472 | bytes 12582912 | tf_op jit(solution)/shard_map/pallas_call | solution.py:156
  123.6 4.2 %shard_map.94.refs_4_ = f32[2,512,1024]{2,1,0:T(8,128)S(1)} custom-call(s32[2]{0:T(128)S(1)} %pad_add_fusion.core.refs_0_, bf16[512,3072]{1,0:T(8,128)(2,1)S(1)} %fusion.2.refs_1_, bf16[512,3072]{1,0:T(8,128)(2,1)S(1)} %collective-permute-done.5.refs_2_, f32[2,128]{1,0:T(2,128)S(1)} %pad_maximum_fusion.9.refs_3_, ...), custom_call_target="tpu_custom_call" | custom-call | flops 3221225472 | bytes 12582912 | tf_op jit(solution)/shard_map/pallas_call | solution.py:156
  127.8 4.5 %shard_map.93.refs_4_ = bf16[2,512,512]{2,1,0:T(8,128)(2,1)S(1)} custom-call(s32[2]{0:T(128)S(1)} %pad_add_fusion.core.refs_0_, bf16[512,3072]{1,0:T(8,128)(2,1)S(1)} %fusion.2.refs_1_, bf16[512,3072]{1,0:T(8,128)(2,1)S(1)} %collective-permute-done.5.refs_2_, f32[2,128]{1,0:T(2,128)S(1)} %pad_maximum_fusion.9.refs_3_, ...), custom_call_target="tpu_custom_call" | custom-call | flops 3221225472 | bytes 12582912 | tf_op jit(solution)/shard_map/pallas_call | solution.py:156
  132.3 5.5 %shard_map.96 = (bf16[512,3072]{1,0:T(8,128)(2,1)}, bf16[512,3072]{1,0:T(8,128)(2,1)}, bf16[2,512,512]{2,1,0:T(8,128)(2,1)S(1)}) custom-call(s32[2]{0:T(128)S(1)} %pad_add_fusion.core.refs_0_, bf16[512,3072]{1,0:T(8,128)(2,1)S(1)} %fusion.2.refs_1_, bf16[512,3072]{1,0:T(8,128)(2,1)S(1)} %collective-permute-done.5.refs_2_, ...), custom_call_target="tpu_custom_call" | custom-call | flops 3221225472 | bytes 12582912 | tf_op jit(solution)/shard_map/pallas_call | solution.py:156
  137.9 5.7 %shard_map.97 = (bf16[512,3072]{1,0:T(8,128)(2,1)}, bf16[512,3072]{1,0:T(8,128)(2,1)}, bf16[2,512,512]{2,1,0:T(8,128)(2,1)S(1)}) custom-call(s32[2]{0:T(128)S(1)} %pad_add_fusion.core.refs_0_, bf16[512,3072]{1,0:T(8,128)(2,1)S(1)} %fusion.2.refs_1_, ...), custom_call_target="tpu_custom_call", output_to_operand_aliasing={{0}: (9, {}), {1}: (10, {})} | custom-call | flops 3221225472 | bytes 12582912 | tf_op jit(solution)/shard_map/pallas_call | solution.py:156
  144.1 5.3 %shard_map.98 = (bf16[512,3072]{1,0:T(8,128)(2,1)}, bf16[512,3072]{1,0:T(8,128)(2,1)}, bf16[2,512,512]{2,1,0:T(8,128)(2,1)S(1)}) custom-call(s32[2]{0:T(128)S(1)} %pad_add_fusion.core.refs_0_, bf16[512,3072]{1,0:T(8,128)(2,1)S(1)} %fusion.2.refs_1_, ...), custom_call_target="tpu_custom_call", output_to_operand_aliasing={{0}: (9, {}), {1}: (10, {})} | custom-call | flops 3221225472 | bytes 12582912 | tf_op jit(solution)/shard_map/pallas_call | solution.py:156
  149.5 9.3 %collective-permute-done.4 = bf16[96,1536]{1,0:T(8,128)(2,1)S(1)} collective-permute-done((bf16[96,1536]{1,0:T(8,128)(2,1)S(1)}, bf16[96,1536]{1,0:T(8,128)(2,1)S(1)}, u32[]{:S(2)}, u32[]{:S(2)}) %collective-permute-start.4) | collective-permute-done | bytes 294944 | tf_op jit(solution)/shard_map/ppermute | solution.py:277
  158.8 1.2 multiply_add_fusion
  160.1 2.0 %shard_map.99 = (bf16[512,3072]{1,0:T(8,128)(2,1)}, bf16[512,3072]{1,0:T(8,128)(2,1)}) custom-call(s32[2]{0:T(128)S(1)} %pad_add_fusion.core.refs_0_, bf16[2,512,512]{2,1,0:T(8,128)(2,1)S(1)} %collective-permute-done.28.refs_1_, bf16[2,512,512]{2,1,0:T(8,128)(2,1)S(1)} %collective-permute-done.29.refs_2_, ...), custom_call_target="tpu_custom_call", output_to_operand_aliasing={{0}: (3, {}), {1}: (4, {})} | custom-call | flops 1000000000 | bytes 8388608 | tf_op jit(solution)/shard_map/pallas_call | solution.py:190
  162.0 1.6 shard_map.100
  (86 shorter events, 12.3 us)
Async XLA Ops:
  3.2 2.9 %collective-permute-start = (f32[2,96,1536]{2,1,0:T(8,128)S(1)}, f32[2,96,1536]{2,1,0:T(8,128)S(1)}, u32[]{:S(2)}, u32[]{:S(2)}) collective-permute-start(f32[2,96,1536]{2,1,0:T(8,128)S(1)} %pick.1), channel_id=1, source_target_pairs={{0,32},{32,0},{1,33},{33,1},{2,34},{34,2},{3,35},{35,3},{4,36},{36... | collective-permute-start | bytes 3538952 | tf_op jit(solution)/shard_map/ppermute | solution.py:272
  7.1 5.6 %collective-permute-start.1 = (bf16[96,512]{1,0:T(8,128)(2,1)S(1)}, bf16[96,512]{1,0:T(8,128)(2,1)S(1)}, u32[]{:S(2)}, u32[]{:S(2)}) collective-permute-start(bf16[96,512]{1,0:T(8,128)(2,1)S(1)} %get-tuple-element.28), channel_id=1, source_target_pairs={{0,64},{64,0},{1,65},{65,1},{2,66},{66,2},{3,67},{67,3},{4,68},{68... | collective-permute-start | bytes 294920 | tf_op jit(solution)/shard_map/ppermute | solution.py:276
  9.1 5.2 %collective-permute-start.2 = (bf16[96,512]{1,0:T(8,128)(2,1)S(1)}, bf16[96,512]{1,0:T(8,128)(2,1)S(1)}, u32[]{:S(2)}, u32[]{:S(2)}) collective-permute-start(bf16[96,512]{1,0:T(8,128)(2,1)S(1)} %get-tuple-element.29), channel_id=1, source_target_pairs={{0,64},{64,0},{1,65},{65,1},{2,66},{66,2},{3,67},{67,3},{4,68},{68... | collective-permute-start | bytes 294920 | tf_op jit(solution)/shard_map/ppermute | solution.py:276
  14.3 4.7 %collective-permute-start.20 = (bf16[1,96,512]{2,1,0:T(8,128)(2,1)S(1)}, bf16[1,96,512]{2,1,0:T(8,128)(2,1)S(1)}, u32[]{:S(2)}, u32[]{:S(2)}) collective-permute-start(bf16[1,96,512]{2,1,0:T(8,128)(2,1)S(1)} %get-tuple-element.51), channel_id=1, source_target_pairs={{0,8},{8,0},{16,24},{24,16},{32,56},{40,48},{48,40},{56,32},{1,9},... | collective-permute-start | bytes 294920 | tf_op jit(solution)/shard_map/ppermute | solution.py:32
  19.1 7.0 %collective-permute-start.21 = (bf16[2,96,512]{2,1,0:T(8,128)(2,1)S(1)}, bf16[2,96,512]{2,1,0:T(8,128)(2,1)S(1)}, u32[]{:S(2)}, u32[]{:S(2)}) collective-permute-start(bf16[2,96,512]{2,1,0:T(8,128)(2,1)S(1)} %pad_maximum_fusion.8), channel_id=1, source_target_pairs={{0,24},{8,16},{16,8},{24,0},{32,40},{40,32},{48,56},{56,48},{1,25}... | collective-permute-start | bytes 589832 | tf_op jit(solution)/shard_map/ppermute | solution.py:32
  20.6 61.6 %collective-permute-start.5 = (bf16[512,3072]{1,0:T(8,128)(2,1)S(1)}, bf16[512,3072]{1,0:T(8,128)(2,1)S(1)}, u32[]{:S(2)}, u32[]{:S(2)}) collective-permute-start(bf16[512,3072]{1,0:T(8,128)(2,1)S(1)} %fusion.2.refs_1_), channel_id=1, source_target_pairs={{0,32},{32,0},{1,33},{33,1},{2,34},{34,2},{3,35},{35,3},{4,36},{36... | collective-permute-start | bytes 9437192 | tf_op jit(solution)/shard_map/ppermute | solution.py:291
  20.7 7.2 %collective-permute-start.3 = (bf16[96,512]{1,0:T(8,128)(2,1)S(1)}, bf16[96,512]{1,0:T(8,128)(2,1)S(1)}, u32[]{:S(2)}, u32[]{:S(2)}) collective-permute-start(bf16[96,512]{1,0:T(8,128)(2,1)S(1)} %get-tuple-element.30), channel_id=1, source_target_pairs={{0,64},{64,0},{1,65},{65,1},{2,66},{66,2},{3,67},{67,3},{4,68},{68... | collective-permute-start | bytes 294920 | tf_op jit(solution)/shard_map/ppermute | solution.py:276
  26.1 13.7 %collective-permute-start.22 = (bf16[4,96,512]{2,1,0:T(8,128)(2,1)S(1)}, bf16[4,96,512]{2,1,0:T(8,128)(2,1)S(1)}, u32[]{:S(2)}, u32[]{:S(2)}) collective-permute-start(bf16[4,96,512]{2,1,0:T(8,128)(2,1)S(1)} %pad_maximum_fusion.5), channel_id=1, source_target_pairs={{0,64},{1,65},{32,97},{33,96},{64,0},{65,1},{96,33},{97,32},{2,66}... | collective-permute-start | bytes 1179656 | tf_op jit(solution)/shard_map/ppermute | solution.py:32
  27.9 7.1 %collective-permute-start.13 = (bf16[1,96,512]{2,1,0:T(8,128)(2,1)S(1)}, bf16[1,96,512]{2,1,0:T(8,128)(2,1)S(1)}, u32[]{:S(2)}, u32[]{:S(2)}) collective-permute-start(bf16[1,96,512]{2,1,0:T(8,128)(2,1)S(1)} %get-tuple-element.53), channel_id=1, source_target_pairs={{0,64},{1,65},{32,97},{33,96},{64,0},{65,1},{96,33},{97,32},{2,66}... | collective-permute-start | bytes 294920 | tf_op jit(solution)/shard_map/ppermute | solution.py:32
  28.3 10.9 %collective-permute-start.6 = (bf16[1,96,512]{2,1,0:T(8,128)(2,1)S(1)}, bf16[1,96,512]{2,1,0:T(8,128)(2,1)S(1)}, u32[]{:S(2)}, u32[]{:S(2)}) collective-permute-start(bf16[1,96,512]{2,1,0:T(8,128)(2,1)S(1)} %get-tuple-element.55), channel_id=1, source_target_pairs={{0,2},{2,0},{4,6},{6,4},{32,38},{34,36},{36,34},{38,32},{1,3},{3,1... | collective-permute-start | bytes 294920 | tf_op jit(solution)/shard_map/ppermute | solution.py:32
  35.0 7.8 %collective-permute-start.14 = (bf16[2,96,512]{2,1,0:T(8,128)(2,1)S(1)}, bf16[2,96,512]{2,1,0:T(8,128)(2,1)S(1)}, u32[]{:S(2)}, u32[]{:S(2)}) collective-permute-start(bf16[2,96,512]{2,1,0:T(8,128)(2,1)S(1)} %pad_maximum_fusion.7), channel_id=1, source_target_pairs={{0,65},{1,64},{32,96},{33,97},{64,1},{65,0},{96,32},{97,33},{2,67}... | collective-permute-start | bytes 589832 | tf_op jit(solution)/shard_map/ppermute | solution.py:32
  39.2 8.6 %collective-permute-start.7 = (bf16[2,96,512]{2,1,0:T(8,128)(2,1)S(1)}, bf16[2,96,512]{2,1,0:T(8,128)(2,1)S(1)}, u32[]{:S(2)}, u32[]{:S(2)}) collective-permute-start(bf16[2,96,512]{2,1,0:T(8,128)(2,1)S(1)} %pad_maximum_fusion.6), channel_id=1, source_target_pairs={{0,6},{2,4},{4,2},{6,0},{32,34},{34,32},{36,38},{38,36},{1,7},{3,5... | collective-permute-start | bytes 589832 | tf_op jit(solution)/shard_map/ppermute | solution.py:32
  39.9 20.3 %collective-permute-start.23 = (bf16[8,96,512]{2,1,0:T(8,128)(2,1)S(1)}, bf16[8,96,512]{2,1,0:T(8,128)(2,1)S(1)}, u32[]{:S(2)}, u32[]{:S(2)}) collective-permute-start(bf16[8,96,512]{2,1,0:T(8,128)(2,1)S(1)} %pad_maximum_fusion.2), channel_id=1, source_target_pairs={{0,65},{1,64},{32,96},{33,97},{64,1},{65,0},{96,32},{97,33},{2,67}... | collective-permute-start | bytes 2359304 | tf_op jit(solution)/shard_map/ppermute | solution.py:32
  42.9 8.4 %collective-permute-start.15 = (bf16[4,96,512]{2,1,0:T(8,128)(2,1)S(1)}, bf16[4,96,512]{2,1,0:T(8,128)(2,1)S(1)}, u32[]{:S(2)}, u32[]{:S(2)}) collective-permute-start(bf16[4,96,512]{2,1,0:T(8,128)(2,1)S(1)} %pad_maximum_fusion.4), channel_id=1, source_target_pairs={{0,2},{2,0},{4,6},{6,4},{32,38},{34,36},{36,34},{38,32},{1,3},{3,1... | collective-permute-start | bytes 1179656 | tf_op jit(solution)/shard_map/ppermute | solution.py:32
  47.8 12.1 %collective-permute-start.8 = (bf16[4,96,512]{2,1,0:T(8,128)(2,1)S(1)}, bf16[4,96,512]{2,1,0:T(8,128)(2,1)S(1)}, u32[]{:S(2)}, u32[]{:S(2)}) collective-permute-start(bf16[4,96,512]{2,1,0:T(8,128)(2,1)S(1)} %pad_maximum_fusion.3), channel_id=1, source_target_pairs={{0,8},{8,0},{16,24},{24,16},{32,56},{40,48},{48,40},{56,32},{1,9},... | collective-permute-start | bytes 1179656 | tf_op jit(solution)/shard_map/ppermute | solution.py:32
  51.4 21.7 %collective-permute-start.16 = (bf16[8,96,512]{2,1,0:T(8,128)(2,1)S(1)}, bf16[8,96,512]{2,1,0:T(8,128)(2,1)S(1)}, u32[]{:S(2)}, u32[]{:S(2)}) collective-permute-start(bf16[8,96,512]{2,1,0:T(8,128)(2,1)S(1)} %pad_maximum_fusion.1), channel_id=1, source_target_pairs={{0,6},{2,4},{4,2},{6,0},{32,34},{34,32},{36,38},{38,36},{1,7},{3,5... | collective-permute-start | bytes 2359304 | tf_op jit(solution)/shard_map/ppermute | solution.py:32
  60.0 21.7 %collective-permute-start.9 = (bf16[8,96,512]{2,1,0:T(8,128)(2,1)S(1)}, bf16[8,96,512]{2,1,0:T(8,128)(2,1)S(1)}, u32[]{:S(2)}, u32[]{:S(2)}) collective-permute-start(bf16[8,96,512]{2,1,0:T(8,128)(2,1)S(1)} %pad_maximum_fusion), channel_id=1, source_target_pairs={{0,24},{8,16},{16,8},{24,0},{32,40},{40,32},{48,56},{56,48},{1,25}... | collective-permute-start | bytes 2359304 | tf_op jit(solution)/shard_map/ppermute | solution.py:32
  60.2 34.6 %collective-permute-start.24 = (bf16[16,96,512]{2,1,0:T(8,128)(2,1)S(1)}, bf16[16,96,512]{2,1,0:T(8,128)(2,1)S(1)}, u32[]{:S(2)}, u32[]{:S(2)}) collective-permute-start(bf16[16,96,512]{2,1,0:T(8,128)(2,1)S(1)} %constant_dynamic-update-slice_fusion.10.refs_4_.refs_7_.refs_5_), channel_id=1, source_target_pairs={{0,2},{2,0},{4,6},{6,4},{32,38},{34,36},{36,34},{38,32},{1,3},{3,1... | collective-permute-start | bytes 4718600 | tf_op jit(solution)/shard_map/ppermute | solution.py:32
  60.3 35.1 %collective-permute-start.25 = (bf16[16,96,512]{2,1,0:T(8,128)(2,1)S(1)}, bf16[16,96,512]{2,1,0:T(8,128)(2,1)S(1)}, u32[]{:S(2)}, u32[]{:S(2)}) collective-permute-start(bf16[16,96,512]{2,1,0:T(8,128)(2,1)S(1)} %constant_dynamic-update-slice_fusion.10.refs_4_.refs_7_.refs_5_), channel_id=1, source_target_pairs={{0,6},{2,4},{4,2},{6,0},{32,34},{34,32},{36,38},{38,36},{1,7},{3,5... | collective-permute-start | bytes 4718600 | tf_op jit(solution)/shard_map/ppermute | solution.py:32
  73.1 46.0 %copy-start.5 = (f32[128]{0:T(128)S(1)}, f32[128]{0:T(128)}, u32[]{:S(2)}) copy-start(f32[128]{0:T(128)} %param.11) | copy-start | bytes 1540
  73.2 45.9 %copy-start.6 = (f32[128]{0:T(128)S(1)}, f32[128]{0:T(128)}, u32[]{:S(2)}) copy-start(f32[128]{0:T(128)} %param.10) | copy-start | bytes 1540
  73.2 34.7 %collective-permute-start.17 = (bf16[16,96,512]{2,1,0:T(8,128)(2,1)S(1)}, bf16[16,96,512]{2,1,0:T(8,128)(2,1)S(1)}, u32[]{:S(2)}, u32[]{:S(2)}) collective-permute-start(bf16[16,96,512]{2,1,0:T(8,128)(2,1)S(1)} %constant_dynamic-update-slice_fusion.5.refs_4_.refs_7_.refs_5_), channel_id=1, source_target_pairs={{0,8},{8,0},{16,24},{24,16},{32,56},{40,48},{48,40},{56,32},{1,9},... | collective-permute-start | bytes 4718600 | tf_op jit(solution)/shard_map/ppermute | solution.py:32
  81.7 37.3 %collective-permute-start.10 = (bf16[16,96,512]{2,1,0:T(8,128)(2,1)S(1)}, bf16[16,96,512]{2,1,0:T(8,128)(2,1)S(1)}, u32[]{:S(2)}, u32[]{:S(2)}) collective-permute-start(bf16[16,96,512]{2,1,0:T(8,128)(2,1)S(1)} %constant_dynamic-update-slice_fusion.refs_4_.refs_7_.refs_5_), channel_id=1, source_target_pairs={{0,64},{1,65},{32,97},{33,96},{64,0},{65,1},{96,33},{97,32},{2,66}... | collective-permute-start | bytes 4718600 | tf_op jit(solution)/shard_map/ppermute | solution.py:32
  82.2 41.3 %collective-permute-start.18 = (bf16[16,96,512]{2,1,0:T(8,128)(2,1)S(1)}, bf16[16,96,512]{2,1,0:T(8,128)(2,1)S(1)}, u32[]{:S(2)}, u32[]{:S(2)}) collective-permute-start(bf16[16,96,512]{2,1,0:T(8,128)(2,1)S(1)} %constant_dynamic-update-slice_fusion.5.refs_4_.refs_7_.refs_5_), channel_id=1, source_target_pairs={{0,24},{8,16},{16,8},{24,0},{32,40},{40,32},{48,56},{56,48},{1,25}... | collective-permute-start | bytes 4718600 | tf_op jit(solution)/shard_map/ppermute | solution.py:32
  94.8 33.0 %collective-permute-start.11 = (bf16[16,96,512]{2,1,0:T(8,128)(2,1)S(1)}, bf16[16,96,512]{2,1,0:T(8,128)(2,1)S(1)}, u32[]{:S(2)}, u32[]{:S(2)}) collective-permute-start(bf16[16,96,512]{2,1,0:T(8,128)(2,1)S(1)} %constant_dynamic-update-slice_fusion.refs_4_.refs_7_.refs_5_), channel_id=1, source_target_pairs={{0,65},{1,64},{32,96},{33,97},{64,1},{65,0},{96,32},{97,33},{2,67}... | collective-permute-start | bytes 4718600 | tf_op jit(solution)/shard_map/ppermute | solution.py:32
  95.4 36.9 %collective-permute-start.26 = (bf16[16,96,512]{2,1,0:T(8,128)(2,1)S(1)}, bf16[16,96,512]{2,1,0:T(8,128)(2,1)S(1)}, u32[]{:S(2)}, u32[]{:S(2)}) collective-permute-start(bf16[16,96,512]{2,1,0:T(8,128)(2,1)S(1)} %collective-permute-done.24.refs_5_.refs_6_), channel_id=1, source_target_pairs={{0,6},{2,4},{4,2},{6,0},{32,34},{34,32},{36,38},{38,36},{1,7},{3,5... | collective-permute-start | bytes 4718600 | tf_op jit(solution)/shard_map/ppermute | solution.py:32
  107.9 30.0 %collective-permute-start.19 = (bf16[16,96,512]{2,1,0:T(8,128)(2,1)S(1)}, bf16[16,96,512]{2,1,0:T(8,128)(2,1)S(1)}, u32[]{:S(2)}, u32[]{:S(2)}) collective-permute-start(bf16[16,96,512]{2,1,0:T(8,128)(2,1)S(1)} %collective-permute-done.17.refs_5_.refs_6_), channel_id=1, source_target_pairs={{0,24},{8,16},{16,8},{24,0},{32,40},{40,32},{48,56},{56,48},{1,25}... | collective-permute-start | bytes 4718600 | tf_op jit(solution)/shard_map/ppermute | solution.py:32
  119.1 25.0 %collective-permute-start.12 = (bf16[16,96,512]{2,1,0:T(8,128)(2,1)S(1)}, bf16[16,96,512]{2,1,0:T(8,128)(2,1)S(1)}, u32[]{:S(2)}, u32[]{:S(2)}) collective-permute-start(bf16[16,96,512]{2,1,0:T(8,128)(2,1)S(1)} %collective-permute-done.10.refs_5_.refs_6_), channel_id=1, source_target_pairs={{0,65},{1,64},{32,96},{33,97},{64,1},{65,0},{96,32},{97,33},{2,67}... | collective-permute-start | bytes 4718600 | tf_op jit(solution)/shard_map/ppermute | solution.py:32
  143.6 16.5 %collective-permute-start.29 = (bf16[2,512,512]{2,1,0:T(8,128)(2,1)S(1)}, bf16[2,512,512]{2,1,0:T(8,128)(2,1)S(1)}, u32[]{:S(2)}, u32[]{:S(2)}) collective-permute-start(bf16[2,512,512]{2,1,0:T(8,128)(2,1)S(1)} %get-tuple-element.43), channel_id=1, source_target_pairs={{0,32},{32,0},{1,33},{33,1},{2,34},{34,2},{3,35},{35,3},{4,36},{36... | collective-permute-start | bytes 3145736 | tf_op jit(solution)/shard_map/ppermute | solution.py:308
  143.6 16.5 %collective-permute-start.28 = (bf16[2,512,512]{2,1,0:T(8,128)(2,1)S(1)}, bf16[2,512,512]{2,1,0:T(8,128)(2,1)S(1)}, u32[]{:S(2)}, u32[]{:S(2)}) collective-permute-start(bf16[2,512,512]{2,1,0:T(8,128)(2,1)S(1)} %get-tuple-element.42), channel_id=1, source_target_pairs={{0,32},{32,0},{1,33},{33,1},{2,34},{34,2},{3,35},{35,3},{4,36},{36... | collective-permute-start | bytes 3145736 | tf_op jit(solution)/shard_map/ppermute | solution.py:308
  149.4 12.6 %collective-permute-start.27 = (bf16[2,512,512]{2,1,0:T(8,128)(2,1)S(1)}, bf16[2,512,512]{2,1,0:T(8,128)(2,1)S(1)}, u32[]{:S(2)}, u32[]{:S(2)}) collective-permute-start(bf16[2,512,512]{2,1,0:T(8,128)(2,1)S(1)} %get-tuple-element.41), channel_id=1, source_target_pairs={{0,32},{32,0},{1,33},{33,1},{2,34},{34,2},{3,35},{35,3},{4,36},{36... | collective-permute-start | bytes 3145736 | tf_op jit(solution)/shard_map/ppermute | solution.py:308
  149.4 9.4 %collective-permute-start.4 = (bf16[96,1536]{1,0:T(8,128)(2,1)S(1)}, bf16[96,1536]{1,0:T(8,128)(2,1)S(1)}, u32[]{:S(2)}, u32[]{:S(2)}) collective-permute-start(bf16[96,1536]{1,0:T(8,128)(2,1)S(1)} %get-tuple-element.31), channel_id=1, source_target_pairs={{0,64},{64,0},{1,65},{65,1},{2,66},{66,2},{3,67},{67,3},{4,68},{68... | collective-permute-start | bytes 884744 | tf_op jit(solution)/shard_map/ppermute | solution.py:277
  (5 other events, 33.5 us)

commit v5 on v4

--- a/solution.py
+++ b/solution.py
@@ -303,12 +303,12 @@
         units.append([copied[k], one, two, three])
         begun += project_half(k, 0, where, normed, other, gains, [copied[k], one, two, copied[k]])
     outputs, back = (), []
-    for k in (1, 2, 0):
+    where, student_new, teacher_new = lax.optimization_barrier((where, student_new, teacher_new))
+    for k in range(COLORS):
         *outputs, send = project_half(k, 1, where, normed, other, gains, units[k], begun[k], outputs)
         back.append(lax.ppermute(send, "core", swap))
-    where, student_new, teacher_new = lax.optimization_barrier((where, student_new, teacher_new))
-    outputs = put(1, where, back[:2], *outputs)
-    outputs = put(0, where, back[2:], *outputs)
+    outputs = put(0, where, back[:2], *outputs)
+    outputs = put(2, where, back[2:], *outputs)
     return (teacher_new, student_new, *outputs)
 
 

time: 164 us -> 137 us (0.84)
  the two profiles are of different devices: /device:TPU:30 before, /device:TPU:0 now
where the time goes in v5:
time: 137 us; the launch traced here: 136 us
  starting transfers between devices  49.3 us (36%)
  waiting for transfers between devices  43.9 us (32%)
  Pallas kernels  34.6 us (25%)
  other arithmetic  3.76 us (3%)
  local copies, waits for them, and re-layouts  3.37 us (2%)
    ppermute x21, starting transfers between devices, exchange(): return lax.ppermute(x, axes, pairs)  44.3 us
    ppermute x21, waiting for transfers between devices, exchange(): return lax.ppermute(x, axes, pairs)  41 us
    pallas_call x6, Pallas kernels, project_half(): pl.pallas_call(body, grid_spec=pltpu.PrefetchScalarGridSpec(num_scalar_pr...  29.3 us
    ppermute x3, starting transfers between devices, shards(): arrived.append(lax.ppermute(give[k], 'zlo', swap).astype(jnp.float32))  4.13 us
    pallas_call x2, Pallas kernels, put(): pl.pallas_call(lambda *refs: put_body(len(got), *refs), grid_spec=pltpu.P...  3.55 us
    unnamed x23, local copies, waits for them, and re-layouts  3.17 us
  transfers between devices with their start and end apart: 30, of which 11 were waited for; matrix products, arithmetic and copies ran while one was open for 3% of the time, Pallas kernels for 24%

profile of v5, /device:TPU:0, one launch (start us, length us, event | category | flops | bytes accessed | tf_op | source)
XLA Modules:
  0.0 135.9 jit_solution(11561223701184188366)
XLA Ops:
  0.7 1.7 %copy-done = f32[1,96,6144]{2,1,0:T(8,128)S(1)} copy-done((f32[1,96,6144]{2,1,0:T(8,128)S(1)}, f32[1,96,6144]{2,1,0:T(8,128)}, u32[]{:S(2)}) %copy-start) | copy-done | bytes 2359320
  7.6 2.1 %collective-permute-start.1 = (bf16[96,512]{1,0:T(8,128)(2,1)S(1)}, bf16[96,512]{1,0:T(8,128)(2,1)S(1)}, u32[]{:S(2)}, u32[]{:S(2)}) collective-permute-start(bf16[96,512]{1,0:T(8,128)(2,1)S(1)} %get-tuple-element.28), channel_id=1, source_target_pairs={{0,64},{64,0},{1,65},{65,1},{2,66},{66,2},{3,67},{67,3},{4,68},{68... | collective-permute-start | bytes 294920 | tf_op jit(solution)/shard_map/ppermute | solution.py:276
  9.8 1.9 %collective-permute-start.3 = (bf16[96,512]{1,0:T(8,128)(2,1)S(1)}, bf16[96,512]{1,0:T(8,128)(2,1)S(1)}, u32[]{:S(2)}, u32[]{:S(2)}) collective-permute-start(bf16[96,512]{1,0:T(8,128)(2,1)S(1)} %get-tuple-element.30), channel_id=1, source_target_pairs={{0,64},{64,0},{1,65},{65,1},{2,66},{66,2},{3,67},{67,3},{4,68},{68... | collective-permute-start | bytes 294920 | tf_op jit(solution)/shard_map/ppermute | solution.py:276
  13.4 1.7 %collective-permute-start.20 = (bf16[1,96,512]{2,1,0:T(8,128)(2,1)S(1)}, bf16[1,96,512]{2,1,0:T(8,128)(2,1)S(1)}, u32[]{:S(2)}, u32[]{:S(2)}) collective-permute-start(bf16[1,96,512]{2,1,0:T(8,128)(2,1)S(1)} %get-tuple-element.51), channel_id=1, source_target_pairs={{0,2},{2,0},{4,6},{6,4},{32,38},{34,36},{36,34},{38,32},{1,3},{3,1... | collective-permute-start | bytes 294920 | tf_op jit(solution)/shard_map/ppermute | solution.py:32
  15.5 1.8 %collective-permute-start.13 = (bf16[1,96,512]{2,1,0:T(8,128)(2,1)S(1)}, bf16[1,96,512]{2,1,0:T(8,128)(2,1)S(1)}, u32[]{:S(2)}, u32[]{:S(2)}) collective-permute-start(bf16[1,96,512]{2,1,0:T(8,128)(2,1)S(1)} %get-tuple-element.53), channel_id=1, source_target_pairs={{0,8},{8,0},{16,24},{24,16},{32,56},{40,48},{48,40},{56,32},{1,9},... | collective-permute-start | bytes 294920 | tf_op jit(solution)/shard_map/ppermute | solution.py:32
  17.6 2.1 %collective-permute-start.6 = (bf16[1,96,512]{2,1,0:T(8,128)(2,1)S(1)}, bf16[1,96,512]{2,1,0:T(8,128)(2,1)S(1)}, u32[]{:S(2)}, u32[]{:S(2)}) collective-permute-start(bf16[1,96,512]{2,1,0:T(8,128)(2,1)S(1)} %get-tuple-element.55), channel_id=1, source_target_pairs={{0,64},{1,65},{32,97},{33,96},{64,0},{65,1},{96,33},{97,32},{2,66}... | collective-permute-start | bytes 294920 | tf_op jit(solution)/shard_map/ppermute | solution.py:32
  19.7 2.8 %collective-permute-start.21 = (bf16[2,96,512]{2,1,0:T(8,128)(2,1)S(1)}, bf16[2,96,512]{2,1,0:T(8,128)(2,1)S(1)}, u32[]{:S(2)}, u32[]{:S(2)}) collective-permute-start(bf16[2,96,512]{2,1,0:T(8,128)(2,1)S(1)} %pad_maximum_fusion.8), channel_id=1, source_target_pairs={{0,6},{2,4},{4,2},{6,0},{32,34},{34,32},{36,38},{38,36},{1,7},{3,5... | collective-permute-start | bytes 589832 | tf_op jit(solution)/shard_map/ppermute | solution.py:32
  22.6 3.1 %collective-permute-start.14 = (bf16[2,96,512]{2,1,0:T(8,128)(2,1)S(1)}, bf16[2,96,512]{2,1,0:T(8,128)(2,1)S(1)}, u32[]{:S(2)}, u32[]{:S(2)}) collective-permute-start(bf16[2,96,512]{2,1,0:T(8,128)(2,1)S(1)} %pad_maximum_fusion.7), channel_id=1, source_target_pairs={{0,24},{8,16},{16,8},{24,0},{32,40},{40,32},{48,56},{56,48},{1,25}... | collective-permute-start | bytes 589832 | tf_op jit(solution)/shard_map/ppermute | solution.py:32
  25.7 2.7 %collective-permute-start.7 = (bf16[2,96,512]{2,1,0:T(8,128)(2,1)S(1)}, bf16[2,96,512]{2,1,0:T(8,128)(2,1)S(1)}, u32[]{:S(2)}, u32[]{:S(2)}) collective-permute-start(bf16[2,96,512]{2,1,0:T(8,128)(2,1)S(1)} %pad_maximum_fusion.6), channel_id=1, source_target_pairs={{0,65},{1,64},{32,96},{33,97},{64,1},{65,0},{96,32},{97,33},{2,67}... | collective-permute-start | bytes 589832 | tf_op jit(solution)/shard_map/ppermute | solution.py:32
  28.4 2.2 %collective-permute-start.22 = (bf16[4,96,512]{2,1,0:T(8,128)(2,1)S(1)}, bf16[4,96,512]{2,1,0:T(8,128)(2,1)S(1)}, u32[]{:S(2)}, u32[]{:S(2)}) collective-permute-start(bf16[4,96,512]{2,1,0:T(8,128)(2,1)S(1)} %pad_maximum_fusion.5), channel_id=1, source_target_pairs={{0,8},{8,0},{16,24},{24,16},{32,56},{40,48},{48,40},{56,32},{1,9},... | collective-permute-start | bytes 1179656 | tf_op jit(solution)/shard_map/ppermute | solution.py:32
  30.8 2.8 %collective-permute-done.7 = bf16[2,96,512]{2,1,0:T(8,128)(2,1)S(1)} collective-permute-done((bf16[2,96,512]{2,1,0:T(8,128)(2,1)S(1)}, bf16[2,96,512]{2,1,0:T(8,128)(2,1)S(1)}, u32[]{:S(2)}, u32[]{:S(2)}) %collective-permute-start.7) | collective-permute-done | bytes 196640 | tf_op jit(solution)/shard_map/ppermute | solution.py:32
  35.3 1.9 %collective-permute-done.22 = bf16[4,96,512]{2,1,0:T(8,128)(2,1)S(1)} collective-permute-done((bf16[4,96,512]{2,1,0:T(8,128)(2,1)S(1)}, bf16[4,96,512]{2,1,0:T(8,128)(2,1)S(1)}, u32[]{:S(2)}, u32[]{:S(2)}) %collective-permute-start.22) | collective-permute-done | bytes 393248 | tf_op jit(solution)/shard_map/ppermute | solution.py:32
  37.3 3.0 %collective-permute-start.23 = (bf16[8,96,512]{2,1,0:T(8,128)(2,1)S(1)}, bf16[8,96,512]{2,1,0:T(8,128)(2,1)S(1)}, u32[]{:S(2)}, u32[]{:S(2)}) collective-permute-start(bf16[8,96,512]{2,1,0:T(8,128)(2,1)S(1)} %pad_maximum_fusion.2), channel_id=1, source_target_pairs={{0,24},{8,16},{16,8},{24,0},{32,40},{40,32},{48,56},{56,48},{1,25}... | collective-permute-start | bytes 2359304 | tf_op jit(solution)/shard_map/ppermute | solution.py:32
  40.4 2.6 %collective-permute-start.16 = (bf16[8,96,512]{2,1,0:T(8,128)(2,1)S(1)}, bf16[8,96,512]{2,1,0:T(8,128)(2,1)S(1)}, u32[]{:S(2)}, u32[]{:S(2)}) collective-permute-start(bf16[8,96,512]{2,1,0:T(8,128)(2,1)S(1)} %pad_maximum_fusion.1), channel_id=1, source_target_pairs={{0,65},{1,64},{32,96},{33,97},{64,1},{65,0},{96,32},{97,33},{2,67}... | collective-permute-start | bytes 2359304 | tf_op jit(solution)/shard_map/ppermute | solution.py:32
  43.5 3.2 %collective-permute-start.9 = (bf16[8,96,512]{2,1,0:T(8,128)(2,1)S(1)}, bf16[8,96,512]{2,1,0:T(8,128)(2,1)S(1)}, u32[]{:S(2)}, u32[]{:S(2)}) collective-permute-start(bf16[8,96,512]{2,1,0:T(8,128)(2,1)S(1)} %pad_maximum_fusion), channel_id=1, source_target_pairs={{0,6},{2,4},{4,2},{6,0},{32,34},{34,32},{36,38},{38,36},{1,7},{3,5... | collective-permute-start | bytes 2359304 | tf_op jit(solution)/shard_map/ppermute | solution.py:32
  46.8 3.7 %collective-permute-done.23 = bf16[8,96,512]{2,1,0:T(8,128)(2,1)S(1)} collective-permute-done((bf16[8,96,512]{2,1,0:T(8,128)(2,1)S(1)}, bf16[8,96,512]{2,1,0:T(8,128)(2,1)S(1)}, u32[]{:S(2)}, u32[]{:S(2)}) %collective-permute-start.23) | collective-permute-done | bytes 786464 | tf_op jit(solution)/shard_map/ppermute | solution.py:32
  51.3 6.6 %collective-permute-done.16 = bf16[8,96,512]{2,1,0:T(8,128)(2,1)S(1)} collective-permute-done((bf16[8,96,512]{2,1,0:T(8,128)(2,1)S(1)}, bf16[8,96,512]{2,1,0:T(8,128)(2,1)S(1)}, u32[]{:S(2)}, u32[]{:S(2)}) %collective-permute-start.16) | collective-permute-done | bytes 786464 | tf_op jit(solution)/shard_map/ppermute | solution.py:32
  57.9 2.7 %collective-permute-start.25 = (bf16[16,96,512]{2,1,0:T(8,128)(2,1)S(1)}, bf16[16,96,512]{2,1,0:T(8,128)(2,1)S(1)}, u32[]{:S(2)}, u32[]{:S(2)}) collective-permute-start(bf16[16,96,512]{2,1,0:T(8,128)(2,1)S(1)} %constant_dynamic-update-slice_fusion.10.refs_4_.refs_7_.refs_5_), channel_id=1, source_target_pairs={{0,65},{1,64},{32,96},{33,97},{64,1},{65,0},{96,32},{97,33},{2,67}... | collective-permute-start | bytes 4718600 | tf_op jit(solution)/shard_map/ppermute | solution.py:32
  61.5 3.9 %collective-permute-start.10 = (bf16[16,96,512]{2,1,0:T(8,128)(2,1)S(1)}, bf16[16,96,512]{2,1,0:T(8,128)(2,1)S(1)}, u32[]{:S(2)}, u32[]{:S(2)}) collective-permute-start(bf16[16,96,512]{2,1,0:T(8,128)(2,1)S(1)} %constant_dynamic-update-slice_fusion.refs_4_.refs_7_.refs_5_), channel_id=1, source_target_pairs={{0,8},{8,0},{16,24},{24,16},{32,56},{40,48},{48,40},{56,32},{1,9},... | collective-permute-start | bytes 4718600 | tf_op jit(solution)/shard_map/ppermute | solution.py:32
  65.3 2.5 %collective-permute-start.18 = (bf16[16,96,512]{2,1,0:T(8,128)(2,1)S(1)}, bf16[16,96,512]{2,1,0:T(8,128)(2,1)S(1)}, u32[]{:S(2)}, u32[]{:S(2)}) collective-permute-start(bf16[16,96,512]{2,1,0:T(8,128)(2,1)S(1)} %constant_dynamic-update-slice_fusion.5.refs_4_.refs_7_.refs_5_), channel_id=1, source_target_pairs={{0,6},{2,4},{4,2},{6,0},{32,34},{34,32},{36,38},{38,36},{1,7},{3,5... | collective-permute-start | bytes 4718600 | tf_op jit(solution)/shard_map/ppermute | solution.py:32
  67.8 17.4 %collective-permute-done.24.refs_5_.refs_6_ = bf16[16,96,512]{2,1,0:T(8,128)(2,1)S(1)} collective-permute-done((bf16[16,96,512]{2,1,0:T(8,128)(2,1)S(1)}, bf16[16,96,512]{2,1,0:T(8,128)(2,1)S(1)}, u32[]{:S(2)}, u32[]{:S(2)}) %collective-permute-start.24) | collective-permute-done | bytes 1572896 | tf_op jit(solution)/shard_map/ppermute | solution.py:32
  85.2 2.9 %collective-permute-start.11 = (bf16[16,96,512]{2,1,0:T(8,128)(2,1)S(1)}, bf16[16,96,512]{2,1,0:T(8,128)(2,1)S(1)}, u32[]{:S(2)}, u32[]{:S(2)}) collective-permute-start(bf16[16,96,512]{2,1,0:T(8,128)(2,1)S(1)} %constant_dynamic-update-slice_fusion.refs_4_.refs_7_.refs_5_), channel_id=1, source_target_pairs={{0,24},{8,16},{16,8},{24,0},{32,40},{40,32},{48,56},{56,48},{1,25}... | collective-permute-start | bytes 4718600 | tf_op jit(solution)/shard_map/ppermute | solution.py:32
  88.1 1.8 %collective-permute-start.26 = (bf16[16,96,512]{2,1,0:T(8,128)(2,1)S(1)}, bf16[16,96,512]{2,1,0:T(8,128)(2,1)S(1)}, u32[]{:S(2)}, u32[]{:S(2)}) collective-permute-start(bf16[16,96,512]{2,1,0:T(8,128)(2,1)S(1)} %collective-permute-done.24.refs_5_.refs_6_), channel_id=1, source_target_pairs={{0,65},{1,64},{32,96},{33,97},{64,1},{65,0},{96,32},{97,33},{2,67}... | collective-permute-start | bytes 4718600 | tf_op jit(solution)/shard_map/ppermute | solution.py:32
  90.0 8.0 %collective-permute-done.17.refs_5_.refs_6_ = bf16[16,96,512]{2,1,0:T(8,128)(2,1)S(1)} collective-permute-done((bf16[16,96,512]{2,1,0:T(8,128)(2,1)S(1)}, bf16[16,96,512]{2,1,0:T(8,128)(2,1)S(1)}, u32[]{:S(2)}, u32[]{:S(2)}) %collective-permute-start.17) | collective-permute-done | bytes 1572896 | tf_op jit(solution)/shard_map/ppermute | solution.py:32
  98.0 2.5 %collective-permute-start.19 = (bf16[16,96,512]{2,1,0:T(8,128)(2,1)S(1)}, bf16[16,96,512]{2,1,0:T(8,128)(2,1)S(1)}, u32[]{:S(2)}, u32[]{:S(2)}) collective-permute-start(bf16[16,96,512]{2,1,0:T(8,128)(2,1)S(1)} %collective-permute-done.17.refs_5_.refs_6_), channel_id=1, source_target_pairs={{0,6},{2,4},{4,2},{6,0},{32,34},{34,32},{36,38},{38,36},{1,7},{3,5... | collective-permute-start | bytes 4718600 | tf_op jit(solution)/shard_map/ppermute | solution.py:32
  101.8 4.4 %shard_map.95.refs_4_ = bf16[2,512,512]{2,1,0:T(8,128)(2,1)S(1)} custom-call(s32[2]{0:T(128)S(1)} %pad_add_fusion.core.refs_0_, bf16[512,3072]{1,0:T(8,128)(2,1)S(1)} %fusion.2.refs_1_, bf16[512,3072]{1,0:T(8,128)(2,1)S(1)} %collective-permute-done.5.refs_2_, f32[2,128]{1,0:T(2,128)S(1)} %pad_maximum_fusion.9.refs_3_, ...), custom_call_target="tpu_custom_call" | custom-call | flops 3221225472 | bytes 12582912 | tf_op jit(solution)/shard_map/pallas_call | solution.py:156
  106.2 4.2 %shard_map.94.refs_4_ = f32[2,512,1024]{2,1,0:T(8,128)S(1)} custom-call(s32[2]{0:T(128)S(1)} %pad_add_fusion.core.refs_0_, bf16[512,3072]{1,0:T(8,128)(2,1)S(1)} %fusion.2.refs_1_, bf16[512,3072]{1,0:T(8,128)(2,1)S(1)} %collective-permute-done.5.refs_2_, f32[2,128]{1,0:T(2,128)S(1)} %pad_maximum_fusion.9.refs_3_, ...), custom_call_target="tpu_custom_call" | custom-call | flops 3221225472 | bytes 12582912 | tf_op jit(solution)/shard_map/pallas_call | solution.py:156
  110.4 4.3 %shard_map.93.refs_4_ = f32[2,512,1024]{2,1,0:T(8,128)S(1)} custom-call(s32[2]{0:T(128)S(1)} %pad_add_fusion.core.refs_0_, bf16[512,3072]{1,0:T(8,128)(2,1)S(1)} %fusion.2.refs_1_, bf16[512,3072]{1,0:T(8,128)(2,1)S(1)} %collective-permute-done.5.refs_2_, f32[2,128]{1,0:T(2,128)S(1)} %pad_maximum_fusion.9.refs_3_, ...), custom_call_target="tpu_custom_call" | custom-call | flops 3221225472 | bytes 12582912 | tf_op jit(solution)/shard_map/pallas_call | solution.py:156
  114.7 5.2 %shard_map.96 = (bf16[512,3072]{1,0:T(8,128)(2,1)}, bf16[512,3072]{1,0:T(8,128)(2,1)}, bf16[2,512,512]{2,1,0:T(8,128)(2,1)S(1)}) custom-call(s32[2]{0:T(128)S(1)} %pad_add_fusion.core.refs_0_, bf16[512,3072]{1,0:T(8,128)(2,1)S(1)} %fusion.2.refs_1_, bf16[512,3072]{1,0:T(8,128)(2,1)S(1)} %collective-permute-done.5.refs_2_, ...), custom_call_target="tpu_custom_call" | custom-call | flops 3221225472 | bytes 12582912 | tf_op jit(solution)/shard_map/pallas_call | solution.py:156
  119.9 5.8 %shard_map.97 = (bf16[512,3072]{1,0:T(8,128)(2,1)}, bf16[512,3072]{1,0:T(8,128)(2,1)}, bf16[2,512,512]{2,1,0:T(8,128)(2,1)S(1)}) custom-call(s32[2]{0:T(128)S(1)} %pad_add_fusion.core.refs_0_, bf16[512,3072]{1,0:T(8,128)(2,1)S(1)} %fusion.2.refs_1_, ...), custom_call_target="tpu_custom_call", output_to_operand_aliasing={{0}: (9, {}), {1}: (10, {})} | custom-call | flops 3221225472 | bytes 12582912 | tf_op jit(solution)/shard_map/pallas_call | solution.py:156
  126.2 5.4 %shard_map.98 = (bf16[512,3072]{1,0:T(8,128)(2,1)}, bf16[512,3072]{1,0:T(8,128)(2,1)}, bf16[2,512,512]{2,1,0:T(8,128)(2,1)S(1)}) custom-call(s32[2]{0:T(128)S(1)} %pad_add_fusion.core.refs_0_, bf16[512,3072]{1,0:T(8,128)(2,1)S(1)} %fusion.2.refs_1_, ...), custom_call_target="tpu_custom_call", output_to_operand_aliasing={{0}: (9, {}), {1}: (10, {})} | custom-call | flops 3221225472 | bytes 12582912 | tf_op jit(solution)/shard_map/pallas_call | solution.py:156
  131.7 2.0 %shard_map.99 = (bf16[512,3072]{1,0:T(8,128)(2,1)}, bf16[512,3072]{1,0:T(8,128)(2,1)}) custom-call(s32[2]{0:T(128)S(1)} %pad_add_fusion.core.refs_0_, bf16[2,512,512]{2,1,0:T(8,128)(2,1)S(1)} %collective-permute-done.28.refs_1_, bf16[2,512,512]{2,1,0:T(8,128)(2,1)S(1)} %collective-permute-done.29.refs_2_, ...), custom_call_target="tpu_custom_call", output_to_operand_aliasing={{0}: (3, {}), {1}: (4, {})} | custom-call | flops 1000000000 | bytes 8388608 | tf_op jit(solution)/shard_map/pallas_call | solution.py:190
  (86 shorter events, 16.1 us)
Async XLA Ops:
  3.2 3.1 %collective-permute-start = (f32[2,96,1536]{2,1,0:T(8,128)S(1)}, f32[2,96,1536]{2,1,0:T(8,128)S(1)}, u32[]{:S(2)}, u32[]{:S(2)}) collective-permute-start(f32[2,96,1536]{2,1,0:T(8,128)S(1)} %pick.1), channel_id=1, source_target_pairs={{0,32},{32,0},{1,33},{33,1},{2,34},{34,2},{3,35},{35,3},{4,36},{36... | collective-permute-start | bytes 3538952 | tf_op jit(solution)/shard_map/ppermute | solution.py:272
  6.2 59.1 %collective-permute-start.5 = (bf16[512,3072]{1,0:T(8,128)(2,1)S(1)}, bf16[512,3072]{1,0:T(8,128)(2,1)S(1)}, u32[]{:S(2)}, u32[]{:S(2)}) collective-permute-start(bf16[512,3072]{1,0:T(8,128)(2,1)S(1)} %fusion.2.refs_1_), channel_id=1, source_target_pairs={{0,32},{32,0},{1,33},{33,1},{2,34},{34,2},{3,35},{35,3},{4,36},{36... | collective-permute-start | bytes 9437192 | tf_op jit(solution)/shard_map/ppermute | solution.py:291
  7.6 5.8 %collective-permute-start.1 = (bf16[96,512]{1,0:T(8,128)(2,1)S(1)}, bf16[96,512]{1,0:T(8,128)(2,1)S(1)}, u32[]{:S(2)}, u32[]{:S(2)}) collective-permute-start(bf16[96,512]{1,0:T(8,128)(2,1)S(1)} %get-tuple-element.28), channel_id=1, source_target_pairs={{0,64},{64,0},{1,65},{65,1},{2,66},{66,2},{3,67},{67,3},{4,68},{68... | collective-permute-start | bytes 294920 | tf_op jit(solution)/shard_map/ppermute | solution.py:276
  9.7 5.8 %collective-permute-start.2 = (bf16[96,512]{1,0:T(8,128)(2,1)S(1)}, bf16[96,512]{1,0:T(8,128)(2,1)S(1)}, u32[]{:S(2)}, u32[]{:S(2)}) collective-permute-start(bf16[96,512]{1,0:T(8,128)(2,1)S(1)} %get-tuple-element.29), channel_id=1, source_target_pairs={{0,64},{64,0},{1,65},{65,1},{2,66},{66,2},{3,67},{67,3},{4,68},{68... | collective-permute-start | bytes 294920 | tf_op jit(solution)/shard_map/ppermute | solution.py:276
  9.8 7.8 %collective-permute-start.3 = (bf16[96,512]{1,0:T(8,128)(2,1)S(1)}, bf16[96,512]{1,0:T(8,128)(2,1)S(1)}, u32[]{:S(2)}, u32[]{:S(2)}) collective-permute-start(bf16[96,512]{1,0:T(8,128)(2,1)S(1)} %get-tuple-element.30), channel_id=1, source_target_pairs={{0,64},{64,0},{1,65},{65,1},{2,66},{66,2},{3,67},{67,3},{4,68},{68... | collective-permute-start | bytes 294920 | tf_op jit(solution)/shard_map/ppermute | solution.py:276
  11.7 49.8 %collective-permute-start.4 = (bf16[96,1536]{1,0:T(8,128)(2,1)S(1)}, bf16[96,1536]{1,0:T(8,128)(2,1)S(1)}, u32[]{:S(2)}, u32[]{:S(2)}) collective-permute-start(bf16[96,1536]{1,0:T(8,128)(2,1)S(1)} %get-tuple-element.31), channel_id=1, source_target_pairs={{0,64},{64,0},{1,65},{65,1},{2,66},{66,2},{3,67},{67,3},{4,68},{68... | collective-permute-start | bytes 884744 | tf_op jit(solution)/shard_map/ppermute | solution.py:277
  13.4 6.3 %collective-permute-start.20 = (bf16[1,96,512]{2,1,0:T(8,128)(2,1)S(1)}, bf16[1,96,512]{2,1,0:T(8,128)(2,1)S(1)}, u32[]{:S(2)}, u32[]{:S(2)}) collective-permute-start(bf16[1,96,512]{2,1,0:T(8,128)(2,1)S(1)} %get-tuple-element.51), channel_id=1, source_target_pairs={{0,2},{2,0},{4,6},{6,4},{32,38},{34,36},{36,34},{38,32},{1,3},{3,1... | collective-permute-start | bytes 294920 | tf_op jit(solution)/shard_map/ppermute | solution.py:32
  15.5 7.1 %collective-permute-start.13 = (bf16[1,96,512]{2,1,0:T(8,128)(2,1)S(1)}, bf16[1,96,512]{2,1,0:T(8,128)(2,1)S(1)}, u32[]{:S(2)}, u32[]{:S(2)}) collective-permute-start(bf16[1,96,512]{2,1,0:T(8,128)(2,1)S(1)} %get-tuple-element.53), channel_id=1, source_target_pairs={{0,8},{8,0},{16,24},{24,16},{32,56},{40,48},{48,40},{56,32},{1,9},... | collective-permute-start | bytes 294920 | tf_op jit(solution)/shard_map/ppermute | solution.py:32
  17.6 8.1 %collective-permute-start.6 = (bf16[1,96,512]{2,1,0:T(8,128)(2,1)S(1)}, bf16[1,96,512]{2,1,0:T(8,128)(2,1)S(1)}, u32[]{:S(2)}, u32[]{:S(2)}) collective-permute-start(bf16[1,96,512]{2,1,0:T(8,128)(2,1)S(1)} %get-tuple-element.55), channel_id=1, source_target_pairs={{0,64},{1,65},{32,97},{33,96},{64,0},{65,1},{96,33},{97,32},{2,66}... | collective-permute-start | bytes 294920 | tf_op jit(solution)/shard_map/ppermute | solution.py:32
  19.7 8.7 %collective-permute-start.21 = (bf16[2,96,512]{2,1,0:T(8,128)(2,1)S(1)}, bf16[2,96,512]{2,1,0:T(8,128)(2,1)S(1)}, u32[]{:S(2)}, u32[]{:S(2)}) collective-permute-start(bf16[2,96,512]{2,1,0:T(8,128)(2,1)S(1)} %pad_maximum_fusion.8), channel_id=1, source_target_pairs={{0,6},{2,4},{4,2},{6,0},{32,34},{34,32},{36,38},{38,36},{1,7},{3,5... | collective-permute-start | bytes 589832 | tf_op jit(solution)/shard_map/ppermute | solution.py:32
  22.6 8.1 %collective-permute-start.14 = (bf16[2,96,512]{2,1,0:T(8,128)(2,1)S(1)}, bf16[2,96,512]{2,1,0:T(8,128)(2,1)S(1)}, u32[]{:S(2)}, u32[]{:S(2)}) collective-permute-start(bf16[2,96,512]{2,1,0:T(8,128)(2,1)S(1)} %pad_maximum_fusion.7), channel_id=1, source_target_pairs={{0,24},{8,16},{16,8},{24,0},{32,40},{40,32},{48,56},{56,48},{1,25}... | collective-permute-start | bytes 589832 | tf_op jit(solution)/shard_map/ppermute | solution.py:32
  25.7 8.0 %collective-permute-start.7 = (bf16[2,96,512]{2,1,0:T(8,128)(2,1)S(1)}, bf16[2,96,512]{2,1,0:T(8,128)(2,1)S(1)}, u32[]{:S(2)}, u32[]{:S(2)}) collective-permute-start(bf16[2,96,512]{2,1,0:T(8,128)(2,1)S(1)} %pad_maximum_fusion.6), channel_id=1, source_target_pairs={{0,65},{1,64},{32,96},{33,97},{64,1},{65,0},{96,32},{97,33},{2,67}... | collective-permute-start | bytes 589832 | tf_op jit(solution)/shard_map/ppermute | solution.py:32
  28.4 8.8 %collective-permute-start.22 = (bf16[4,96,512]{2,1,0:T(8,128)(2,1)S(1)}, bf16[4,96,512]{2,1,0:T(8,128)(2,1)S(1)}, u32[]{:S(2)}, u32[]{:S(2)}) collective-permute-start(bf16[4,96,512]{2,1,0:T(8,128)(2,1)S(1)} %pad_maximum_fusion.5), channel_id=1, source_target_pairs={{0,8},{8,0},{16,24},{24,16},{32,56},{40,48},{48,40},{56,32},{1,9},... | collective-permute-start | bytes 1179656 | tf_op jit(solution)/shard_map/ppermute | solution.py:32
  30.7 9.5 %collective-permute-start.15 = (bf16[4,96,512]{2,1,0:T(8,128)(2,1)S(1)}, bf16[4,96,512]{2,1,0:T(8,128)(2,1)S(1)}, u32[]{:S(2)}, u32[]{:S(2)}) collective-permute-start(bf16[4,96,512]{2,1,0:T(8,128)(2,1)S(1)} %pad_maximum_fusion.4), channel_id=1, source_target_pairs={{0,64},{1,65},{32,97},{33,96},{64,0},{65,1},{96,33},{97,32},{2,66}... | collective-permute-start | bytes 1179656 | tf_op jit(solution)/shard_map/ppermute | solution.py:32
  33.7 9.8 %collective-permute-start.8 = (bf16[4,96,512]{2,1,0:T(8,128)(2,1)S(1)}, bf16[4,96,512]{2,1,0:T(8,128)(2,1)S(1)}, u32[]{:S(2)}, u32[]{:S(2)}) collective-permute-start(bf16[4,96,512]{2,1,0:T(8,128)(2,1)S(1)} %pad_maximum_fusion.3), channel_id=1, source_target_pairs={{0,2},{2,0},{4,6},{6,4},{32,38},{34,36},{36,34},{38,32},{1,3},{3,1... | collective-permute-start | bytes 1179656 | tf_op jit(solution)/shard_map/ppermute | solution.py:32
  37.3 13.3 %collective-permute-start.23 = (bf16[8,96,512]{2,1,0:T(8,128)(2,1)S(1)}, bf16[8,96,512]{2,1,0:T(8,128)(2,1)S(1)}, u32[]{:S(2)}, u32[]{:S(2)}) collective-permute-start(bf16[8,96,512]{2,1,0:T(8,128)(2,1)S(1)} %pad_maximum_fusion.2), channel_id=1, source_target_pairs={{0,24},{8,16},{16,8},{24,0},{32,40},{40,32},{48,56},{56,48},{1,25}... | collective-permute-start | bytes 2359304 | tf_op jit(solution)/shard_map/ppermute | solution.py:32
  40.4 17.5 %collective-permute-start.16 = (bf16[8,96,512]{2,1,0:T(8,128)(2,1)S(1)}, bf16[8,96,512]{2,1,0:T(8,128)(2,1)S(1)}, u32[]{:S(2)}, u32[]{:S(2)}) collective-permute-start(bf16[8,96,512]{2,1,0:T(8,128)(2,1)S(1)} %pad_maximum_fusion.1), channel_id=1, source_target_pairs={{0,65},{1,64},{32,96},{33,97},{64,1},{65,0},{96,32},{97,33},{2,67}... | collective-permute-start | bytes 2359304 | tf_op jit(solution)/shard_map/ppermute | solution.py:32
  43.5 17.1 %collective-permute-start.9 = (bf16[8,96,512]{2,1,0:T(8,128)(2,1)S(1)}, bf16[8,96,512]{2,1,0:T(8,128)(2,1)S(1)}, u32[]{:S(2)}, u32[]{:S(2)}) collective-permute-start(bf16[8,96,512]{2,1,0:T(8,128)(2,1)S(1)} %pad_maximum_fusion), channel_id=1, source_target_pairs={{0,6},{2,4},{4,2},{6,0},{32,34},{34,32},{36,38},{38,36},{1,7},{3,5... | collective-permute-start | bytes 2359304 | tf_op jit(solution)/shard_map/ppermute | solution.py:32
  50.6 34.6 %collective-permute-start.24 = (bf16[16,96,512]{2,1,0:T(8,128)(2,1)S(1)}, bf16[16,96,512]{2,1,0:T(8,128)(2,1)S(1)}, u32[]{:S(2)}, u32[]{:S(2)}) collective-permute-start(bf16[16,96,512]{2,1,0:T(8,128)(2,1)S(1)} %constant_dynamic-update-slice_fusion.10.refs_4_.refs_7_.refs_5_), channel_id=1, source_target_pairs={{0,64},{1,65},{32,97},{33,96},{64,0},{65,1},{96,33},{97,32},{2,66}... | collective-permute-start | bytes 4718600 | tf_op jit(solution)/shard_map/ppermute | solution.py:32
  51.3 38.6 %copy-start.5 = (f32[128]{0:T(128)S(1)}, f32[128]{0:T(128)}, u32[]{:S(2)}) copy-start(f32[128]{0:T(128)} %param.11) | copy-start | bytes 1540
  57.9 30.2 %collective-permute-start.25 = (bf16[16,96,512]{2,1,0:T(8,128)(2,1)S(1)}, bf16[16,96,512]{2,1,0:T(8,128)(2,1)S(1)}, u32[]{:S(2)}, u32[]{:S(2)}) collective-permute-start(bf16[16,96,512]{2,1,0:T(8,128)(2,1)S(1)} %constant_dynamic-update-slice_fusion.10.refs_4_.refs_7_.refs_5_), channel_id=1, source_target_pairs={{0,65},{1,64},{32,96},{33,97},{64,1},{65,0},{96,32},{97,33},{2,67}... | collective-permute-start | bytes 4718600 | tf_op jit(solution)/shard_map/ppermute | solution.py:32
  60.7 39.9 %copy-start.3 = (f32[96,1536]{1,0:T(8,128)S(1)}, f32[96,1536]{1,0:T(8,128)}, u32[]{:S(2)}) copy-start(f32[96,1536]{1,0:T(8,128)} %param.8) | copy-start | bytes 1769476
  60.7 37.3 %collective-permute-start.17 = (bf16[16,96,512]{2,1,0:T(8,128)(2,1)S(1)}, bf16[16,96,512]{2,1,0:T(8,128)(2,1)S(1)}, u32[]{:S(2)}, u32[]{:S(2)}) collective-permute-start(bf16[16,96,512]{2,1,0:T(8,128)(2,1)S(1)} %constant_dynamic-update-slice_fusion.5.refs_4_.refs_7_.refs_5_), channel_id=1, source_target_pairs={{0,2},{2,0},{4,6},{6,4},{32,38},{34,36},{36,34},{38,32},{1,3},{3,1... | collective-permute-start | bytes 4718600 | tf_op jit(solution)/shard_map/ppermute | solution.py:32
  61.5 39.1 %collective-permute-start.10 = (bf16[16,96,512]{2,1,0:T(8,128)(2,1)S(1)}, bf16[16,96,512]{2,1,0:T(8,128)(2,1)S(1)}, u32[]{:S(2)}, u32[]{:S(2)}) collective-permute-start(bf16[16,96,512]{2,1,0:T(8,128)(2,1)S(1)} %constant_dynamic-update-slice_fusion.refs_4_.refs_7_.refs_5_), channel_id=1, source_target_pairs={{0,8},{8,0},{16,24},{24,16},{32,56},{40,48},{48,40},{56,32},{1,9},... | collective-permute-start | bytes 4718600 | tf_op jit(solution)/shard_map/ppermute | solution.py:32
  65.3 40.8 %collective-permute-start.18 = (bf16[16,96,512]{2,1,0:T(8,128)(2,1)S(1)}, bf16[16,96,512]{2,1,0:T(8,128)(2,1)S(1)}, u32[]{:S(2)}, u32[]{:S(2)}) collective-permute-start(bf16[16,96,512]{2,1,0:T(8,128)(2,1)S(1)} %constant_dynamic-update-slice_fusion.5.refs_4_.refs_7_.refs_5_), channel_id=1, source_target_pairs={{0,6},{2,4},{4,2},{6,0},{32,34},{34,32},{36,38},{38,36},{1,7},{3,5... | collective-permute-start | bytes 4718600 | tf_op jit(solution)/shard_map/ppermute | solution.py:32
  85.2 25.2 %collective-permute-start.11 = (bf16[16,96,512]{2,1,0:T(8,128)(2,1)S(1)}, bf16[16,96,512]{2,1,0:T(8,128)(2,1)S(1)}, u32[]{:S(2)}, u32[]{:S(2)}) collective-permute-start(bf16[16,96,512]{2,1,0:T(8,128)(2,1)S(1)} %constant_dynamic-update-slice_fusion.refs_4_.refs_7_.refs_5_), channel_id=1, source_target_pairs={{0,24},{8,16},{16,8},{24,0},{32,40},{40,32},{48,56},{56,48},{1,25}... | collective-permute-start | bytes 4718600 | tf_op jit(solution)/shard_map/ppermute | solution.py:32
  88.1 26.6 %collective-permute-start.26 = (bf16[16,96,512]{2,1,0:T(8,128)(2,1)S(1)}, bf16[16,96,512]{2,1,0:T(8,128)(2,1)S(1)}, u32[]{:S(2)}, u32[]{:S(2)}) collective-permute-start(bf16[16,96,512]{2,1,0:T(8,128)(2,1)S(1)} %collective-permute-done.24.refs_5_.refs_6_), channel_id=1, source_target_pairs={{0,65},{1,64},{32,96},{33,97},{64,1},{65,0},{96,32},{97,33},{2,67}... | collective-permute-start | bytes 4718600 | tf_op jit(solution)/shard_map/ppermute | solution.py:32
  98.0 21.9 %collective-permute-start.19 = (bf16[16,96,512]{2,1,0:T(8,128)(2,1)S(1)}, bf16[16,96,512]{2,1,0:T(8,128)(2,1)S(1)}, u32[]{:S(2)}, u32[]{:S(2)}) collective-permute-start(bf16[16,96,512]{2,1,0:T(8,128)(2,1)S(1)} %collective-permute-done.17.refs_5_.refs_6_), channel_id=1, source_target_pairs={{0,6},{2,4},{4,2},{6,0},{32,34},{34,32},{36,38},{38,36},{1,7},{3,5... | collective-permute-start | bytes 4718600 | tf_op jit(solution)/shard_map/ppermute | solution.py:32
  100.5 25.7 %collective-permute-start.12 = (bf16[16,96,512]{2,1,0:T(8,128)(2,1)S(1)}, bf16[16,96,512]{2,1,0:T(8,128)(2,1)S(1)}, u32[]{:S(2)}, u32[]{:S(2)}) collective-permute-start(bf16[16,96,512]{2,1,0:T(8,128)(2,1)S(1)} %collective-permute-done.10.refs_5_.refs_6_), channel_id=1, source_target_pairs={{0,24},{8,16},{16,8},{24,0},{32,40},{40,32},{48,56},{56,48},{1,25}... | collective-permute-start | bytes 4718600 | tf_op jit(solution)/shard_map/ppermute | solution.py:32
  125.7 6.0 %collective-permute-start.29 = (bf16[2,512,512]{2,1,0:T(8,128)(2,1)S(1)}, bf16[2,512,512]{2,1,0:T(8,128)(2,1)S(1)}, u32[]{:S(2)}, u32[]{:S(2)}) collective-permute-start(bf16[2,512,512]{2,1,0:T(8,128)(2,1)S(1)} %get-tuple-element.43), channel_id=1, source_target_pairs={{0,32},{32,0},{1,33},{33,1},{2,34},{34,2},{3,35},{35,3},{4,36},{36... | collective-permute-start | bytes 3145736 | tf_op jit(solution)/shard_map/ppermute | solution.py:309
  125.7 6.0 %collective-permute-start.28 = (bf16[2,512,512]{2,1,0:T(8,128)(2,1)S(1)}, bf16[2,512,512]{2,1,0:T(8,128)(2,1)S(1)}, u32[]{:S(2)}, u32[]{:S(2)}) collective-permute-start(bf16[2,512,512]{2,1,0:T(8,128)(2,1)S(1)} %get-tuple-element.42), channel_id=1, source_target_pairs={{0,32},{32,0},{1,33},{33,1},{2,34},{34,2},{3,35},{35,3},{4,36},{36... | collective-permute-start | bytes 3145736 | tf_op jit(solution)/shard_map/ppermute | solution.py:309
  131.7 2.7 %collective-permute-start.27 = (bf16[2,512,512]{2,1,0:T(8,128)(2,1)S(1)}, bf16[2,512,512]{2,1,0:T(8,128)(2,1)S(1)}, u32[]{:S(2)}, u32[]{:S(2)}) collective-permute-start(bf16[2,512,512]{2,1,0:T(8,128)(2,1)S(1)} %get-tuple-element.41), channel_id=1, source_target_pairs={{0,32},{32,0},{1,33},{33,1},{2,34},{34,2},{3,35},{35,3},{4,36},{36... | collective-permute-start | bytes 3145736 | tf_op jit(solution)/shard_map/ppermute | solution.py:309
  (5 other events, 45.7 us)
